TPU v7x, 256 devices: a whole 4x4x8 slice. The times are simulated.
256 devices in a mesh: region: 8 (over x, y_lo), scen: 32 (over y_hi, z, core).
Axes of the slice: x: 4, y: 4 (y_hi: 2, y_lo: 2; y = y_hi * 2 + y_lo), z: 8, core: 2. Of those that a mesh axis runs over, the one named last changes fastest.
Arguments:
- start_state: float32 [8, 512, 24, 1024], P('region', 'scen'), may hold values from -6 to 6
- price: float32 [8, 512, 24, 1024], P('region', 'scen'), may hold values from -6 to 6
- demand: float32 [8, 512, 24, 1024], P('region', 'scen'), may hold values from 0.2 to 2
- sens: bfloat16 [8, 1024, 1024], P('region'), as said below
- gen_bus: int32 [8, 512], P('region'), may hold values from 0 to 1023
- gen_cap: float32 [8, 512], P('region'), may hold values from 0.5 to 3
- tie_index: int32 [8, 2, 512], P('region'), may hold values from 0 to 1023, as said below
- tie_len: int32 [8, 2], P('region'), may hold values from 128 to 512, as said below
Outputs:
- final_state: float32 [8, 512, 24, 1024], P('region', 'scen')
- plan: float32 [8, 24, 1024], P('region')
Inputs may be any that keep to these rules, and one draw needn't show every extreme that they name: `tie_index`: for each region the two rows together hold each of the 1024 bus numbers exactly once. tie_len[r, 1] equals tie_len[(r + 1) mod 8, 0]; some border has exactly 512 live slots. `sens`: each matrix has a positive diagonal between 0.5 and 2 and off-diagonal entries of order 1 / sqrt(1024).
All inputs are finite; a program needn't handle non-finite values.
Results may differ from a plain program's by a relative error of at most 0.00098.
Values sent between devices are 32-bit elements; how exact they have to be, the bound alone decides.
No kernel may reach another device: no remote copies, remote signals or barrier semaphores. Data moves between devices by JAX's collectives and lax.ppermute only.
A program may use at most 64 MiB of HBM per device.

v0:
```python
import jax
import jax.numpy as jnp
from jax import lax
from jax.sharding import PartitionSpec as P

SWEEPS = 2
STEPS = 3


step_rate = 0.3
tie_weight = 1.0
day_weight = 0.5


def extended(value, sides, width):
    for axis, dim in sides:
        size, length = (lax.axis_size(axis), value.shape[dim])
        up = [(i, (i + 1) % size) for i in range(size)]
        down = [(j, i) for i, j in up]
        last = lax.slice_in_dim(value, length - width, length, axis=dim)
        initial = lax.slice_in_dim(value, 0, width, axis=dim)
        before = lax.ppermute(last, axis, up)
        after = lax.ppermute(initial, axis, down)
        value = jnp.concatenate([before, value, after], axis=dim)
    return value


def cut_along(value, dim, size):
    before, after = (value.shape[:dim], value.shape[dim + 1 :])
    return jnp.moveaxis(value.reshape(*before, size, -1, *after), dim, 0)


def sent_and_summed(value, axis, dim):
    size = lax.axis_size(axis)
    pieces = lax.all_to_all(cut_along(value, dim, size), axis, 0, 0, tiled=True)
    return jnp.sum(pieces, axis=0)


def copy_for_each(value, axis):
    size = lax.axis_size(axis)
    return lax.all_to_all(
        jnp.broadcast_to(value[None], (size, *value.shape)), axis, 0, 0, tiled=True
    )


def in_order(pieces, dim):
    dims = list(pieces.shape[1:])
    dims[dim] *= pieces.shape[0]
    return jnp.moveaxis(pieces, 0, dim).reshape(dims)


def gather_directly(value, axis, dim):
    pieces = copy_for_each(value, axis)
    return in_order(pieces, dim)


def select_dot(left, right):
    return jnp.dot(left, right, precision=lax.Precision.HIGHEST, preferred_element_type=jnp.float32)


def tie_target(state, permuter, live, tie_dual):
    scens, hours, buses = state.shape
    slots = live.shape[1]
    blocks = select_dot(state.reshape(-1, buses), permuter).reshape(scens, hours, 2, slots)
    padded = extended(blocks, (("region", 2),), 1)
    theirs = jnp.stack([padded[:, :, 0], padded[:, :, 3]], axis=2)
    middle = 0.5 * (blocks + theirs)
    tie_dual = tie_dual + blocks - middle
    target_blocks = (middle - tie_dual) * live
    target = select_dot(target_blocks.reshape(-1, buses), permuter.T).reshape(state.shape)
    return (target, tie_dual)


def day_ahead(state, day_dual, total_scen):
    local_sum = jnp.sum(state + day_dual, axis=0)
    share = sent_and_summed(local_sum, "scen", 1)
    plan = gather_directly(share / total_scen, "scen", 1)
    return (plan, day_dual + state - plan[None])


def descend(state, prices, lower, matrix, target, tie_mask, plan, day_dual, upper):
    buses = state.shape[-1]
    for repeat in range(STEPS):
        rounded = state.reshape(-1, buses).astype(jnp.bfloat16)
        slope = jnp.dot(rounded, matrix, preferred_element_type=jnp.float32).reshape(state.shape)
        slope = (
            slope
            + prices
            + tie_weight * tie_mask * (state - target)
            + day_weight * (state - plan + day_dual)
        )
        state = jnp.clip(state - step_rate * slope, lower, upper)
    return state


def body(start_state, price, demand, sens, gen_bus, gen_cap, tie_index, tie_len):
    state = start_state[0]
    prices = price[0]
    lower = -demand[0]
    matrix = sens[0]
    indices = tie_index[0]
    buses = state.shape[-1]
    slots = indices.shape[1]
    total_scen = state.shape[0] * lax.axis_size("scen")
    bus_ids = jnp.arange(buses, dtype=jnp.int32)
    permuter = (bus_ids[:, None] == indices.reshape(-1)[None, :]).astype(jnp.float32)
    live = (jnp.arange(slots, dtype=jnp.int32)[None, :] < tie_len[0][:, None]).astype(jnp.float32)
    tie_mask = select_dot(permuter, live.reshape(-1))
    gen_onehot = (gen_bus[0][:, None] == bus_ids[None, :]).astype(jnp.float32)
    upper = select_dot(gen_cap[0][None, :], gen_onehot)[0]
    tie_dual = jnp.zeros(state.shape[:2] + (2, slots), jnp.float32)
    day_dual = jnp.zeros_like(state)
    plan = jnp.zeros(state.shape[1:], jnp.float32)
    for sweep in range(SWEEPS):
        target, tie_dual = tie_target(state, permuter, live, tie_dual)
        plan, day_dual = day_ahead(state, day_dual, total_scen)
        state = descend(state, prices, lower, matrix, target, tie_mask, plan, day_dual, upper)
    return (state[None], plan[None])


def solution(mesh):
    in_specs = (
        P("region", "scen", None, None),
        P("region", "scen", None, None),
        P("region", "scen", None, None),
        P("region", None, None),
        P("region", None),
        P("region", None),
        P("region", None, None),
        P("region", None),
    )
    out_specs = (P("region", "scen", None, None), P("region", None, None))
    return jax.shard_map(body, mesh=mesh, in_specs=in_specs, out_specs=out_specs, check_vma=False)
```

profile of v0, /device:TPU:8, one launch (start us, length us, event | category | flops | bytes accessed | tf_op | source)
XLA Modules:
  0.0 169.3 jit_solution(6474913847969551330)
XLA Ops:
  0.6 0.8 copy.40
  1.5 5.4 %fusion.83 = f32[384,1024]{1,0:T(8,128)} fusion(f32[384,1024]{1,0:T(8,128)} %bitcast.186, s32[1024]{0:T(1024)S(1)} %bitcast.215), kind=kOutput, calls=%fused_computation.82 | convolution fusion | flops 4832886784 | bytes 3149824 | tf_op jit(solution)/shard_map/dot_general | solution.py:58
  6.9 3.4 %reshape.101 = f32[16,24,2,512]{3,2,1,0:T(2,128)} reshape(f32[384,1024]{1,0:T(8,128)} %fusion.83) | data formatting | bytes 3145728 | tf_op jit(solution)/shard_map/reshape | solution.py:64
  10.3 3.5 %fusion.97 = (f32[16,24,1,512]{3,2,1,0:T(1,128)S(1)}, f32[16,24,1,512]{3,2,1,0:T(1,128)S(1)}) fusion(f32[16,24,2,512]{3,2,1,0:T(2,128)} %reshape.101), kind=kLoop, calls=%fused_computation.103 | loop fusion | bytes 3145728 | tf_op jit(solution)/shard_map/slice | solution.py:21
  13.8 0.9 copy.45
  14.7 1.4 collective-permute-start
  16.1 0.9 copy.46
  17.1 0.8 collective-permute-start.1
  17.8 1.5 reduce_sum.36
  19.3 0.1 reshape.102
  19.5 0.2 copy.30
  19.7 0.8 reshape.112
  20.6 10.5 %all-to-all-start = ((f32[32,1,768]{2,1,0:T(1,128)}), f32[32,1,768]{2,1,0:T(1,128)S(1)}, u32[]{:S(2)}, u32[]{:S(2)}) async-start(f32[32,1,768]{2,1,0:T(1,128)} %reshape.112), calls=%async_computation | async-start | bytes 196608 | tf_op jit(solution)/shard_map/all_to_all | solution.py:35
  31.0 0.1 broadcast_bitcast_fusion
  31.1 0.1 lt.45
  31.2 0.8 fusion.2
  32.0 23.1 %all-to-all-done = f32[32,1,768]{2,1,0:T(1,128)S(1)} async-done(((f32[32,1,768]{2,1,0:T(1,128)}), f32[32,1,768]{2,1,0:T(1,128)S(1)}, u32[]{:S(2)}, u32[]{:S(2)}) %all-to-all-start) | async-done | bytes 98336 | tf_op jit(solution)/shard_map/all_to_all | solution.py:35
  55.1 0.6 broadcast.69
  55.7 0.9 reduce.1
  56.6 0.1 reshape.113
  56.9 0.8 reshape.114
  57.7 9.6 %all-to-all-start.1 = ((f32[32,1,768]{2,1,0:T(1,128)}), f32[32,1,768]{2,1,0:T(1,128)S(1)}, u32[]{:S(2)}, u32[]{:S(2)}) async-start(f32[32,1,768]{2,1,0:T(1,128)} %reshape.114), calls=%async_computation.1 | async-start | bytes 196608 | tf_op jit(solution)/shard_map/all_to_all | solution.py:41
  67.3 0.8 fusion.27
  68.1 10.2 %all-to-all-done.1 = f32[32,1,768]{2,1,0:T(1,128)S(1)} async-done(((f32[32,1,768]{2,1,0:T(1,128)}), f32[32,1,768]{2,1,0:T(1,128)S(1)}, u32[]{:S(2)}, u32[]{:S(2)}) %all-to-all-start.1) | async-done | bytes 98336 | tf_op jit(solution)/shard_map/all_to_all | solution.py:41
  78.3 0.9 reduce.2
  79.3 0.1 reshape.115
  79.4 0.1 copy.31
  79.5 0.2 sub.109
  79.7 1.2 constant_dynamic-update-slice_fusion.1
  80.9 1.2 constant_dynamic-update-slice_fusion
  82.1 1.2 copy.29
  83.3 0.3 copy.43
  83.7 1.1 copy-done.9
  84.7 0.4 fusion.28
  85.2 2.9 %fusion.5 = f32[16,24,1024]{2,1,0:T(8,128)S(1)} fusion(f32[16,24,1024]{2,1,0:T(8,128)S(1)} %bitcast.194, s32[1024]{0:T(1024)S(1)} %bitcast.217), kind=kOutput, calls=%fused_computation.6 | convolution fusion | flops 4832886784 | bytes 3149824 | tf_op jit(solution)/shard_map/dot_general | solution.py:58
  88.1 1.4 fusion.38
  89.5 1.5 fusion.44
  91.0 2.7 %fusion.94 = (f32[24,1024]{1,0:T(8,128)S(1)}, f32[16,24,1024]{2,1,0:T(8,128)}, f32[16,24,1024]{2,1,0:T(8,128)S(1)}) fusion(f32[24,1024]{1,0:T(8,128)S(1)} %sub.109, f32[1,16,24,1024]{3,2,1,0:T(8,128)S(1)} %copy-done.6, f32[16,24,1024]{2,1,0:T(8,128)S(1)} %fusion.44, f32[16,24,1024]{2,1,0:T(8,128)S(1)} %fusion.5, f32[1024]{0:T(1024)S(1)} %bitcast.197, ...), kind=kOutput, calls=%fused_computation.101 | convolution fusion | flops 811966464 | bytes 13312000 | tf_op jit(solution)/shard_map/dot_general | solution.py:85
  93.8 3.2 %fusion.8 = f32[16,24,2,512]{3,1,2,0:T(8,128)S(1)} fusion(s32[2,512]{1,0:T(2,128)S(1)} %bitcast.214, f32[16,24,1024]{2,1,0:T(8,128)S(1)} %get-tuple-element.10), kind=kOutput, calls=%fused_computation.8 | convolution fusion | flops 4832886784 | bytes 3149824 | tf_op jit(solution)/shard_map/dot_general | solution.py:58
  97.0 1.5 fusion.96
  98.6 0.2 copy-done.8
  98.8 0.4 collective-permute-start.2
  99.2 1.6 collective-permute-start.3
  100.8 0.1 reshape.103
  100.9 0.2 copy.35
  101.2 0.2 reshape.116
  101.4 34.2 %all_to_all.20 = f32[32,1,768]{2,1,0:T(1,128)S(1)} all-to-all(f32[32,1,768]{2,1,0:T(1,128)S(1)} %reshape.116), channel_id=1, replica_groups=mesh['region'=8,'scen'=32] {'scen'}, dimensions={0} | all-to-all | bytes 196608 | tf_op jit(solution)/shard_map/all_to_all | solution.py:35
  135.6 0.9 reduce.3
  136.5 0.1 reshape.117
  136.8 0.8 reshape.118
  137.6 5.5 %all-to-all-start.3 = ((f32[32,1,768]{2,1,0:T(1,128)}), f32[32,1,768]{2,1,0:T(1,128)S(1)}, u32[]{:S(2)}, u32[]{:S(2)}) async-start(f32[32,1,768]{2,1,0:T(1,128)} %reshape.118), calls=%async_computation.3 | async-start | bytes 196608 | tf_op jit(solution)/shard_map/all_to_all | solution.py:41
  143.1 0.1 compare_convert_fusion
  143.2 11.2 %all-to-all-done.3 = f32[32,1,768]{2,1,0:T(1,128)S(1)} async-done(((f32[32,1,768]{2,1,0:T(1,128)}), f32[32,1,768]{2,1,0:T(1,128)S(1)}, u32[]{:S(2)}, u32[]{:S(2)}) %all-to-all-start.3) | async-done | bytes 98336 | tf_op jit(solution)/shard_map/all_to_all | solution.py:41
  154.4 0.9 reduce.4
  155.3 0.1 reshape.119
  155.4 0.1 copy.36
  155.5 0.2 sub.123
  155.7 0.8 broadcast_in_dim_reshape.2
  156.5 3.8 %fusion.30 = f32[16,2,3,8,512]{4,3,2,1,0:T(8,128)S(1)} fusion(f32[16,24,2,512]{3,1,2,0:T(8,128)} %copy-done.8, f32[16,24,1,512]{3,1,2,0:T(8,128)} %collective-permute-done.3, f32[16,24,1,512]{3,1,2,0:T(8,128)} %collective-permute-done.2, f32[16,24,2,512]{3,1,2,0:T(8,128)} %copy-done.7, f32[2,512]{1,0:T(2,128)S(1)} %compare_convert_fusion, ...), kind=kLoop, calls=%fused_computation.32 | loop fusion | flops 3932160 | bytes 7868416
  160.3 0.1 copy.39
  160.5 2.9 %fusion.3 = f32[16,24,1024]{2,1,0:T(8,128)S(1)} fusion(f32[16,24,1024]{2,1,0:T(8,128)S(1)} %bitcast.189, s32[1024]{0:T(1024)S(1)} %bitcast.218), kind=kOutput, calls=%fused_computation.5 | convolution fusion | flops 4832886784 | bytes 3149824 | tf_op jit(solution)/shard_map/dot_general | solution.py:58
  163.4 1.6 fusion.56
  165.0 1.6 fusion.62
  166.6 2.7 %fusion.69 = f32[1,16,24,1024]{3,2,1,0:T(8,128)} fusion(f32[16,24,1024]{2,1,0:T(8,128)S(1)} %fusion.62, f32[1,16,24,1024]{3,2,1,0:T(8,128)S(1)} %copy-done.2, f32[16,24,1024]{2,1,0:T(8,128)S(1)} %fusion.3, bf16[1,1024,1024]{2,1,0:T(8,128)(2,1)S(1)} %copy-done, f32[16,24,1024]{2,1,0:T(8,128)S(1)} %copy-done.5, f32[1,16,24,1024]{3,2,1,0:T(8,128)S(1)} %copy-done.4, ...), kind=kOutput, calls=%fused_computation.78 | convolution fusion | flops 811204608 | bytes 11640832 | tf_op jit(solution)/shard_map/dot_general | solution.py:85
  (45 shorter events, 0.3 us)
Async XLA Ops:
  0.6 87.5 %copy-start = (bf16[1,1024,1024]{2,1,0:T(8,128)(2,1)S(1)}, bf16[1,1024,1024]{2,1,0:T(8,128)(2,1)}, u32[]{:S(2)}) copy-start(bf16[1,1024,1024]{2,1,0:T(8,128)(2,1)} %param.11) | copy-start | bytes 6291460
  14.7 65.0 %collective-permute-start = (f32[16,24,1,512]{3,1,2,0:T(8,128)}, f32[16,24,1,512]{3,1,2,0:T(8,128)}, u32[]{:S(2)}, u32[]{:S(2)}) collective-permute-start(f32[16,24,1,512]{3,1,2,0:T(8,128)} %copy.45), channel_id=1, source_target_pairs={{0,32},{32,64},{64,96},{96,128},{128,160},{160,192},{192,224},{224... | collective-permute-start | bytes 2359304 | tf_op jit(solution)/shard_map/ppermute | solution.py:22
  17.0 14.0 %copy-start.12 = (s32[1,2]{1,0:T(1,128)S(1)}, s32[1,2]{1,0:T(1,128)}, u32[]{:S(2)}) copy-start(s32[1,2]{1,0:T(1,128)} %param.15) | copy-start | bytes 28
  17.1 63.8 %collective-permute-start.1 = (f32[16,24,1,512]{3,1,2,0:T(8,128)}, f32[16,24,1,512]{3,1,2,0:T(8,128)}, u32[]{:S(2)}, u32[]{:S(2)}) collective-permute-start(f32[16,24,1,512]{3,1,2,0:T(8,128)} %copy.46), channel_id=1, source_target_pairs={{32,0},{64,32},{96,64},{128,96},{160,128},{192,160},{224,192},{0,2... | collective-permute-start | bytes 2359304 | tf_op jit(solution)/shard_map/ppermute | solution.py:23
  20.6 34.5 %all-to-all-start = ((f32[32,1,768]{2,1,0:T(1,128)}), f32[32,1,768]{2,1,0:T(1,128)S(1)}, u32[]{:S(2)}, u32[]{:S(2)}) async-start(f32[32,1,768]{2,1,0:T(1,128)} %reshape.112), calls=%async_computation | async-start | bytes 196608 | tf_op jit(solution)/shard_map/all_to_all | solution.py:35
  31.2 36.1 %copy-start.14 = (s32[1,512]{1,0:T(1,128)S(1)}, s32[1,512]{1,0:T(1,128)}, u32[]{:S(2)}) copy-start(s32[1,512]{1,0:T(1,128)} %param.12) | copy-start | bytes 6148
  31.2 36.1 %copy-start.15 = (f32[1,512]{1,0:T(1,128)S(1)}, f32[1,512]{1,0:T(1,128)}, u32[]{:S(2)}) copy-start(f32[1,512]{1,0:T(1,128)} %param.13) | copy-start | bytes 6148
  57.7 20.6 %all-to-all-start.1 = ((f32[32,1,768]{2,1,0:T(1,128)}), f32[32,1,768]{2,1,0:T(1,128)S(1)}, u32[]{:S(2)}, u32[]{:S(2)}) async-start(f32[32,1,768]{2,1,0:T(1,128)} %reshape.114), calls=%async_computation.1 | async-start | bytes 196608 | tf_op jit(solution)/shard_map/all_to_all | solution.py:41
  82.1 1.2 copy-start.7
  83.3 1.4 copy-start.9
  85.1 3.0 %copy-start.1 = (f32[1,16,24,1024]{3,2,1,0:T(8,128)S(1)}, f32[1,16,24,1024]{3,2,1,0:T(8,128)}, u32[]{:S(2)}) copy-start(f32[1,16,24,1024]{3,2,1,0:T(8,128)} %param.9) | copy-start | bytes 4718596
  85.1 3.0 %copy-start.3 = (f32[1,16,24,1024]{3,2,1,0:T(8,128)S(1)}, f32[1,16,24,1024]{3,2,1,0:T(8,128)}, u32[]{:S(2)}) copy-start(f32[1,16,24,1024]{3,2,1,0:T(8,128)} %param.10) | copy-start | bytes 4718596
  85.2 3.0 %copy-start.6 = (f32[1,16,24,1024]{3,2,1,0:T(8,128)S(1)}, f32[1,16,24,1024]{3,2,1,0:T(8,128)}, u32[]{:S(2)}) copy-start(f32[1,16,24,1024]{3,2,1,0:T(8,128)} %param.8) | copy-start | bytes 4718596
  91.0 2.7 %copy-start.13 = (s32[1,2,512]{2,1,0:T(2,128)S(1)}, s32[1,2,512]{2,1,0:T(2,128)}, u32[]{:S(2)}) copy-start(s32[1,2,512]{2,1,0:T(2,128)} %param.14) | copy-start | bytes 12292
  93.8 3.3 %copy-start.10 = (f32[16,24,1024]{2,1,0:T(8,128)}, f32[16,24,1024]{2,1,0:T(8,128)S(1)}, u32[]{:S(2)}) copy-start(f32[16,24,1024]{2,1,0:T(8,128)S(1)} %get-tuple-element.10) | copy-start | bytes 4718596
  97.0 1.7 %copy-start.8 = (f32[16,24,2,512]{3,1,2,0:T(8,128)}, f32[16,24,2,512]{3,1,2,0:T(8,128)S(1)}, u32[]{:S(2)}) copy-start(f32[16,24,2,512]{3,1,2,0:T(8,128)S(1)} %fusion.8) | copy-start | bytes 4718596
  98.8 57.8 %collective-permute-start.2 = (f32[16,24,1,512]{3,1,2,0:T(8,128)}, f32[16,24,1,512]{3,1,2,0:T(8,128)}, u32[]{:S(2)}, u32[]{:S(2)}) collective-permute-start(f32[16,24,1,512]{3,1,2,0:T(8,128)} %get-tuple-element.4), channel_id=1, source_target_pairs={{0,32},{32,64},{64,96},{96,128},{128,160},{160,192},{192,224},{224... | collective-permute-start | bytes 2359304 | tf_op jit(solution)/shard_map/ppermute | solution.py:22
  99.2 57.4 %collective-permute-start.3 = (f32[16,24,1,512]{3,1,2,0:T(8,128)}, f32[16,24,1,512]{3,1,2,0:T(8,128)}, u32[]{:S(2)}, u32[]{:S(2)}) collective-permute-start(f32[16,24,1,512]{3,1,2,0:T(8,128)} %get-tuple-element.5), channel_id=1, source_target_pairs={{32,0},{64,32},{96,64},{128,96},{160,128},{192,160},{224,192},{0,2... | collective-permute-start | bytes 2359304 | tf_op jit(solution)/shard_map/ppermute | solution.py:23
  137.6 16.7 %all-to-all-start.3 = ((f32[32,1,768]{2,1,0:T(1,128)}), f32[32,1,768]{2,1,0:T(1,128)S(1)}, u32[]{:S(2)}, u32[]{:S(2)}) async-start(f32[32,1,768]{2,1,0:T(1,128)} %reshape.118), calls=%async_computation.3 | async-start | bytes 196608 | tf_op jit(solution)/shard_map/all_to_all | solution.py:41
  160.3 3.1 %copy-start.11 = (f32[16,24,1024]{2,1,0:T(8,128)S(1)}, f32[16,24,1024]{2,1,0:T(8,128)}, u32[]{:S(2)}) copy-start(f32[16,24,1024]{2,1,0:T(8,128)} %copy-done.10) | copy-start | bytes 4718596
  160.4 3.0 %copy-start.2 = (f32[1,16,24,1024]{3,2,1,0:T(8,128)S(1)}, f32[1,16,24,1024]{3,2,1,0:T(8,128)}, u32[]{:S(2)}) copy-start(f32[1,16,24,1024]{3,2,1,0:T(8,128)} %param.9) | copy-start | bytes 4718596
  160.4 3.0 %copy-start.4 = (f32[1,16,24,1024]{3,2,1,0:T(8,128)S(1)}, f32[1,16,24,1024]{3,2,1,0:T(8,128)}, u32[]{:S(2)}) copy-start(f32[1,16,24,1024]{3,2,1,0:T(8,128)} %param.10) | copy-start | bytes 4718596
  160.5 3.0 %copy-start.5 = (f32[16,24,1024]{2,1,0:T(8,128)S(1)}, f32[16,24,1024]{2,1,0:T(8,128)}, u32[]{:S(2)}) copy-start(f32[16,24,1024]{2,1,0:T(8,128)} %get-tuple-element.3) | copy-start | bytes 4718596
where the time goes:
time: 170 us; the launch traced here: 169 us
  waiting for transfers between devices  44.5 us (26%)
  blocking collectives  34.2 us (20%)
  starting transfers between devices  29.7 us (17%)
  matrix products  27.5 us (16%)
  local copies, waits for them, and re-layouts  22.7 us (13%)
  other arithmetic  9.51 us (6%)
    all_to_all x1, blocking collectives, sent_and_summed(): pieces = lax.all_to_all(cut_along(value, dim, size), axis, 0, 0, tiled=True)  34.2 us
    all_to_all x1, waiting for transfers between devices, sent_and_summed(): pieces = lax.all_to_all(cut_along(value, dim, size), axis, 0, 0, tiled=True)  23.1 us
    all_to_all x2, waiting for transfers between devices, copy_for_each(): lax.all_to_all(jnp.broadcast_to(value[None], (size, *value.shape)), axis,...  21.4 us
    dot_general x6, matrix products, select_dot(): jnp.dot(left, right, precision=lax.Precision.HIGHEST, preferred_element_t...  16 us
    all_to_all x2, starting transfers between devices, copy_for_each(): lax.all_to_all(jnp.broadcast_to(value[None], (size, *value.shape)), axis,...  15 us
    dot_general x6, matrix products, descend(): jnp.dot(rounded, matrix, preferred_element_type=jnp.float32)  11.5 us
    all_to_all x1, starting transfers between devices, sent_and_summed(): pieces = lax.all_to_all(cut_along(value, dim, size), axis, 0, 0, tiled=True)  10.5 us
    unnamed x49, local copies, waits for them, and re-layouts  8.94 us
  transfers between devices with their start and end apart: 7, of which 3 were waited for; matrix products, arithmetic and copies ran while one was open for 9% of the time, Pallas kernels for 0%

commit v1 on v0

v1 whole, which is shorter than its diff:
```python
import jax
import jax.numpy as jnp
from jax import lax
from jax.experimental import pallas as pl
from jax.experimental.pallas import tpu as pltpu
from jax.sharding import PartitionSpec as P


CHUNKS = (6, 10)
BLOCK = 256
step_rate = 0.3
tie_weight = 1.0
day_weight = 0.5


F32 = jnp.float32
BF16 = jnp.bfloat16


def dot(a, b):
    return lax.dot_general(a, b, (((1,), (0,)), ((), ())), preferred_element_type=F32)


def dot_t(a, b):
    return lax.dot_general(a, b, (((1,), (1,)), ((), ())), preferred_element_type=F32)


def high_low(x):
    high = x.astype(BF16)
    return high, (x - high.astype(F32)).astype(BF16)


def call(kernel, outs, *, n_in, scratch=()):
    vmem = pl.BlockSpec(memory_space=pltpu.VMEM)
    return pl.pallas_call(
        kernel,
        out_shape=outs,
        in_specs=[vmem] * n_in,
        out_specs=jax.tree.map(lambda _: vmem, outs),
        scratch_shapes=list(scratch),
        compiler_params=pltpu.CompilerParams(vmem_limit_bytes=24 << 20),
    )


def over_scenarios(value, hours):
    rows, width = value.shape
    return jnp.sum(value.reshape(rows // hours, hours, width), axis=0)


def for_scenarios(value, rows):
    hours, width = value.shape
    return jnp.broadcast_to(value[None], (rows // hours, hours, width)).reshape(rows, width)


def sum_kernel(state, out):
    hours = out.shape[0]

    def one(n, _):
        at = pl.ds(pl.multiple_of(n * BLOCK, BLOCK), BLOCK)
        out[:, at] = over_scenarios(state[:, at], hours)
        return 0

    lax.fori_loop(0, out.shape[1] // BLOCK, one, 0)


def select_kernel(index, out):
    rows = 128

    def one(n, _):
        start = pl.multiple_of(n * rows, rows)
        bus = lax.broadcasted_iota(jnp.int32, (rows, out.shape[1]), 0) + start
        out[pl.ds(start, rows), :] = jnp.where(bus == index[...], 1.0, 0.0).astype(BF16)
        return 0

    lax.fori_loop(0, out.shape[0] // rows, one, 0)


def pick_into(pair, select, outs):
    rows, width = outs[0].shape

    for side, out in enumerate(outs):

        def one(n, _):
            at = pl.ds(pl.multiple_of(side * width + n * BLOCK, BLOCK), BLOCK)
            both = dot(pair[...], select[:, at])
            out[:, pl.ds(pl.multiple_of(n * BLOCK, BLOCK), BLOCK)] = both[:rows] + both[rows:]
            return 0

        lax.fori_loop(0, width // BLOCK, one, 0)


def split_into(pair, value, at):
    rows = value.shape[0]
    high, low = high_low(value)
    pair[:rows, at] = high
    pair[rows:, at] = low


def pick_kernel(start, state, select, *rest):
    outs, pair = rest[:2], rest[2]
    rows, _ = outs[0].shape

    def one(n, _):
        at = pl.ds(pl.multiple_of(n * BLOCK, BLOCK), BLOCK)
        split_into(pair, state[start : start + rows, at], at)
        return 0

    lax.fori_loop(0, state.shape[1] // BLOCK, one, 0)
    pick_into(pair, select, outs)


def bounds_kernel(select, live, gen_bus, gen_cap, mask, upper):
    mask[...] = dot_t(jnp.broadcast_to(live[...], (8, live.shape[1])).astype(BF16), select[...])
    caps = jnp.broadcast_to(gen_cap[...], (8, gen_cap.shape[1]))
    high, rest = high_low(caps)
    middle, low = high_low(caps - high.astype(F32))
    del rest
    three = jnp.concatenate([high, middle, low], axis=0)
    rows = 128

    def one(n, _):
        start = pl.multiple_of(n * rows, rows)
        bus = lax.broadcasted_iota(jnp.int32, (rows, gen_bus.shape[1]), 0) + start
        chosen = jnp.where(bus == gen_bus[...], 1.0, 0.0).astype(BF16)
        parts = dot_t(three, chosen)
        upper[:, pl.ds(start, rows)] = parts[:8] + parts[8:16] + parts[16:]
        return 0

    lax.fori_loop(0, upper.shape[1] // rows, one, 0)


def steps(state, rounded, base, matrix, demand, mask, upper, start, out, first, extra=None):
    rows, buses = state.shape
    blocks = buses // BLOCK

    def step(k, source, target_rounded, target, last):
        def one(n, _):
            at = pl.ds(pl.multiple_of(n * BLOCK, BLOCK), BLOCK)
            slope = dot(rounded[source], matrix[:, at])
            if k == 0:
                now = first(at)
            else:
                now = state[:, at]
            slope = slope + base[:, at] + (tie_weight * mask[:1, at] + day_weight) * now
            new = jnp.minimum(
                jnp.maximum(now - step_rate * slope, -demand[start : start + rows, at]), upper[:1, at]
            )
            target[:, at] = new
            if not last:
                rounded[target_rounded, :, at] = new.astype(BF16)
            elif extra is not None:
                extra(at, new)
            return 0

        lax.fori_loop(0, blocks, one, 0)

    step(0, 0, 1, state, False)
    step(1, 1, 0, state, False)
    step(2, 0, 1, out, True)


def first_kernel(start, state0, price, demand, matrix, select, left, right, mask, upper, plan, out, dual_out, total, picked_a, picked_b, state, rounded, base, pair):
    rows, buses = out.shape
    hours = plan.shape[0]
    slots = left.shape[1]

    def load(n, _):
        at = pl.ds(pl.multiple_of(n * BLOCK, BLOCK), BLOCK)
        rounded[0, :, at] = state0[start : start + rows, at].astype(BF16)
        return 0

    lax.fori_loop(0, buses // BLOCK, load, 0)
    split_into(pair, left[...], pl.ds(0, slots))
    split_into(pair, right[...], pl.ds(slots, slots))

    def first(at):
        return state0[start : start + rows, at]

    def constant(n, _):
        at = pl.ds(pl.multiple_of(n * BLOCK, BLOCK), BLOCK)
        both = dot_t(pair[...], select[at, :])
        theirs = both[:rows] + both[rows:]
        now = first(at)
        middle = 0.5 * (now + theirs)
        dual = now - middle
        target = mask[:1, at] * (middle - dual)
        dual_out[:, at] = dual
        day_plan = for_scenarios(plan[:, at], rows)
        day_dual = now - day_plan
        base[:, at] = (
            price[start : start + rows, at]
            - tie_weight * mask[:1, at] * target
            + day_weight * (day_dual - day_plan)
        )
        return 0

    lax.fori_loop(0, buses // BLOCK, constant, 0)

    def extra(at, new):
        split_into(pair, new, at)
        day_plan = for_scenarios(plan[:, at], rows)
        total[:, at] = over_scenarios(new + (first(at) - day_plan), hours)

    steps(state, rounded, base, matrix, demand, mask, upper, start, out, first, extra)
    pick_into(pair, select, (picked_a, picked_b))


def second_kernel(start, state0, state1, dual1, price, demand, matrix, select, left, right, mask, upper, plan1, plan2, out, state, rounded, base, pair):
    rows, buses = out.shape
    slots = left.shape[1]

    def load(n, _):
        at = pl.ds(pl.multiple_of(n * BLOCK, BLOCK), BLOCK)
        rounded[0, :, at] = state1[:, at].astype(BF16)
        return 0

    lax.fori_loop(0, buses // BLOCK, load, 0)
    split_into(pair, left[...], pl.ds(0, slots))
    split_into(pair, right[...], pl.ds(slots, slots))

    def first(at):
        return state1[:, at]

    def constant(n, _):
        at = pl.ds(pl.multiple_of(n * BLOCK, BLOCK), BLOCK)
        both = dot_t(pair[...], select[at, :])
        theirs = both[:rows] + both[rows:]
        now = first(at)
        middle = 0.5 * (now + theirs)
        dual = dual1[:, at] + now - middle
        target = mask[:1, at] * (middle - dual)
        day_plan = for_scenarios(plan2[:, at], rows)
        day_dual = state0[start : start + rows, at] - for_scenarios(plan1[:, at], rows)
        day_dual = day_dual + now - day_plan
        base[:, at] = (
            price[start : start + rows, at]
            - tie_weight * mask[:1, at] * target
            + day_weight * (day_dual - day_plan)
        )
        return 0

    lax.fori_loop(0, buses // BLOCK, constant, 0)
    steps(state, rounded, base, matrix, demand, mask, upper, start, out, first)


def flipped(size, bit):
    return [(i, i ^ bit) for i in range(size)]


def borders(size, first):
    pairs = [((i + first) % size, (i + first + 1) % size) for i in range(0, size, 2)]
    return [pair for a, b in pairs for pair in ((a, b), (b, a))]


def exchange(a, b):
    size = lax.axis_size("region")
    return (
        lax.ppermute(a, "region", borders(size, 0)),
        lax.ppermute(b, "region", borders(size, 1)),
    )


def summed(total, core):
    size = lax.axis_size("scen")
    half = total.shape[1] // 2
    mine = jnp.where(core == 0, total[:, :half], total[:, half:])
    other = jnp.where(core == 0, total[:, half:], total[:, :half])
    part = mine + lax.ppermute(other, "scen", flipped(size, 1))
    for group in ((size // 2,), (2,), (4, 8, 12)):
        others = []
        for bit in group:
            others.append(lax.ppermute(part, "scen", flipped(size, bit)))
        part = part + others[0]
        if len(group) > 1:
            part = part + (others[1] + others[2])
    back = lax.ppermute(part, "scen", flipped(size, 1))
    return jnp.where(
        core == 0, jnp.concatenate([part, back], axis=1), jnp.concatenate([back, part], axis=1)
    )


def inner(start_state, price, demand, sens, gen_bus, gen_cap, tie_index, tie_len):
    scens, hours, buses = start_state.shape[1:]
    slots = tie_index.shape[2]
    rows = scens * hours
    total_scen = scens * lax.axis_size("scen")
    state0 = start_state.reshape(rows, buses)
    prices = price.reshape(rows, buses)
    demands = demand.reshape(rows, buses)
    matrix = sens[0]
    core = lax.axis_index("scen") % 2
    odd = lax.axis_index("region") % 2

    def by_border(pair):
        return jnp.where(odd == 0, jnp.concatenate([pair[1], pair[0]]), jnp.concatenate([pair[0], pair[1]]))[None]

    index = by_border(tie_index[0])
    live = (jnp.arange(slots, dtype=jnp.int32)[None, :] < tie_len[0][:, None]).astype(F32)
    live = by_border(live)

    def shape(*dims, dtype=F32):
        return jax.ShapeDtypeStruct(dims, dtype)

    total0 = call(sum_kernel, shape(hours, buses), n_in=1)(state0)
    select = call(select_kernel, shape(buses, 2 * slots, dtype=BF16), n_in=1)(index)
    starts = [sum(CHUNKS[:c]) * hours for c in range(len(CHUNKS))]
    sizes = [c * hours for c in CHUNKS]
    theirs = []
    for at, size in zip(starts, sizes):
        picked = call(
            lambda *refs, at=at: pick_kernel(at, *refs),
            (shape(size, slots), shape(size, slots)),
            n_in=2,
            scratch=[pltpu.VMEM((2 * size, buses), BF16)],
        )(state0, select)
        theirs.append(exchange(*picked))
    mask, upper = call(bounds_kernel, (shape(8, buses), shape(8, buses)), n_in=4)(
        select, live, gen_bus, gen_cap
    )
    plan1 = summed(total0, core) / total_scen

    def scratch(size):
        return [
            pltpu.VMEM((size, buses), F32),
            pltpu.VMEM((2, size, buses), BF16),
            pltpu.VMEM((size, buses), F32),
            pltpu.VMEM((2 * size, buses), BF16),
        ]

    firsts = []
    theirs1 = []
    for c, (at, size) in enumerate(zip(starts, sizes)):
        first = call(
            lambda *refs, at=at: first_kernel(at, *refs),
            (
                shape(size, buses),
                shape(size, buses),
                shape(hours, buses),
                shape(size, slots),
                shape(size, slots),
            ),
            n_in=10,
            scratch=scratch(size),
        )(state0, prices, demands, matrix, select, *theirs[c], mask, upper, plan1)
        firsts.append(first)
        theirs1.append(exchange(first[3], first[4]))
    total1 = sum(f[2] for f in firsts[1:]) + firsts[0][2]
    plan2 = summed(total1, core) / total_scen
    finals = []
    for c, (at, size) in enumerate(zip(starts, sizes)):
        final = call(
            lambda *refs, at=at: second_kernel(at, *refs),
            shape(size, buses),
            n_in=13,
            scratch=scratch(size),
        )(state0, firsts[c][0], firsts[c][1], prices, demands, matrix, select, *theirs1[c], mask, upper, plan1, plan2)
        finals.append(final)
    final_state = jnp.concatenate(finals, axis=0).reshape(scens, hours, buses)
    return (final_state[None], plan2[None])


def solution(mesh):
    in_specs = (
        P("region", "scen", None, None),
        P("region", "scen", None, None),
        P("region", "scen", None, None),
        P("region", None, None),
        P("region", None),
        P("region", None),
        P("region", None, None),
        P("region", None),
    )
    out_specs = (P("region", "scen", None, None), P("region", None, None))
    return jax.shard_map(inner, mesh=mesh, in_specs=in_specs, out_specs=out_specs, check_vma=False)
```

time: 170 us -> 121 us (0.71)
  blocking collectives: 34.2 us -> 0 us
  Pallas kernels: 0 us -> 31.2 us
  matrix products: 27.5 us -> 0 us
  local copies, waits for them, and re-layouts: 22.7 us -> 1.46 us
  starting transfers between devices: 29.7 us -> 40.8 us
  other arithmetic: 9.51 us -> 2.2 us
    all_to_all x3 -> x0, waiting for transfers between devices: 44.5 us -> none  [the longest x1 23.1 us: sent_and_summed(): pieces = lax.all_to_all(cut_along(value, dim, size), axis, 0, 0, tiled=True)]
    ppermute x4 -> x22, waiting for transfers between devices: 0.01 us -> 43.7 us  [the longest x4 29.9 us: exchange(): lax.ppermute(a, 'region', borders(size, 0))]
    ppermute x4 -> x22, starting transfers between devices: 4.19 us -> 40.8 us  [the longest x10 25.6 us: summed(): others.append(lax.ppermute(part, 'scen', flipped(size, bit)))]
    all_to_all x1 -> x0, blocking collectives: 34.2 us -> none  [sent_and_summed(): pieces = lax.all_to_all(cut_along(value, dim, size), axis, 0, 0, tiled=True)]
    pallas_call x0 -> x9, Pallas kernels: none -> 31.2 us  [the longest x2 14.4 us: inner(): call(lambda *refs, at=at: first_kernel(at, *refs), (shape(size, buses), s...]
    dot_general x12 -> x0, matrix products: 27.5 us -> none  [the longest x6 16 us: select_dot(): jnp.dot(left, right, precision=lax.Precision.HIGHEST, preferred_element_t...]
    all_to_all x3 -> x0, starting transfers between devices: 25.5 us -> none  [the longest x2 15 us: copy_for_each(): lax.all_to_all(jnp.broadcast_to(value[None], (size, *value.shape)), axis,...]
    unnamed x49 -> x18, local copies, waits for them, and re-layouts: 8.94 us -> 1.45 us
  transfers between devices with their start and end apart: 7 -> 22, of which waited for: 3 -> 10; matrix products, arithmetic and copies ran while one was open for 9% -> 1% of each run, Pallas kernels for 0% -> 14%
where the time goes in v1:
time: 121 us; the launch traced here: 120 us
  waiting for transfers between devices  43.7 us (36%)
  starting transfers between devices  40.8 us (34%)
  Pallas kernels  31.2 us (26%)
  other arithmetic  2.2 us (2%)
  local copies, waits for them, and re-layouts  1.46 us (1%)
    ppermute x4, waiting for transfers between devices, exchange(): lax.ppermute(a, 'region', borders(size, 0))  29.9 us
    ppermute x10, starting transfers between devices, summed(): others.append(lax.ppermute(part, 'scen', flipped(size, bit)))  25.6 us
    pallas_call x2, Pallas kernels, inner(): call(lambda *refs, at=at: first_kernel(at, *refs), (shape(size, buses), s...  14.4 us
    pallas_call x2, Pallas kernels, inner(): call(lambda *refs, at=at: second_kernel(at, *refs), shape(size, buses), n...  11 us
    ppermute x10, waiting for transfers between devices, summed(): others.append(lax.ppermute(part, 'scen', flipped(size, bit)))  10.1 us
    ppermute x4, starting transfers between devices, exchange(): lax.ppermute(a, 'region', borders(size, 0))  8.08 us
    ppermute x4, starting transfers between devices, exchange(): lax.ppermute(b, 'region', borders(size, 1))  6.82 us
    pallas_call x2, Pallas kernels, inner(): call(lambda *refs, at=at: pick_kernel(at, *refs), (shape(size, slots), sh...  3.34 us
  transfers between devices with their start and end apart: 22, of which 10 were waited for; matrix products, arithmetic and copies ran while one was open for 1% of the time, Pallas kernels for 14%

profile of v1, /device:TPU:8, one launch (start us, length us, event | category | flops | bytes accessed | tf_op | source)
XLA Modules:
  0.0 120.4 jit_solution(4243877742481941252)
XLA Ops:
  0.7 0.0 copy-start
  0.7 1.4 %copy-done = f32[1,16,24,1024]{3,2,1,0:T(8,128)S(1)} copy-done((f32[1,16,24,1024]{3,2,1,0:T(8,128)S(1)}, f32[1,16,24,1024]{3,2,1,0:T(8,128)}, u32[]{:S(2)}) %copy-start) | copy-done | bytes 1572888
  2.1 0.1 shard_map.98
  2.2 0.0 copy-start.1
  2.2 0.1 collective-permute-start.2
  2.3 0.0 copy-done.7
  2.4 1.2 collective-permute-done.2
  3.6 2.4 %collective-permute-start.3 = (f32[24,512]{1,0:T(8,128)S(1)}, f32[24,512]{1,0:T(8,128)S(1)}, u32[]{:S(2)}, u32[]{:S(2)}) collective-permute-start(f32[24,512]{1,0:T(8,128)S(1)} %select_add_fusion.1), channel_id=1, source_target_pairs={{0,16},{1,17},{2,18},{3,19},{4,20},{5,21},{6,22},{7,23},{8,24},{9,... | collective-permute-start | bytes 147464 | tf_op jit(solution)/shard_map/ppermute | solution.py:272
  5.9 0.4 shard_map.95.refs_1_.select.refs_4_.refs_6_
  6.4 0.0 copy-start.8
  6.4 1.9 %shard_map.100 = (f32[240,512]{1,0:T(8,128)S(1)}, f32[240,512]{1,0:T(8,128)S(1)}) custom-call(f32[384,1024]{1,0:T(8,128)S(1)} %bitcast.13, bf16[1024,1024]{1,0:T(8,128)(2,1)S(1)} %shard_map.95.refs_1_.select.refs_4_.refs_6_), custom_call_target="tpu_custom_call" | custom-call | tf_op jit(solution)/shard_map/pallas_call | solution.py:310
  8.3 1.4 %collective-permute-start.11 = (f32[240,512]{1,0:T(8,128)S(1)}, f32[240,512]{1,0:T(8,128)S(1)}, u32[]{:S(2)}, u32[]{:S(2)}) collective-permute-start(f32[240,512]{1,0:T(8,128)S(1)} %get-tuple-element.26), channel_id=1, source_target_pairs={{0,32},{32,0},{64,96},{96,64},{128,160},{160,128},{192,224},{224,1... | collective-permute-start | bytes 1474568 | tf_op jit(solution)/shard_map/ppermute | solution.py:258
  9.7 1.6 %collective-permute-start.12 = (f32[240,512]{1,0:T(8,128)S(1)}, f32[240,512]{1,0:T(8,128)S(1)}, u32[]{:S(2)}, u32[]{:S(2)}) collective-permute-start(f32[240,512]{1,0:T(8,128)S(1)} %get-tuple-element.27), channel_id=1, source_target_pairs={{32,64},{64,32},{96,128},{128,96},{160,192},{192,160},{224,0},{0,2... | collective-permute-start | bytes 1474568 | tf_op jit(solution)/shard_map/ppermute | solution.py:259
  11.3 0.0 collective-permute-done.3
  11.3 2.0 %collective-permute-start.4 = (f32[24,512]{1,0:T(8,128)S(1)}, f32[24,512]{1,0:T(8,128)S(1)}, u32[]{:S(2)}, u32[]{:S(2)}) collective-permute-start(f32[24,512]{1,0:T(8,128)S(1)} %add.49), channel_id=1, source_target_pairs={{0,2},{1,3},{2,0},{3,1},{4,6},{5,7},{6,4},{7,5},{8,10},{9,11},{10,... | collective-permute-start | bytes 147464 | tf_op jit(solution)/shard_map/ppermute | solution.py:272
  13.4 0.1 compare_convert_fusion
  13.4 2.1 %collective-permute-done.4 = f32[24,512]{1,0:T(8,128)S(1)} collective-permute-done((f32[24,512]{1,0:T(8,128)S(1)}, f32[24,512]{1,0:T(8,128)S(1)}, u32[]{:S(2)}, u32[]{:S(2)}) %collective-permute-start.4) | collective-permute-done | bytes 49184 | tf_op jit(solution)/shard_map/ppermute | solution.py:272
  15.5 6.4 %collective-permute-start.7 = (f32[24,512]{1,0:T(8,128)S(1)}, f32[24,512]{1,0:T(8,128)S(1)}, u32[]{:S(2)}, u32[]{:S(2)}) collective-permute-start(f32[24,512]{1,0:T(8,128)S(1)} %add.50), channel_id=1, source_target_pairs={{0,12},{1,13},{2,14},{3,15},{4,8},{5,9},{6,10},{7,11},{8,4},{9,5},... | collective-permute-start | bytes 147464 | tf_op jit(solution)/shard_map/ppermute | solution.py:272
  21.9 1.0 collective-permute-start.6
  22.9 1.5 %collective-permute-start.5 = (f32[24,512]{1,0:T(8,128)S(1)}, f32[24,512]{1,0:T(8,128)S(1)}, u32[]{:S(2)}, u32[]{:S(2)}) collective-permute-start(f32[24,512]{1,0:T(8,128)S(1)} %add.50), channel_id=1, source_target_pairs={{0,4},{1,5},{2,6},{3,7},{4,0},{5,1},{6,2},{7,3},{8,12},{9,13},{10,... | collective-permute-start | bytes 147464 | tf_op jit(solution)/shard_map/ppermute | solution.py:272
  24.4 0.0 copy-start.3
  24.4 0.0 copy-start.4
  24.4 1.4 %shard_map.96 = (f32[144,512]{1,0:T(8,128)S(1)}, f32[144,512]{1,0:T(8,128)S(1)}) custom-call(f32[384,1024]{1,0:T(8,128)S(1)} %bitcast.14, bf16[1024,1024]{1,0:T(8,128)(2,1)S(1)} %shard_map.95.refs_1_.select.refs_4_.refs_6_), custom_call_target="tpu_custom_call" | custom-call | tf_op jit(solution)/shard_map/pallas_call | solution.py:310
  25.9 0.0 copy-start.2
  25.9 0.0 collective-permute-done.7
  25.9 2.7 %collective-permute-start = (f32[144,512]{1,0:T(8,128)S(1)}, f32[144,512]{1,0:T(8,128)S(1)}, u32[]{:S(2)}, u32[]{:S(2)}) collective-permute-start(f32[144,512]{1,0:T(8,128)S(1)} %get-tuple-element.18), channel_id=1, source_target_pairs={{0,32},{32,0},{64,96},{96,64},{128,160},{160,128},{192,224},{224,1... | collective-permute-start | bytes 884744 | tf_op jit(solution)/shard_map/ppermute | solution.py:258
  28.6 1.4 %collective-permute-done.6 = f32[24,512]{1,0:T(8,128)S(1)} collective-permute-done((f32[24,512]{1,0:T(8,128)S(1)}, f32[24,512]{1,0:T(8,128)S(1)}, u32[]{:S(2)}, u32[]{:S(2)}) %collective-permute-start.6) | collective-permute-done | bytes 49184 | tf_op jit(solution)/shard_map/ppermute | solution.py:272
  30.0 1.3 %collective-permute-start.1 = (f32[144,512]{1,0:T(8,128)S(1)}, f32[144,512]{1,0:T(8,128)S(1)}, u32[]{:S(2)}, u32[]{:S(2)}) collective-permute-start(f32[144,512]{1,0:T(8,128)S(1)} %get-tuple-element.19), channel_id=1, source_target_pairs={{32,64},{64,32},{96,128},{128,96},{160,192},{192,160},{224,0},{0,2... | collective-permute-start | bytes 884744 | tf_op jit(solution)/shard_map/ppermute | solution.py:259
  31.4 0.0 collective-permute-done.5
  31.4 0.1 collective-permute-start.8
  31.5 1.9 %shard_map.97 = (f32[8,1024]{1,0:T(8,128)S(1)}, f32[8,1024]{1,0:T(8,128)S(1)}) custom-call(bf16[1024,1024]{1,0:T(8,128)(2,1)S(1)} %shard_map.95.refs_1_.select.refs_4_.refs_6_, f32[1,1024]{1,0:T(1,128)S(1)} %broadcast_select_fusion.live, s32[1,512]{1,0:T(1,128)S(1)} %copy-done.5, f32[1,512]{1,0:T(1,128)S(1)} %copy-done.6), custom_call_target="tpu_custom_call" | custom-call | tf_op jit(solution)/shard_map/pallas_call | solution.py:317
  33.4 0.0 collective-permute-done.8
  33.5 11.1 %collective-permute-done.refs_5_ = f32[144,512]{1,0:T(8,128)S(1)} collective-permute-done((f32[144,512]{1,0:T(8,128)S(1)}, f32[144,512]{1,0:T(8,128)S(1)}, u32[]{:S(2)}, u32[]{:S(2)}) %collective-permute-start) | collective-permute-done | bytes 294944 | tf_op jit(solution)/shard_map/ppermute | solution.py:258
  44.6 0.0 collective-permute-done.1.refs_6_
  44.6 6.4 %shard_map.99 = (f32[144,1024]{1,0:T(8,128)S(1)}, f32[144,1024]{1,0:T(8,128)S(1)}, f32[24,1024]{1,0:T(8,128)S(1)}, f32[144,512]{1,0:T(8,128)S(1)}, f32[144,512]{1,0:T(8,128)S(1)}) custom-call(f32[384,1024]{1,0:T(8,128)S(1)} %bitcast.15, f32[384,1024]{1,0:T(8,128)S(1)} %bitcast.23, f32[384,1024]{1,0:T(8,128)S(1)} %bitcast.27, ...), custom_call_target="tpu_custom_call" | custom-call | tf_op jit(solution)/shard_map/pallas_call | solution.py:333
  50.9 0.0 collective-permute-done.11.refs_5_
  51.0 0.0 collective-permute-done.12.refs_6_
  51.0 8.1 %shard_map.101 = (f32[240,1024]{1,0:T(8,128)S(1)}, f32[240,1024]{1,0:T(8,128)S(1)}, f32[24,1024]{1,0:T(8,128)S(1)}, f32[240,512]{1,0:T(8,128)S(1)}, f32[240,512]{1,0:T(8,128)S(1)}) custom-call(f32[384,1024]{1,0:T(8,128)S(1)} %bitcast.16, f32[384,1024]{1,0:T(8,128)S(1)} %bitcast.24, f32[384,1024]{1,0:T(8,128)S(1)} %bitcast.28, ...), custom_call_target="tpu_custom_call" | custom-call | tf_op jit(solution)/shard_map/pallas_call | solution.py:333
  59.1 0.1 collective-permute-start.13
  59.2 1.2 %collective-permute-done.13 = f32[24,512]{1,0:T(8,128)S(1)} collective-permute-done((f32[24,512]{1,0:T(8,128)S(1)}, f32[24,512]{1,0:T(8,128)S(1)}, u32[]{:S(2)}, u32[]{:S(2)}) %collective-permute-start.13) | collective-permute-done | bytes 49184 | tf_op jit(solution)/shard_map/ppermute | solution.py:268
  60.4 1.3 %collective-permute-start.14 = (f32[24,512]{1,0:T(8,128)S(1)}, f32[24,512]{1,0:T(8,128)S(1)}, u32[]{:S(2)}, u32[]{:S(2)}) collective-permute-start(f32[24,512]{1,0:T(8,128)S(1)} %select_add_fusion), channel_id=1, source_target_pairs={{0,16},{1,17},{2,18},{3,19},{4,20},{5,21},{6,22},{7,23},{8,24},{9,... | collective-permute-start | bytes 147464 | tf_op jit(solution)/shard_map/ppermute | solution.py:272
  61.7 4.4 %collective-permute-done.14 = f32[24,512]{1,0:T(8,128)S(1)} collective-permute-done((f32[24,512]{1,0:T(8,128)S(1)}, f32[24,512]{1,0:T(8,128)S(1)}, u32[]{:S(2)}, u32[]{:S(2)}) %collective-permute-start.14) | collective-permute-done | bytes 49184 | tf_op jit(solution)/shard_map/ppermute | solution.py:272
  66.1 2.2 %collective-permute-start.15 = (f32[24,512]{1,0:T(8,128)S(1)}, f32[24,512]{1,0:T(8,128)S(1)}, u32[]{:S(2)}, u32[]{:S(2)}) collective-permute-start(f32[24,512]{1,0:T(8,128)S(1)} %add.56), channel_id=1, source_target_pairs={{0,2},{1,3},{2,0},{3,1},{4,6},{5,7},{6,4},{7,5},{8,10},{9,11},{10,... | collective-permute-start | bytes 147464 | tf_op jit(solution)/shard_map/ppermute | solution.py:272
  68.3 2.2 %collective-permute-done.15 = f32[24,512]{1,0:T(8,128)S(1)} collective-permute-done((f32[24,512]{1,0:T(8,128)S(1)}, f32[24,512]{1,0:T(8,128)S(1)}, u32[]{:S(2)}, u32[]{:S(2)}) %collective-permute-start.15) | collective-permute-done | bytes 49184 | tf_op jit(solution)/shard_map/ppermute | solution.py:272
  70.5 6.4 %collective-permute-start.18 = (f32[24,512]{1,0:T(8,128)S(1)}, f32[24,512]{1,0:T(8,128)S(1)}, u32[]{:S(2)}, u32[]{:S(2)}) collective-permute-start(f32[24,512]{1,0:T(8,128)S(1)} %add.57), channel_id=1, source_target_pairs={{0,12},{1,13},{2,14},{3,15},{4,8},{5,9},{6,10},{7,11},{8,4},{9,5},... | collective-permute-start | bytes 147464 | tf_op jit(solution)/shard_map/ppermute | solution.py:272
  76.9 1.0 collective-permute-start.17
  77.8 1.5 %collective-permute-start.16 = (f32[24,512]{1,0:T(8,128)S(1)}, f32[24,512]{1,0:T(8,128)S(1)}, u32[]{:S(2)}, u32[]{:S(2)}) collective-permute-start(f32[24,512]{1,0:T(8,128)S(1)} %add.57), channel_id=1, source_target_pairs={{0,4},{1,5},{2,6},{3,7},{4,0},{5,1},{6,2},{7,3},{8,12},{9,13},{10,... | collective-permute-start | bytes 147464 | tf_op jit(solution)/shard_map/ppermute | solution.py:272
  79.3 1.3 %collective-permute-start.9 = (f32[144,512]{1,0:T(8,128)S(1)}, f32[144,512]{1,0:T(8,128)S(1)}, u32[]{:S(2)}, u32[]{:S(2)}) collective-permute-start(f32[144,512]{1,0:T(8,128)S(1)} %get-tuple-element.24), channel_id=1, source_target_pairs={{0,32},{32,0},{64,96},{96,64},{128,160},{160,128},{192,224},{224,1... | collective-permute-start | bytes 884744 | tf_op jit(solution)/shard_map/ppermute | solution.py:258
  80.7 1.6 %collective-permute-start.10 = (f32[144,512]{1,0:T(8,128)S(1)}, f32[144,512]{1,0:T(8,128)S(1)}, u32[]{:S(2)}, u32[]{:S(2)}) collective-permute-start(f32[144,512]{1,0:T(8,128)S(1)} %get-tuple-element.25), channel_id=1, source_target_pairs={{32,64},{64,32},{96,128},{128,96},{160,192},{192,160},{224,0},{0,2... | collective-permute-start | bytes 884744 | tf_op jit(solution)/shard_map/ppermute | solution.py:259
  82.3 0.0 collective-permute-done.18
  82.3 2.6 %collective-permute-start.20 = (f32[240,512]{1,0:T(8,128)S(1)}, f32[240,512]{1,0:T(8,128)S(1)}, u32[]{:S(2)}, u32[]{:S(2)}) collective-permute-start(f32[240,512]{1,0:T(8,128)S(1)} %get-tuple-element.32), channel_id=1, source_target_pairs={{0,32},{32,0},{64,96},{96,64},{128,160},{160,128},{192,224},{224,1... | collective-permute-start | bytes 1474568 | tf_op jit(solution)/shard_map/ppermute | solution.py:258
  84.9 0.0 collective-permute-done.17
  84.9 2.3 %collective-permute-start.21 = (f32[240,512]{1,0:T(8,128)S(1)}, f32[240,512]{1,0:T(8,128)S(1)}, u32[]{:S(2)}, u32[]{:S(2)}) collective-permute-start(f32[240,512]{1,0:T(8,128)S(1)} %get-tuple-element.33), channel_id=1, source_target_pairs={{32,64},{64,32},{96,128},{128,96},{160,192},{192,160},{224,0},{0,2... | collective-permute-start | bytes 1474568 | tf_op jit(solution)/shard_map/ppermute | solution.py:259
  87.2 0.0 collective-permute-done.16
  87.2 0.1 collective-permute-start.19
  87.3 1.2 %collective-permute-done.19 = f32[24,512]{1,0:T(8,128)S(1)} collective-permute-done((f32[24,512]{1,0:T(8,128)S(1)}, f32[24,512]{1,0:T(8,128)S(1)}, u32[]{:S(2)}, u32[]{:S(2)}) %collective-permute-start.19) | collective-permute-done | bytes 49184 | tf_op jit(solution)/shard_map/ppermute | solution.py:276
  88.6 15.9 %collective-permute-done.9.refs_7_ = f32[144,512]{1,0:T(8,128)S(1)} collective-permute-done((f32[144,512]{1,0:T(8,128)S(1)}, f32[144,512]{1,0:T(8,128)S(1)}, u32[]{:S(2)}, u32[]{:S(2)}) %collective-permute-start.9) | collective-permute-done | bytes 294944 | tf_op jit(solution)/shard_map/ppermute | solution.py:258
  104.4 0.0 collective-permute-done.10.refs_8_
  104.4 4.9 %shard_map.102 = f32[144,1024]{1,0:T(8,128)S(1)} custom-call(f32[384,1024]{1,0:T(8,128)S(1)} %bitcast.17, f32[144,1024]{1,0:T(8,128)S(1)} %get-tuple-element.22.refs_1_, f32[144,1024]{1,0:T(8,128)S(1)} %get-tuple-element.23.refs_2_, f32[384,1024]{1,0:T(8,128)S(1)} %bitcast.25, f32[384,1024]{1,0:T(8,128)S(1)} %bitcast.29, bf16[1024,1024]{1,0:T(8,128)(2,1)S(1)} %bitcast.21, ...), custom_call_target="tpu_custom_call" | custom-call | tf_op jit(solution)/shard_map/pallas_call | solution.py:351
  109.3 0.7 fusion.2
  110.0 2.9 %collective-permute-done.20.refs_7_ = f32[240,512]{1,0:T(8,128)S(1)} collective-permute-done((f32[240,512]{1,0:T(8,128)S(1)}, f32[240,512]{1,0:T(8,128)S(1)}, u32[]{:S(2)}, u32[]{:S(2)}) %collective-permute-start.20) | collective-permute-done | bytes 491552 | tf_op jit(solution)/shard_map/ppermute | solution.py:258
  112.9 0.0 collective-permute-done.21.refs_8_
  112.9 6.1 %shard_map.103 = f32[240,1024]{1,0:T(8,128)S(1)} custom-call(f32[384,1024]{1,0:T(8,128)S(1)} %bitcast.18, f32[240,1024]{1,0:T(8,128)S(1)} %get-tuple-element.30.refs_1_, f32[240,1024]{1,0:T(8,128)S(1)} %get-tuple-element.31.refs_2_, f32[384,1024]{1,0:T(8,128)S(1)} %bitcast.26, f32[384,1024]{1,0:T(8,128)S(1)} %bitcast.30, bf16[1024,1024]{1,0:T(8,128)(2,1)S(1)} %bitcast.22, ...), custom_call_target="tpu_custom_call" | custom-call | tf_op jit(solution)/shard_map/pallas_call | solution.py:351
  119.0 1.3 %pad_maximum_fusion = f32[384,1024]{1,0:T(8,128)} fusion(f32[240,1024]{1,0:T(8,128)S(1)} %shard_map.103, f32[144,1024]{1,0:T(8,128)S(1)} %shard_map.102), kind=kLoop, calls=%fused_computation | loop fusion | flops 393216 | bytes 3145728 | tf_op jit(solution)/shard_map/concatenate | solution.py:358
  (27 shorter events, 0.2 us)
Async XLA Ops:
  0.6 1.7 %copy-start.7 = (s32[1,2,512]{2,1,0:T(2,128)S(1)}, s32[1,2,512]{2,1,0:T(2,128)}, u32[]{:S(2)}) copy-start(s32[1,2,512]{2,1,0:T(2,128)} %param.14) | copy-start | bytes 12292
  0.7 1.4 %copy-start = (f32[1,16,24,1024]{3,2,1,0:T(8,128)S(1)}, f32[1,16,24,1024]{3,2,1,0:T(8,128)}, u32[]{:S(2)}) copy-start(f32[1,16,24,1024]{3,2,1,0:T(8,128)} %param.8) | copy-start | bytes 4718596
  2.2 4.2 %copy-start.1 = (f32[1,16,24,1024]{3,2,1,0:T(8,128)S(1)}, f32[1,16,24,1024]{3,2,1,0:T(8,128)}, u32[]{:S(2)}) copy-start(f32[1,16,24,1024]{3,2,1,0:T(8,128)} %param.8) | copy-start | bytes 4718596
  2.2 1.3 %collective-permute-start.2 = (f32[24,512]{1,0:T(8,128)S(1)}, f32[24,512]{1,0:T(8,128)S(1)}, u32[]{:S(2)}, u32[]{:S(2)}) collective-permute-start(f32[24,512]{1,0:T(8,128)S(1)} %slice_select_fusion.1), channel_id=1, source_target_pairs={{0,1},{1,0},{2,3},{3,2},{4,5},{5,4},{6,7},{7,6},{8,9},{9,8},{10,11... | collective-permute-start | bytes 147464 | tf_op jit(solution)/shard_map/ppermute | solution.py:268
  3.6 7.8 %collective-permute-start.3 = (f32[24,512]{1,0:T(8,128)S(1)}, f32[24,512]{1,0:T(8,128)S(1)}, u32[]{:S(2)}, u32[]{:S(2)}) collective-permute-start(f32[24,512]{1,0:T(8,128)S(1)} %select_add_fusion.1), channel_id=1, source_target_pairs={{0,16},{1,17},{2,18},{3,19},{4,20},{5,21},{6,22},{7,23},{8,24},{9,... | collective-permute-start | bytes 147464 | tf_op jit(solution)/shard_map/ppermute | solution.py:272
  6.4 7.0 %copy-start.8 = (s32[1,2]{1,0:T(1,128)S(1)}, s32[1,2]{1,0:T(1,128)}, u32[]{:S(2)}) copy-start(s32[1,2]{1,0:T(1,128)} %param.15) | copy-start | bytes 28
  8.3 42.6 %collective-permute-start.11 = (f32[240,512]{1,0:T(8,128)S(1)}, f32[240,512]{1,0:T(8,128)S(1)}, u32[]{:S(2)}, u32[]{:S(2)}) collective-permute-start(f32[240,512]{1,0:T(8,128)S(1)} %get-tuple-element.26), channel_id=1, source_target_pairs={{0,32},{32,0},{64,96},{96,64},{128,160},{160,128},{192,224},{224,1... | collective-permute-start | bytes 1474568 | tf_op jit(solution)/shard_map/ppermute | solution.py:258
  9.7 41.2 %collective-permute-start.12 = (f32[240,512]{1,0:T(8,128)S(1)}, f32[240,512]{1,0:T(8,128)S(1)}, u32[]{:S(2)}, u32[]{:S(2)}) collective-permute-start(f32[240,512]{1,0:T(8,128)S(1)} %get-tuple-element.27), channel_id=1, source_target_pairs={{32,64},{64,32},{96,128},{128,96},{160,192},{192,160},{224,0},{0,2... | collective-permute-start | bytes 1474568 | tf_op jit(solution)/shard_map/ppermute | solution.py:259
  11.3 4.2 %collective-permute-start.4 = (f32[24,512]{1,0:T(8,128)S(1)}, f32[24,512]{1,0:T(8,128)S(1)}, u32[]{:S(2)}, u32[]{:S(2)}) collective-permute-start(f32[24,512]{1,0:T(8,128)S(1)} %add.49), channel_id=1, source_target_pairs={{0,2},{1,3},{2,0},{3,1},{4,6},{5,7},{6,4},{7,5},{8,10},{9,11},{10,... | collective-permute-start | bytes 147464 | tf_op jit(solution)/shard_map/ppermute | solution.py:272
  15.5 10.3 %collective-permute-start.7 = (f32[24,512]{1,0:T(8,128)S(1)}, f32[24,512]{1,0:T(8,128)S(1)}, u32[]{:S(2)}, u32[]{:S(2)}) collective-permute-start(f32[24,512]{1,0:T(8,128)S(1)} %add.50), channel_id=1, source_target_pairs={{0,12},{1,13},{2,14},{3,15},{4,8},{5,9},{6,10},{7,11},{8,4},{9,5},... | collective-permute-start | bytes 147464 | tf_op jit(solution)/shard_map/ppermute | solution.py:272
  21.9 8.1 %collective-permute-start.6 = (f32[24,512]{1,0:T(8,128)S(1)}, f32[24,512]{1,0:T(8,128)S(1)}, u32[]{:S(2)}, u32[]{:S(2)}) collective-permute-start(f32[24,512]{1,0:T(8,128)S(1)} %add.50), channel_id=1, source_target_pairs={{0,8},{1,9},{2,10},{3,11},{4,12},{5,13},{6,14},{7,15},{8,0},{9,1},... | collective-permute-start | bytes 147464 | tf_op jit(solution)/shard_map/ppermute | solution.py:272
  22.9 8.4 %collective-permute-start.5 = (f32[24,512]{1,0:T(8,128)S(1)}, f32[24,512]{1,0:T(8,128)S(1)}, u32[]{:S(2)}, u32[]{:S(2)}) collective-permute-start(f32[24,512]{1,0:T(8,128)S(1)} %add.50), channel_id=1, source_target_pairs={{0,4},{1,5},{2,6},{3,7},{4,0},{5,1},{6,2},{7,3},{8,12},{9,13},{10,... | collective-permute-start | bytes 147464 | tf_op jit(solution)/shard_map/ppermute | solution.py:272
  24.4 7.1 %copy-start.5 = (s32[1,512]{1,0:T(1,128)S(1)}, s32[1,512]{1,0:T(1,128)}, u32[]{:S(2)}) copy-start(s32[1,512]{1,0:T(1,128)} %gen_bus.1) | copy-start | bytes 6148
  24.4 7.1 %copy-start.6 = (f32[1,512]{1,0:T(1,128)S(1)}, f32[1,512]{1,0:T(1,128)}, u32[]{:S(2)}) copy-start(f32[1,512]{1,0:T(1,128)} %gen_cap.1) | copy-start | bytes 6148
  24.4 20.2 %copy-start.3 = (f32[1,16,24,1024]{3,2,1,0:T(8,128)S(1)}, f32[1,16,24,1024]{3,2,1,0:T(8,128)}, u32[]{:S(2)}) copy-start(f32[1,16,24,1024]{3,2,1,0:T(8,128)} %param.9) | copy-start | bytes 4718596
  24.4 20.2 %copy-start.4 = (f32[1,16,24,1024]{3,2,1,0:T(8,128)S(1)}, f32[1,16,24,1024]{3,2,1,0:T(8,128)}, u32[]{:S(2)}) copy-start(f32[1,16,24,1024]{3,2,1,0:T(8,128)} %param.10) | copy-start | bytes 4718596
  25.9 18.7 %copy-start.2 = (bf16[1,1024,1024]{2,1,0:T(8,128)(2,1)S(1)}, bf16[1,1024,1024]{2,1,0:T(8,128)(2,1)}, u32[]{:S(2)}) copy-start(bf16[1,1024,1024]{2,1,0:T(8,128)(2,1)} %param.11) | copy-start | bytes 6291460
  25.9 18.7 %collective-permute-start = (f32[144,512]{1,0:T(8,128)S(1)}, f32[144,512]{1,0:T(8,128)S(1)}, u32[]{:S(2)}, u32[]{:S(2)}) collective-permute-start(f32[144,512]{1,0:T(8,128)S(1)} %get-tuple-element.18), channel_id=1, source_target_pairs={{0,32},{32,0},{64,96},{96,64},{128,160},{160,128},{192,224},{224,1... | collective-permute-start | bytes 884744 | tf_op jit(solution)/shard_map/ppermute | solution.py:258
  30.0 14.5 %collective-permute-start.1 = (f32[144,512]{1,0:T(8,128)S(1)}, f32[144,512]{1,0:T(8,128)S(1)}, u32[]{:S(2)}, u32[]{:S(2)}) collective-permute-start(f32[144,512]{1,0:T(8,128)S(1)} %get-tuple-element.19), channel_id=1, source_target_pairs={{32,64},{64,32},{96,128},{128,96},{160,192},{192,160},{224,0},{0,2... | collective-permute-start | bytes 884744 | tf_op jit(solution)/shard_map/ppermute | solution.py:259
  31.4 2.1 %collective-permute-start.8 = (f32[24,512]{1,0:T(8,128)S(1)}, f32[24,512]{1,0:T(8,128)S(1)}, u32[]{:S(2)}, u32[]{:S(2)}) collective-permute-start(f32[24,512]{1,0:T(8,128)S(1)} %add_add_fusion.1), channel_id=1, source_target_pairs={{0,1},{1,0},{2,3},{3,2},{4,5},{5,4},{6,7},{7,6},{8,9},{9,8},{10,11... | collective-permute-start | bytes 147464 | tf_op jit(solution)/shard_map/ppermute | solution.py:276
  59.1 1.3 %collective-permute-start.13 = (f32[24,512]{1,0:T(8,128)S(1)}, f32[24,512]{1,0:T(8,128)S(1)}, u32[]{:S(2)}, u32[]{:S(2)}) collective-permute-start(f32[24,512]{1,0:T(8,128)S(1)} %slice_select_fusion), channel_id=1, source_target_pairs={{0,1},{1,0},{2,3},{3,2},{4,5},{5,4},{6,7},{7,6},{8,9},{9,8},{10,11... | collective-permute-start | bytes 147464 | tf_op jit(solution)/shard_map/ppermute | solution.py:268
  60.4 5.7 %collective-permute-start.14 = (f32[24,512]{1,0:T(8,128)S(1)}, f32[24,512]{1,0:T(8,128)S(1)}, u32[]{:S(2)}, u32[]{:S(2)}) collective-permute-start(f32[24,512]{1,0:T(8,128)S(1)} %select_add_fusion), channel_id=1, source_target_pairs={{0,16},{1,17},{2,18},{3,19},{4,20},{5,21},{6,22},{7,23},{8,24},{9,... | collective-permute-start | bytes 147464 | tf_op jit(solution)/shard_map/ppermute | solution.py:272
  66.1 4.4 %collective-permute-start.15 = (f32[24,512]{1,0:T(8,128)S(1)}, f32[24,512]{1,0:T(8,128)S(1)}, u32[]{:S(2)}, u32[]{:S(2)}) collective-permute-start(f32[24,512]{1,0:T(8,128)S(1)} %add.56), channel_id=1, source_target_pairs={{0,2},{1,3},{2,0},{3,1},{4,6},{5,7},{6,4},{7,5},{8,10},{9,11},{10,... | collective-permute-start | bytes 147464 | tf_op jit(solution)/shard_map/ppermute | solution.py:272
  70.5 11.8 %collective-permute-start.18 = (f32[24,512]{1,0:T(8,128)S(1)}, f32[24,512]{1,0:T(8,128)S(1)}, u32[]{:S(2)}, u32[]{:S(2)}) collective-permute-start(f32[24,512]{1,0:T(8,128)S(1)} %add.57), channel_id=1, source_target_pairs={{0,12},{1,13},{2,14},{3,15},{4,8},{5,9},{6,10},{7,11},{8,4},{9,5},... | collective-permute-start | bytes 147464 | tf_op jit(solution)/shard_map/ppermute | solution.py:272
  76.9 8.1 %collective-permute-start.17 = (f32[24,512]{1,0:T(8,128)S(1)}, f32[24,512]{1,0:T(8,128)S(1)}, u32[]{:S(2)}, u32[]{:S(2)}) collective-permute-start(f32[24,512]{1,0:T(8,128)S(1)} %add.57), channel_id=1, source_target_pairs={{0,8},{1,9},{2,10},{3,11},{4,12},{5,13},{6,14},{7,15},{8,0},{9,1},... | collective-permute-start | bytes 147464 | tf_op jit(solution)/shard_map/ppermute | solution.py:272
  77.8 9.4 %collective-permute-start.16 = (f32[24,512]{1,0:T(8,128)S(1)}, f32[24,512]{1,0:T(8,128)S(1)}, u32[]{:S(2)}, u32[]{:S(2)}) collective-permute-start(f32[24,512]{1,0:T(8,128)S(1)} %add.57), channel_id=1, source_target_pairs={{0,4},{1,5},{2,6},{3,7},{4,0},{5,1},{6,2},{7,3},{8,12},{9,13},{10,... | collective-permute-start | bytes 147464 | tf_op jit(solution)/shard_map/ppermute | solution.py:272
  79.3 25.1 %collective-permute-start.9 = (f32[144,512]{1,0:T(8,128)S(1)}, f32[144,512]{1,0:T(8,128)S(1)}, u32[]{:S(2)}, u32[]{:S(2)}) collective-permute-start(f32[144,512]{1,0:T(8,128)S(1)} %get-tuple-element.24), channel_id=1, source_target_pairs={{0,32},{32,0},{64,96},{96,64},{128,160},{160,128},{192,224},{224,1... | collective-permute-start | bytes 884744 | tf_op jit(solution)/shard_map/ppermute | solution.py:258
  80.7 23.8 %collective-permute-start.10 = (f32[144,512]{1,0:T(8,128)S(1)}, f32[144,512]{1,0:T(8,128)S(1)}, u32[]{:S(2)}, u32[]{:S(2)}) collective-permute-start(f32[144,512]{1,0:T(8,128)S(1)} %get-tuple-element.25), channel_id=1, source_target_pairs={{32,64},{64,32},{96,128},{128,96},{160,192},{192,160},{224,0},{0,2... | collective-permute-start | bytes 884744 | tf_op jit(solution)/shard_map/ppermute | solution.py:259
  82.3 30.6 %collective-permute-start.20 = (f32[240,512]{1,0:T(8,128)S(1)}, f32[240,512]{1,0:T(8,128)S(1)}, u32[]{:S(2)}, u32[]{:S(2)}) collective-permute-start(f32[240,512]{1,0:T(8,128)S(1)} %get-tuple-element.32), channel_id=1, source_target_pairs={{0,32},{32,0},{64,96},{96,64},{128,160},{160,128},{192,224},{224,1... | collective-permute-start | bytes 1474568 | tf_op jit(solution)/shard_map/ppermute | solution.py:258
  84.9 28.0 %collective-permute-start.21 = (f32[240,512]{1,0:T(8,128)S(1)}, f32[240,512]{1,0:T(8,128)S(1)}, u32[]{:S(2)}, u32[]{:S(2)}) collective-permute-start(f32[240,512]{1,0:T(8,128)S(1)} %get-tuple-element.33), channel_id=1, source_target_pairs={{32,64},{64,32},{96,128},{128,96},{160,192},{192,160},{224,0},{0,2... | collective-permute-start | bytes 1474568 | tf_op jit(solution)/shard_map/ppermute | solution.py:259
  87.2 1.3 %collective-permute-start.19 = (f32[24,512]{1,0:T(8,128)S(1)}, f32[24,512]{1,0:T(8,128)S(1)}, u32[]{:S(2)}, u32[]{:S(2)}) collective-permute-start(f32[24,512]{1,0:T(8,128)S(1)} %add_add_fusion), channel_id=1, source_target_pairs={{0,1},{1,0},{2,3},{3,2},{4,5},{5,4},{6,7},{7,6},{8,9},{9,8},{10,11... | collective-permute-start | bytes 147464 | tf_op jit(solution)/shard_map/ppermute | solution.py:276

commit v2 on v1

v2 whole, which is shorter than its diff:
```python
import jax
import jax.numpy as jnp
from jax import lax
from jax.experimental import pallas as pl
from jax.experimental.pallas import tpu as pltpu
from jax.sharding import PartitionSpec as P


CHUNKS = (6, 10)
BLOCK = 256
step_rate = 0.3
tie_weight = 1.0
day_weight = 0.5


F32 = jnp.float32
BF16 = jnp.bfloat16


def dot(a, b):
    return lax.dot_general(a, b, (((1,), (0,)), ((), ())), preferred_element_type=F32)


def dot_t(a, b):
    return lax.dot_general(a, b, (((1,), (1,)), ((), ())), preferred_element_type=F32)


def high_low(x):
    high = x.astype(BF16)
    return high, (x - high.astype(F32)).astype(BF16)


def call(kernel, outs, *, n_in, scratch=()):
    vmem = pl.BlockSpec(memory_space=pltpu.VMEM)
    return pl.pallas_call(
        kernel,
        out_shape=outs,
        in_specs=[vmem] * n_in,
        out_specs=jax.tree.map(lambda _: vmem, outs),
        scratch_shapes=list(scratch),
        compiler_params=pltpu.CompilerParams(vmem_limit_bytes=24 << 20),
    )


def over_scenarios(value, hours):
    rows, width = value.shape
    return jnp.sum(value.reshape(rows // hours, hours, width), axis=0)


def for_scenarios(value, rows):
    hours, width = value.shape
    return jnp.broadcast_to(value[None], (rows // hours, hours, width)).reshape(rows, width)


def over_blocks(width, one):
    for n in range(width // BLOCK):
        one(pl.ds(n * BLOCK, BLOCK))


def sum_kernel(state, out):
    hours = out.shape[0]

    def one(n, _):
        at = pl.ds(pl.multiple_of(n * BLOCK, BLOCK), BLOCK)
        out[:, at] = over_scenarios(state[:, at], hours)
        return 0

    lax.fori_loop(0, out.shape[1] // BLOCK, one, 0)


def select_kernel(index, out):
    rows = 128

    def one(n, _):
        start = pl.multiple_of(n * rows, rows)
        bus = lax.broadcasted_iota(jnp.int32, (rows, out.shape[1]), 0) + start
        out[pl.ds(start, rows), :] = jnp.where(bus == index[...], 1.0, 0.0).astype(BF16)
        return 0

    lax.fori_loop(0, out.shape[0] // rows, one, 0)


def split_into(pair, value, at):
    rows = value.shape[0]
    high, low = high_low(value)
    pair[:rows, at] = high
    pair[rows:, at] = low


def pick_kernel(start, state, select, left, right, pair):
    rows, slots = left.shape
    over_blocks(state.shape[1], lambda at: split_into(pair, state[start : start + rows, at], at))

    def one(at):
        both = dot(pair[...], select[:, at])
        out, base = (left, 0) if at.start < slots else (right, slots)
        out[:, pl.ds(at.start - base, at.size)] = both[:rows] + both[rows:]

    over_blocks(2 * slots, one)


def bounds_kernel(select, live, gen_bus, gen_cap, mask, upper):
    mask[...] = dot_t(jnp.broadcast_to(live[...], (8, live.shape[1])).astype(BF16), select[...])
    caps = jnp.broadcast_to(gen_cap[...], (8, gen_cap.shape[1]))
    high, rest = high_low(caps)
    middle, low = high_low(caps - high.astype(F32))
    del rest
    three = jnp.concatenate([high, middle, low], axis=0)
    rows = 128

    def one(n, _):
        start = pl.multiple_of(n * rows, rows)
        bus = lax.broadcasted_iota(jnp.int32, (rows, gen_bus.shape[1]), 0) + start
        chosen = jnp.where(bus == gen_bus[...], 1.0, 0.0).astype(BF16)
        parts = dot_t(three, chosen)
        upper[:, pl.ds(start, rows)] = parts[:8] + parts[8:16] + parts[16:]
        return 0

    lax.fori_loop(0, upper.shape[1] // rows, one, 0)


def theirs_into(pair, left, right):
    slots = left.shape[1]
    split_into(pair, left[...], pl.ds(0, slots))
    split_into(pair, right[...], pl.ds(slots, slots))


def theirs_at(pair, select, at):
    both = dot_t(pair[...], select[at, :])
    rows = both.shape[0] // 2
    return both[:rows] + both[rows:]


def stepped(now, slope, base, mask, lower, upper):
    slope = slope + base + (tie_weight * mask + day_weight) * now
    return jnp.minimum(jnp.maximum(now - step_rate * slope, lower), upper)


def first_kernel(start, state0, price, demand, matrix, select, left, right, mask, upper, plan, out, dual_out, total, even, other, base, pair):
    rows, buses = out.shape
    hours = plan.shape[0]
    part = slice(start, start + rows)
    theirs_into(pair, left, right)

    def load(at):
        even[:, at] = state0[part, at].astype(BF16)

    over_blocks(buses, load)

    def zero(at):
        now = state0[part, at]
        theirs = theirs_at(pair, select, at)
        middle = 0.5 * (now + theirs)
        dual = now - middle
        target = mask[:1, at] * (middle - dual)
        dual_out[:, at] = dual
        day_plan = for_scenarios(plan[:, at], rows)
        day_dual = now - day_plan
        constant = price[part, at] - tie_weight * mask[:1, at] * target + day_weight * (day_dual - day_plan)
        base[:, at] = constant
        new = stepped(now, dot(even[...], matrix[:, at]), constant, mask[:1, at], -demand[part, at], upper[:1, at])
        out[:, at] = new
        other[:, at] = new.astype(BF16)

    def one(at):
        new = stepped(out[:, at], dot(other[...], matrix[:, at]), base[:, at], mask[:1, at], -demand[part, at], upper[:1, at])
        out[:, at] = new
        even[:, at] = new.astype(BF16)

    def two(at):
        new = stepped(out[:, at], dot(even[...], matrix[:, at]), base[:, at], mask[:1, at], -demand[part, at], upper[:1, at])
        out[:, at] = new
        day_plan = for_scenarios(plan[:, at], rows)
        total[:, at] = over_scenarios(new + (state0[part, at] - day_plan), hours)

    over_blocks(buses, zero)
    over_blocks(buses, one)
    over_blocks(buses, two)


def prepare_kernel(start, state0, state1, dual1, price, select, left, right, mask, plan1, base, pair):
    rows, buses = base.shape
    part = slice(start, start + rows)
    theirs_into(pair, left, right)

    def zero(at):
        now = state1[:, at]
        middle = 0.5 * (now + theirs_at(pair, select, at))
        dual = dual1[:, at] + now - middle
        target = mask[:1, at] * (middle - dual)
        day_dual = state0[part, at] - for_scenarios(plan1[:, at], rows)
        base[:, at] = price[part, at] - tie_weight * mask[:1, at] * target + day_weight * (day_dual + now)

    over_blocks(buses, zero)


def final_kernel(*refs):
    count = len(CHUNKS)
    states, bases = refs[:count], refs[count : 2 * count]
    demand, matrix, mask, upper, plan, out, plan_out, even, other, base = refs[2 * count :]
    buses = out.shape[1]
    ends = [sum(r.shape[0] for r in states[:c]) for c in range(count + 1)]
    plan_out[...] = plan[...]

    def load(at):
        for c in range(count):
            even[ends[c] : ends[c + 1], at] = states[c][:, at].astype(BF16)

    over_blocks(buses, load)

    def step(source, target, first, last):
        def one(at):
            slope = dot(source[...], matrix[:, at])
            for c in range(count):
                part = slice(ends[c], ends[c + 1])
                if first:
                    day_plan = for_scenarios(plan[:, at], ends[c + 1] - ends[c])
                    constant = bases[c][:, at] - 2 * day_weight * day_plan
                    base[part, at] = constant
                    now = states[c][:, at]
                else:
                    constant = base[part, at]
                    now = out[part, at]
                new = stepped(now, slope[part], constant, mask[:1, at], -demand[part, at], upper[:1, at])
                out[part, at] = new
                if not last:
                    target[part, at] = new.astype(BF16)

        over_blocks(buses, one)

    step(even, other, True, False)
    step(other, even, False, False)
    step(even, other, False, True)


def flipped(size, bit):
    return [(i, i ^ bit) for i in range(size)]


def borders(size, first):
    pairs = [((i + first) % size, (i + first + 1) % size) for i in range(0, size, 2)]
    return [pair for a, b in pairs for pair in ((a, b), (b, a))]


def exchange(a, b):
    size = lax.axis_size("region")
    return (
        lax.ppermute(a, "region", borders(size, 0)),
        lax.ppermute(b, "region", borders(size, 1)),
    )


def summed(total, core):
    size = lax.axis_size("scen")
    half = total.shape[1] // 2
    mine = jnp.where(core == 0, total[:, :half], total[:, half:])
    other = jnp.where(core == 0, total[:, half:], total[:, :half])
    part = mine + lax.ppermute(other, "scen", flipped(size, 1))
    for group in ((size // 2,), (2,), (4, 8, 12)):
        others = []
        for bit in group:
            others.append(lax.ppermute(part, "scen", flipped(size, bit)))
        part = part + others[0]
        if len(group) > 1:
            part = part + (others[1] + others[2])
    back = lax.ppermute(part, "scen", flipped(size, 1))
    return jnp.where(
        core == 0, jnp.concatenate([part, back], axis=1), jnp.concatenate([back, part], axis=1)
    )


def inner(start_state, price, demand, sens, gen_bus, gen_cap, tie_index, tie_len):
    scens, hours, buses = start_state.shape[1:]
    slots = tie_index.shape[2]
    rows = scens * hours
    total_scen = scens * lax.axis_size("scen")
    state0 = start_state.reshape(rows, buses)
    prices = price.reshape(rows, buses)
    demands = demand.reshape(rows, buses)
    matrix = sens[0]
    core = lax.axis_index("scen") % 2
    odd = lax.axis_index("region") % 2

    def by_border(pair):
        return jnp.where(odd == 0, jnp.concatenate([pair[1], pair[0]]), jnp.concatenate([pair[0], pair[1]]))[None]

    index = by_border(tie_index[0])
    live = (jnp.arange(slots, dtype=jnp.int32)[None, :] < tie_len[0][:, None]).astype(F32)
    live = by_border(live)

    def shape(*dims, dtype=F32):
        return jax.ShapeDtypeStruct(dims, dtype)

    def pick(at, state, size):
        return call(
            lambda *refs: pick_kernel(at, *refs),
            (shape(size, slots), shape(size, slots)),
            n_in=2,
            scratch=[pltpu.VMEM((2 * size, buses), BF16)],
        )(state, select)

    total0 = call(sum_kernel, shape(hours, buses), n_in=1)(state0)
    select = call(select_kernel, shape(buses, 2 * slots, dtype=BF16), n_in=1)(index)
    starts = [sum(CHUNKS[:c]) * hours for c in range(len(CHUNKS))]
    sizes = [c * hours for c in CHUNKS]
    theirs = []
    for at, size in zip(starts, sizes):
        picked = pick(at, state0, size)
        theirs.append(exchange(*picked))
    mask, upper = call(bounds_kernel, (shape(8, buses), shape(8, buses)), n_in=4)(select, live, gen_bus, gen_cap)
    plan1 = summed(total0, core) / total_scen

    firsts = []
    theirs1 = []
    for c, (at, size) in enumerate(zip(starts, sizes)):
        wide = shape(size, buses)
        first = call(
            lambda *refs, at=at: first_kernel(at, *refs),
            (wide, wide, shape(hours, buses)),
            n_in=10,
            scratch=[
                pltpu.VMEM((size, buses), BF16),
                pltpu.VMEM((size, buses), BF16),
                pltpu.VMEM((size, buses), F32),
                pltpu.VMEM((2 * size, buses), BF16),
            ],
        )(state0, prices, demands, matrix, select, *theirs[c], mask, upper, plan1)
        firsts.append(first)
        picked = pick(0, first[0], size)
        theirs1.append(exchange(*picked))
    total1 = sum(f[2] for f in firsts[1:]) + firsts[0][2]
    bases = []
    for c, (at, size) in enumerate(zip(starts, sizes)):
        bases.append(
            call(
                lambda *refs, at=at: prepare_kernel(at, *refs),
                shape(size, buses),
                n_in=9,
                scratch=[pltpu.VMEM((2 * size, buses), BF16)],
            )(state0, firsts[c][0], firsts[c][1], prices, select, *theirs1[c], mask, plan1)
        )
    plan2 = summed(total1, core) / total_scen
    final_state, plan2 = call(
        final_kernel,
        (shape(rows, buses), shape(hours, buses)),
        n_in=2 * len(CHUNKS) + 5,
        scratch=[
            pltpu.VMEM((rows, buses), BF16),
            pltpu.VMEM((rows, buses), BF16),
            pltpu.VMEM((rows, buses), F32),
        ],
    )(*[f[0] for f in firsts], *bases, demands, matrix, mask, upper, plan2)
    return (final_state.reshape(start_state.shape), plan2[None])


def solution(mesh):
    in_specs = (
        P("region", "scen", None, None),
        P("region", "scen", None, None),
        P("region", "scen", None, None),
        P("region", None, None),
        P("region", None),
        P("region", None),
        P("region", None, None),
        P("region", None),
    )
    out_specs = (P("region", "scen", None, None), P("region", None, None))
    return jax.shard_map(inner, mesh=mesh, in_specs=in_specs, out_specs=out_specs, check_vma=False)
```

time: 121 us -> 103 us (0.85)
  Pallas kernels: 31.2 us -> 18.8 us
  waiting for transfers between devices: 43.7 us -> 41.1 us
  other arithmetic: 2.2 us -> 0.23 us
  starting transfers between devices: 40.8 us -> 39.2 us
    pallas_call x6 -> x9, Pallas kernels: 28.8 us -> 16.4 us  [the longest x2 5.56 us: inner(): call(lambda *refs, at=at: first_kernel(at, *refs), (wide, wide, shape(hou...]
    ppermute x4, waiting for transfers between devices: 29.9 us -> 28 us  [exchange(): lax.ppermute(a, 'region', borders(size, 0))]
    concatenate x1 -> x0, other arithmetic: 1.32 us -> none  [inner(): final_state = jnp.concatenate(finals, axis=0).reshape(scens, hours, buses)]
    ppermute x2, waiting for transfers between devices: 1.22 us -> 0.01 us  [summed(): back = lax.ppermute(part, 'scen', flipped(size, 1))]
  transfers between devices with their start and end apart: 22 -> 22, of which waited for: 10 -> 8; matrix products, arithmetic and copies ran while one was open for 1% -> 0% of each run, Pallas kernels for 14% -> 9%
where the time goes in v2:
time: 103 us; the launch traced here: 102 us
  waiting for transfers between devices  41.1 us (40%)
  starting transfers between devices  39.2 us (38%)
  Pallas kernels  18.8 us (18%)
  local copies, waits for them, and re-layouts  1.46 us (1%)
  between operations  1.03 us (1%)
    ppermute x4, waiting for transfers between devices, exchange(): lax.ppermute(a, 'region', borders(size, 0))  28 us
    ppermute x10, starting transfers between devices, summed(): others.append(lax.ppermute(part, 'scen', flipped(size, bit)))  24.5 us
    ppermute x10, waiting for transfers between devices, summed(): others.append(lax.ppermute(part, 'scen', flipped(size, bit)))  10.7 us
    ppermute x4, starting transfers between devices, exchange(): lax.ppermute(a, 'region', borders(size, 0))  8.26 us
    ppermute x4, starting transfers between devices, exchange(): lax.ppermute(b, 'region', borders(size, 1))  5.85 us
    pallas_call x2, Pallas kernels, inner(): call(lambda *refs, at=at: first_kernel(at, *refs), (wide, wide, shape(hou...  5.56 us
    pallas_call x1, Pallas kernels, inner(): call(final_kernel, (shape(rows, buses), shape(hours, buses)), n_in=2 * le...  4.52 us
    pallas_call x4, Pallas kernels, pick(): call(lambda *refs: pick_kernel(at, *refs), (shape(size, slots), shape(siz...  3.9 us
  transfers between devices with their start and end apart: 22, of which 8 were waited for; matrix products, arithmetic and copies ran while one was open for 0% of the time, Pallas kernels for 9%

profile of v2, /device:TPU:8, one launch (start us, length us, event | category | flops | bytes accessed | tf_op | source)
XLA Modules:
  0.0 101.8 jit_solution(3909007436795782400)
XLA Ops:
  0.7 0.0 copy-start
  0.7 1.4 %copy-done = f32[1,16,24,1024]{3,2,1,0:T(8,128)S(1)} copy-done((f32[1,16,24,1024]{3,2,1,0:T(8,128)S(1)}, f32[1,16,24,1024]{3,2,1,0:T(8,128)}, u32[]{:S(2)}) %copy-start) | copy-done | bytes 1572888
  2.1 0.1 shard_map.98
  2.2 0.0 copy-start.1
  2.2 0.1 collective-permute-start.2
  2.4 1.2 %collective-permute-done.2 = f32[24,512]{1,0:T(8,128)S(1)} collective-permute-done((f32[24,512]{1,0:T(8,128)S(1)}, f32[24,512]{1,0:T(8,128)S(1)}, u32[]{:S(2)}, u32[]{:S(2)}) %collective-permute-start.2) | collective-permute-done | bytes 49184 | tf_op jit(solution)/shard_map/ppermute | solution.py:258
  3.6 2.4 %collective-permute-start.3 = (f32[24,512]{1,0:T(8,128)S(1)}, f32[24,512]{1,0:T(8,128)S(1)}, u32[]{:S(2)}, u32[]{:S(2)}) collective-permute-start(f32[24,512]{1,0:T(8,128)S(1)} %select_add_fusion.1), channel_id=1, source_target_pairs={{0,16},{1,17},{2,18},{3,19},{4,20},{5,21},{6,22},{7,23},{8,24},{9,... | collective-permute-start | bytes 147464 | tf_op jit(solution)/shard_map/ppermute | solution.py:262
  5.9 0.4 shard_map.95.refs_1_.select.refs_4_
  6.4 0.0 copy-start.8
  6.4 1.2 %shard_map.100 = (f32[240,512]{1,0:T(8,128)S(1)}, f32[240,512]{1,0:T(8,128)S(1)}) custom-call(f32[384,1024]{1,0:T(8,128)S(1)} %bitcast.12, bf16[1024,1024]{1,0:T(8,128)(2,1)S(1)} %shard_map.95.refs_1_.select.refs_4_), custom_call_target="tpu_custom_call" | custom-call | tf_op jit(solution)/shard_map/pallas_call | solution.py:295
  7.6 1.4 %collective-permute-start.9 = (f32[240,512]{1,0:T(8,128)S(1)}, f32[240,512]{1,0:T(8,128)S(1)}, u32[]{:S(2)}, u32[]{:S(2)}) collective-permute-start(f32[240,512]{1,0:T(8,128)S(1)} %get-tuple-element.25), channel_id=1, source_target_pairs={{0,32},{32,0},{64,96},{96,64},{128,160},{160,128},{192,224},{224,1... | collective-permute-start | bytes 1474568 | tf_op jit(solution)/shard_map/ppermute | solution.py:248
  9.0 1.6 %collective-permute-start.10 = (f32[240,512]{1,0:T(8,128)S(1)}, f32[240,512]{1,0:T(8,128)S(1)}, u32[]{:S(2)}, u32[]{:S(2)}) collective-permute-start(f32[240,512]{1,0:T(8,128)S(1)} %get-tuple-element.26), channel_id=1, source_target_pairs={{32,64},{64,32},{96,128},{128,96},{160,192},{192,160},{224,0},{0,2... | collective-permute-start | bytes 1474568 | tf_op jit(solution)/shard_map/ppermute | solution.py:249
  10.6 0.0 collective-permute-done.3
  10.6 2.0 %collective-permute-start.4 = (f32[24,512]{1,0:T(8,128)S(1)}, f32[24,512]{1,0:T(8,128)S(1)}, u32[]{:S(2)}, u32[]{:S(2)}) collective-permute-start(f32[24,512]{1,0:T(8,128)S(1)} %add.49), channel_id=1, source_target_pairs={{0,2},{1,3},{2,0},{3,1},{4,6},{5,7},{6,4},{7,5},{8,10},{9,11},{10,... | collective-permute-start | bytes 147464 | tf_op jit(solution)/shard_map/ppermute | solution.py:262
  12.6 0.1 compare_convert_fusion
  12.7 2.1 %collective-permute-done.4 = f32[24,512]{1,0:T(8,128)S(1)} collective-permute-done((f32[24,512]{1,0:T(8,128)S(1)}, f32[24,512]{1,0:T(8,128)S(1)}, u32[]{:S(2)}, u32[]{:S(2)}) %collective-permute-start.4) | collective-permute-done | bytes 49184 | tf_op jit(solution)/shard_map/ppermute | solution.py:262
  14.8 6.4 %collective-permute-start.7 = (f32[24,512]{1,0:T(8,128)S(1)}, f32[24,512]{1,0:T(8,128)S(1)}, u32[]{:S(2)}, u32[]{:S(2)}) collective-permute-start(f32[24,512]{1,0:T(8,128)S(1)} %add.50), channel_id=1, source_target_pairs={{0,12},{1,13},{2,14},{3,15},{4,8},{5,9},{6,10},{7,11},{8,4},{9,5},... | collective-permute-start | bytes 147464 | tf_op jit(solution)/shard_map/ppermute | solution.py:262
  21.2 1.0 collective-permute-start.6
  22.2 1.5 %collective-permute-start.5 = (f32[24,512]{1,0:T(8,128)S(1)}, f32[24,512]{1,0:T(8,128)S(1)}, u32[]{:S(2)}, u32[]{:S(2)}) collective-permute-start(f32[24,512]{1,0:T(8,128)S(1)} %add.50), channel_id=1, source_target_pairs={{0,4},{1,5},{2,6},{3,7},{4,0},{5,1},{6,2},{7,3},{8,12},{9,13},{10,... | collective-permute-start | bytes 147464 | tf_op jit(solution)/shard_map/ppermute | solution.py:262
  23.7 0.0 copy-start.3
  23.7 0.0 copy-start.4
  23.7 0.8 shard_map.96
  24.5 0.0 copy-start.2
  24.5 0.0 collective-permute-done.7
  24.5 2.7 %collective-permute-start = (f32[144,512]{1,0:T(8,128)S(1)}, f32[144,512]{1,0:T(8,128)S(1)}, u32[]{:S(2)}, u32[]{:S(2)}) collective-permute-start(f32[144,512]{1,0:T(8,128)S(1)} %get-tuple-element.20), channel_id=1, source_target_pairs={{0,32},{32,0},{64,96},{96,64},{128,160},{160,128},{192,224},{224,1... | collective-permute-start | bytes 884744 | tf_op jit(solution)/shard_map/ppermute | solution.py:248
  27.2 2.1 %collective-permute-done.6 = f32[24,512]{1,0:T(8,128)S(1)} collective-permute-done((f32[24,512]{1,0:T(8,128)S(1)}, f32[24,512]{1,0:T(8,128)S(1)}, u32[]{:S(2)}, u32[]{:S(2)}) %collective-permute-start.6) | collective-permute-done | bytes 49184 | tf_op jit(solution)/shard_map/ppermute | solution.py:262
  29.3 1.3 %collective-permute-start.1 = (f32[144,512]{1,0:T(8,128)S(1)}, f32[144,512]{1,0:T(8,128)S(1)}, u32[]{:S(2)}, u32[]{:S(2)}) collective-permute-start(f32[144,512]{1,0:T(8,128)S(1)} %get-tuple-element.21), channel_id=1, source_target_pairs={{32,64},{64,32},{96,128},{128,96},{160,192},{192,160},{224,0},{0,2... | collective-permute-start | bytes 884744 | tf_op jit(solution)/shard_map/ppermute | solution.py:249
  30.6 0.0 collective-permute-done.5
  30.6 0.3 collective-permute-start.8
  31.0 1.9 %shard_map.97 = (f32[8,1024]{1,0:T(8,128)S(1)}, f32[8,1024]{1,0:T(8,128)S(1)}) custom-call(bf16[1024,1024]{1,0:T(8,128)(2,1)S(1)} %shard_map.95.refs_1_.select.refs_4_, f32[1,1024]{1,0:T(1,128)S(1)} %broadcast_select_fusion.live, s32[1,512]{1,0:T(1,128)S(1)} %copy-done.5, f32[1,512]{1,0:T(1,128)S(1)} %copy-done.6), custom_call_target="tpu_custom_call" | custom-call | tf_op jit(solution)/shard_map/pallas_call | solution.py:310
  32.9 0.0 collective-permute-done.8
  32.9 10.9 %collective-permute-done.refs_5_ = f32[144,512]{1,0:T(8,128)S(1)} collective-permute-done((f32[144,512]{1,0:T(8,128)S(1)}, f32[144,512]{1,0:T(8,128)S(1)}, u32[]{:S(2)}, u32[]{:S(2)}) %collective-permute-start) | collective-permute-done | bytes 294944 | tf_op jit(solution)/shard_map/ppermute | solution.py:248
  43.8 0.0 collective-permute-done.1.refs_6_
  43.9 2.2 %shard_map.99 = (f32[144,1024]{1,0:T(8,128)S(1)}, f32[144,1024]{1,0:T(8,128)S(1)}, f32[24,1024]{1,0:T(8,128)S(1)}) custom-call(f32[384,1024]{1,0:T(8,128)S(1)} %bitcast.14, f32[384,1024]{1,0:T(8,128)S(1)} %bitcast.18, f32[384,1024]{1,0:T(8,128)S(1)} %bitcast.25, bf16[1024,1024]{1,0:T(8,128)(2,1)S(1)} %bitcast.22, ...), custom_call_target="tpu_custom_call" | custom-call | tf_op jit(solution)/shard_map/pallas_call | solution.py:317
  46.1 0.0 collective-permute-done.9.refs_5_
  46.1 0.0 collective-permute-done.10.refs_6_
  46.1 3.3 %shard_map.101 = (f32[240,1024]{1,0:T(8,128)S(1)}, f32[240,1024]{1,0:T(8,128)S(1)}, f32[24,1024]{1,0:T(8,128)S(1)}) custom-call(f32[384,1024]{1,0:T(8,128)S(1)} %bitcast.15, f32[384,1024]{1,0:T(8,128)S(1)} %bitcast.19, f32[384,1024]{1,0:T(8,128)S(1)} %bitcast.26, bf16[1024,1024]{1,0:T(8,128)(2,1)S(1)} %bitcast.23, ...), custom_call_target="tpu_custom_call" | custom-call | tf_op jit(solution)/shard_map/pallas_call | solution.py:317
  49.5 0.1 collective-permute-start.15
  49.6 1.2 %collective-permute-done.15 = f32[24,512]{1,0:T(8,128)S(1)} collective-permute-done((f32[24,512]{1,0:T(8,128)S(1)}, f32[24,512]{1,0:T(8,128)S(1)}, u32[]{:S(2)}, u32[]{:S(2)}) %collective-permute-start.15) | collective-permute-done | bytes 49184 | tf_op jit(solution)/shard_map/ppermute | solution.py:258
  50.8 1.3 %collective-permute-start.16 = (f32[24,512]{1,0:T(8,128)S(1)}, f32[24,512]{1,0:T(8,128)S(1)}, u32[]{:S(2)}, u32[]{:S(2)}) collective-permute-start(f32[24,512]{1,0:T(8,128)S(1)} %select_add_fusion), channel_id=1, source_target_pairs={{0,16},{1,17},{2,18},{3,19},{4,20},{5,21},{6,22},{7,23},{8,24},{9,... | collective-permute-start | bytes 147464 | tf_op jit(solution)/shard_map/ppermute | solution.py:262
  52.1 4.3 %collective-permute-done.16 = f32[24,512]{1,0:T(8,128)S(1)} collective-permute-done((f32[24,512]{1,0:T(8,128)S(1)}, f32[24,512]{1,0:T(8,128)S(1)}, u32[]{:S(2)}, u32[]{:S(2)}) %collective-permute-start.16) | collective-permute-done | bytes 49184 | tf_op jit(solution)/shard_map/ppermute | solution.py:262
  56.5 2.0 %collective-permute-start.17 = (f32[24,512]{1,0:T(8,128)S(1)}, f32[24,512]{1,0:T(8,128)S(1)}, u32[]{:S(2)}, u32[]{:S(2)}) collective-permute-start(f32[24,512]{1,0:T(8,128)S(1)} %add.56), channel_id=1, source_target_pairs={{0,2},{1,3},{2,0},{3,1},{4,6},{5,7},{6,4},{7,5},{8,10},{9,11},{10,... | collective-permute-start | bytes 147464 | tf_op jit(solution)/shard_map/ppermute | solution.py:262
  58.5 1.2 %shard_map.104 = (f32[240,512]{1,0:T(8,128)S(1)}, f32[240,512]{1,0:T(8,128)S(1)}) custom-call(f32[240,1024]{1,0:T(8,128)S(1)} %get-tuple-element.27.refs_0_.refs_1_, bf16[1024,1024]{1,0:T(8,128)(2,1)S(1)} %shard_map.95.refs_1_.select.refs_4_), custom_call_target="tpu_custom_call" | custom-call | tf_op jit(solution)/shard_map/pallas_call | solution.py:295
  59.7 1.4 %collective-permute-start.13 = (f32[240,512]{1,0:T(8,128)S(1)}, f32[240,512]{1,0:T(8,128)S(1)}, u32[]{:S(2)}, u32[]{:S(2)}) collective-permute-start(f32[240,512]{1,0:T(8,128)S(1)} %get-tuple-element.32), channel_id=1, source_target_pairs={{0,32},{32,0},{64,96},{96,64},{128,160},{160,128},{192,224},{224,1... | collective-permute-start | bytes 1474568 | tf_op jit(solution)/shard_map/ppermute | solution.py:248
  61.1 1.6 %collective-permute-start.14 = (f32[240,512]{1,0:T(8,128)S(1)}, f32[240,512]{1,0:T(8,128)S(1)}, u32[]{:S(2)}, u32[]{:S(2)}) collective-permute-start(f32[240,512]{1,0:T(8,128)S(1)} %get-tuple-element.33), channel_id=1, source_target_pairs={{32,64},{64,32},{96,128},{128,96},{160,192},{192,160},{224,0},{0,2... | collective-permute-start | bytes 1474568 | tf_op jit(solution)/shard_map/ppermute | solution.py:249
  62.7 0.0 collective-permute-done.17
  62.7 5.5 %collective-permute-start.20 = (f32[24,512]{1,0:T(8,128)S(1)}, f32[24,512]{1,0:T(8,128)S(1)}, u32[]{:S(2)}, u32[]{:S(2)}) collective-permute-start(f32[24,512]{1,0:T(8,128)S(1)} %add.57), channel_id=1, source_target_pairs={{0,12},{1,13},{2,14},{3,15},{4,8},{5,9},{6,10},{7,11},{8,4},{9,5},... | collective-permute-start | bytes 147464 | tf_op jit(solution)/shard_map/ppermute | solution.py:262
  68.2 1.4 %collective-permute-start.19 = (f32[24,512]{1,0:T(8,128)S(1)}, f32[24,512]{1,0:T(8,128)S(1)}, u32[]{:S(2)}, u32[]{:S(2)}) collective-permute-start(f32[24,512]{1,0:T(8,128)S(1)} %add.57), channel_id=1, source_target_pairs={{0,8},{1,9},{2,10},{3,11},{4,12},{5,13},{6,14},{7,15},{8,0},{9,1},... | collective-permute-start | bytes 147464 | tf_op jit(solution)/shard_map/ppermute | solution.py:262
  69.7 1.0 %collective-permute-start.18 = (f32[24,512]{1,0:T(8,128)S(1)}, f32[24,512]{1,0:T(8,128)S(1)}, u32[]{:S(2)}, u32[]{:S(2)}) collective-permute-start(f32[24,512]{1,0:T(8,128)S(1)} %add.57), channel_id=1, source_target_pairs={{0,4},{1,5},{2,6},{3,7},{4,0},{5,1},{6,2},{7,3},{8,12},{9,13},{10,... | collective-permute-start | bytes 147464 | tf_op jit(solution)/shard_map/ppermute | solution.py:262
  70.7 0.8 shard_map.102
  71.5 0.0 collective-permute-done.20
  71.5 2.7 %collective-permute-start.11 = (f32[144,512]{1,0:T(8,128)S(1)}, f32[144,512]{1,0:T(8,128)S(1)}, u32[]{:S(2)}, u32[]{:S(2)}) collective-permute-start(f32[144,512]{1,0:T(8,128)S(1)} %get-tuple-element.29), channel_id=1, source_target_pairs={{0,32},{32,0},{64,96},{96,64},{128,160},{160,128},{192,224},{224,1... | collective-permute-start | bytes 884744 | tf_op jit(solution)/shard_map/ppermute | solution.py:248
  74.2 2.1 %collective-permute-done.19 = f32[24,512]{1,0:T(8,128)S(1)} collective-permute-done((f32[24,512]{1,0:T(8,128)S(1)}, f32[24,512]{1,0:T(8,128)S(1)}, u32[]{:S(2)}, u32[]{:S(2)}) %collective-permute-start.19) | collective-permute-done | bytes 49184 | tf_op jit(solution)/shard_map/ppermute | solution.py:262
  76.3 1.3 %collective-permute-start.12 = (f32[144,512]{1,0:T(8,128)S(1)}, f32[144,512]{1,0:T(8,128)S(1)}, u32[]{:S(2)}, u32[]{:S(2)}) collective-permute-start(f32[144,512]{1,0:T(8,128)S(1)} %get-tuple-element.30), channel_id=1, source_target_pairs={{32,64},{64,32},{96,128},{128,96},{160,192},{192,160},{224,0},{0,2... | collective-permute-start | bytes 884744 | tf_op jit(solution)/shard_map/ppermute | solution.py:249
  77.6 0.0 collective-permute-done.18
  77.6 0.1 collective-permute-start.21
  77.7 17.1 %collective-permute-done.11.refs_5_ = f32[144,512]{1,0:T(8,128)S(1)} collective-permute-done((f32[144,512]{1,0:T(8,128)S(1)}, f32[144,512]{1,0:T(8,128)S(1)}, u32[]{:S(2)}, u32[]{:S(2)}) %collective-permute-start.11) | collective-permute-done | bytes 294944 | tf_op jit(solution)/shard_map/ppermute | solution.py:248
  94.8 0.0 collective-permute-done.12.refs_6_
  94.8 0.9 shard_map.103.refs_2_
  95.8 0.0 collective-permute-done.21
  95.8 0.0 collective-permute-done.13.refs_5_
  95.8 0.0 collective-permute-done.14.refs_6_
  95.8 1.5 %shard_map.105.refs_3_ = f32[240,1024]{1,0:T(8,128)S(1)} custom-call(f32[384,1024]{1,0:T(8,128)S(1)} %bitcast.17, f32[240,1024]{1,0:T(8,128)S(1)} %get-tuple-element.27.refs_0_.refs_1_, f32[240,1024]{1,0:T(8,128)S(1)} %get-tuple-element.31.refs_2_, f32[384,1024]{1,0:T(8,128)S(1)} %bitcast.21, bf16[1024,1024]{1,0:T(8,128)(2,1)S(1)} %shard_map.95.refs_1_.select.refs_4_, ...), custom_call_target="tpu_custom_call" | custom-call | tf_op jit(solution)/shard_map/pallas_call | solution.py:335
  97.3 4.5 %shard_map.106 = (f32[384,1024]{1,0:T(8,128)}, f32[24,1024]{1,0:T(8,128)}) custom-call(f32[144,1024]{1,0:T(8,128)S(1)} %get-tuple-element.24.refs_0_.refs_1_, f32[240,1024]{1,0:T(8,128)S(1)} %get-tuple-element.27.refs_0_.refs_1_, f32[144,1024]{1,0:T(8,128)S(1)} %shard_map.103.refs_2_, f32[240,1024]{1,0:T(8,128)S(1)} %shard_map.105.refs_3_, ...), custom_call_target="tpu_custom_call" | custom-call | tf_op jit(solution)/shard_map/pallas_call | solution.py:343
  (28 shorter events, 0.2 us)
Async XLA Ops:
  0.6 1.7 %copy-start.7 = (s32[1,2,512]{2,1,0:T(2,128)S(1)}, s32[1,2,512]{2,1,0:T(2,128)}, u32[]{:S(2)}) copy-start(s32[1,2,512]{2,1,0:T(2,128)} %param.14) | copy-start | bytes 12292
  0.7 1.4 %copy-start = (f32[1,16,24,1024]{3,2,1,0:T(8,128)S(1)}, f32[1,16,24,1024]{3,2,1,0:T(8,128)}, u32[]{:S(2)}) copy-start(f32[1,16,24,1024]{3,2,1,0:T(8,128)} %param.8) | copy-start | bytes 4718596
  2.2 4.2 %copy-start.1 = (f32[1,16,24,1024]{3,2,1,0:T(8,128)S(1)}, f32[1,16,24,1024]{3,2,1,0:T(8,128)}, u32[]{:S(2)}) copy-start(f32[1,16,24,1024]{3,2,1,0:T(8,128)} %param.8) | copy-start | bytes 4718596
  2.2 1.3 %collective-permute-start.2 = (f32[24,512]{1,0:T(8,128)S(1)}, f32[24,512]{1,0:T(8,128)S(1)}, u32[]{:S(2)}, u32[]{:S(2)}) collective-permute-start(f32[24,512]{1,0:T(8,128)S(1)} %slice_select_fusion.1), channel_id=1, source_target_pairs={{0,1},{1,0},{2,3},{3,2},{4,5},{5,4},{6,7},{7,6},{8,9},{9,8},{10,11... | collective-permute-start | bytes 147464 | tf_op jit(solution)/shard_map/ppermute | solution.py:258
  3.6 7.1 %collective-permute-start.3 = (f32[24,512]{1,0:T(8,128)S(1)}, f32[24,512]{1,0:T(8,128)S(1)}, u32[]{:S(2)}, u32[]{:S(2)}) collective-permute-start(f32[24,512]{1,0:T(8,128)S(1)} %select_add_fusion.1), channel_id=1, source_target_pairs={{0,16},{1,17},{2,18},{3,19},{4,20},{5,21},{6,22},{7,23},{8,24},{9,... | collective-permute-start | bytes 147464 | tf_op jit(solution)/shard_map/ppermute | solution.py:262
  6.4 6.3 %copy-start.8 = (s32[1,2]{1,0:T(1,128)S(1)}, s32[1,2]{1,0:T(1,128)}, u32[]{:S(2)}) copy-start(s32[1,2]{1,0:T(1,128)} %param.15) | copy-start | bytes 28
  7.6 38.5 %collective-permute-start.9 = (f32[240,512]{1,0:T(8,128)S(1)}, f32[240,512]{1,0:T(8,128)S(1)}, u32[]{:S(2)}, u32[]{:S(2)}) collective-permute-start(f32[240,512]{1,0:T(8,128)S(1)} %get-tuple-element.25), channel_id=1, source_target_pairs={{0,32},{32,0},{64,96},{96,64},{128,160},{160,128},{192,224},{224,1... | collective-permute-start | bytes 1474568 | tf_op jit(solution)/shard_map/ppermute | solution.py:248
  9.0 37.1 %collective-permute-start.10 = (f32[240,512]{1,0:T(8,128)S(1)}, f32[240,512]{1,0:T(8,128)S(1)}, u32[]{:S(2)}, u32[]{:S(2)}) collective-permute-start(f32[240,512]{1,0:T(8,128)S(1)} %get-tuple-element.26), channel_id=1, source_target_pairs={{32,64},{64,32},{96,128},{128,96},{160,192},{192,160},{224,0},{0,2... | collective-permute-start | bytes 1474568 | tf_op jit(solution)/shard_map/ppermute | solution.py:249
  10.6 4.2 %collective-permute-start.4 = (f32[24,512]{1,0:T(8,128)S(1)}, f32[24,512]{1,0:T(8,128)S(1)}, u32[]{:S(2)}, u32[]{:S(2)}) collective-permute-start(f32[24,512]{1,0:T(8,128)S(1)} %add.49), channel_id=1, source_target_pairs={{0,2},{1,3},{2,0},{3,1},{4,6},{5,7},{6,4},{7,5},{8,10},{9,11},{10,... | collective-permute-start | bytes 147464 | tf_op jit(solution)/shard_map/ppermute | solution.py:262
  14.8 9.7 %collective-permute-start.7 = (f32[24,512]{1,0:T(8,128)S(1)}, f32[24,512]{1,0:T(8,128)S(1)}, u32[]{:S(2)}, u32[]{:S(2)}) collective-permute-start(f32[24,512]{1,0:T(8,128)S(1)} %add.50), channel_id=1, source_target_pairs={{0,12},{1,13},{2,14},{3,15},{4,8},{5,9},{6,10},{7,11},{8,4},{9,5},... | collective-permute-start | bytes 147464 | tf_op jit(solution)/shard_map/ppermute | solution.py:262
  21.2 8.1 %collective-permute-start.6 = (f32[24,512]{1,0:T(8,128)S(1)}, f32[24,512]{1,0:T(8,128)S(1)}, u32[]{:S(2)}, u32[]{:S(2)}) collective-permute-start(f32[24,512]{1,0:T(8,128)S(1)} %add.50), channel_id=1, source_target_pairs={{0,8},{1,9},{2,10},{3,11},{4,12},{5,13},{6,14},{7,15},{8,0},{9,1},... | collective-permute-start | bytes 147464 | tf_op jit(solution)/shard_map/ppermute | solution.py:262
  22.2 8.4 %collective-permute-start.5 = (f32[24,512]{1,0:T(8,128)S(1)}, f32[24,512]{1,0:T(8,128)S(1)}, u32[]{:S(2)}, u32[]{:S(2)}) collective-permute-start(f32[24,512]{1,0:T(8,128)S(1)} %add.50), channel_id=1, source_target_pairs={{0,4},{1,5},{2,6},{3,7},{4,0},{5,1},{6,2},{7,3},{8,12},{9,13},{10,... | collective-permute-start | bytes 147464 | tf_op jit(solution)/shard_map/ppermute | solution.py:262
  23.7 7.3 %copy-start.5 = (s32[1,512]{1,0:T(1,128)S(1)}, s32[1,512]{1,0:T(1,128)}, u32[]{:S(2)}) copy-start(s32[1,512]{1,0:T(1,128)} %gen_bus.1) | copy-start | bytes 6148
  23.7 7.3 %copy-start.6 = (f32[1,512]{1,0:T(1,128)S(1)}, f32[1,512]{1,0:T(1,128)}, u32[]{:S(2)}) copy-start(f32[1,512]{1,0:T(1,128)} %gen_cap.1) | copy-start | bytes 6148
  23.7 20.2 %copy-start.3 = (bf16[1,1024,1024]{2,1,0:T(8,128)(2,1)S(1)}, bf16[1,1024,1024]{2,1,0:T(8,128)(2,1)}, u32[]{:S(2)}) copy-start(bf16[1,1024,1024]{2,1,0:T(8,128)(2,1)} %param.11) | copy-start | bytes 6291460
  23.7 20.2 %copy-start.4 = (f32[1,16,24,1024]{3,2,1,0:T(8,128)S(1)}, f32[1,16,24,1024]{3,2,1,0:T(8,128)}, u32[]{:S(2)}) copy-start(f32[1,16,24,1024]{3,2,1,0:T(8,128)} %param.10) | copy-start | bytes 4718596
  24.5 19.4 %copy-start.2 = (f32[1,16,24,1024]{3,2,1,0:T(8,128)S(1)}, f32[1,16,24,1024]{3,2,1,0:T(8,128)}, u32[]{:S(2)}) copy-start(f32[1,16,24,1024]{3,2,1,0:T(8,128)} %param.9) | copy-start | bytes 4718596
  24.5 19.3 %collective-permute-start = (f32[144,512]{1,0:T(8,128)S(1)}, f32[144,512]{1,0:T(8,128)S(1)}, u32[]{:S(2)}, u32[]{:S(2)}) collective-permute-start(f32[144,512]{1,0:T(8,128)S(1)} %get-tuple-element.20), channel_id=1, source_target_pairs={{0,32},{32,0},{64,96},{96,64},{128,160},{160,128},{192,224},{224,1... | collective-permute-start | bytes 884744 | tf_op jit(solution)/shard_map/ppermute | solution.py:248
  29.3 14.5 %collective-permute-start.1 = (f32[144,512]{1,0:T(8,128)S(1)}, f32[144,512]{1,0:T(8,128)S(1)}, u32[]{:S(2)}, u32[]{:S(2)}) collective-permute-start(f32[144,512]{1,0:T(8,128)S(1)} %get-tuple-element.21), channel_id=1, source_target_pairs={{32,64},{64,32},{96,128},{128,96},{160,192},{192,160},{224,0},{0,2... | collective-permute-start | bytes 884744 | tf_op jit(solution)/shard_map/ppermute | solution.py:249
  30.6 2.2 %collective-permute-start.8 = (f32[24,512]{1,0:T(8,128)S(1)}, f32[24,512]{1,0:T(8,128)S(1)}, u32[]{:S(2)}, u32[]{:S(2)}) collective-permute-start(f32[24,512]{1,0:T(8,128)S(1)} %add_add_fusion.1), channel_id=1, source_target_pairs={{0,1},{1,0},{2,3},{3,2},{4,5},{5,4},{6,7},{7,6},{8,9},{9,8},{10,11... | collective-permute-start | bytes 147464 | tf_op jit(solution)/shard_map/ppermute | solution.py:266
  49.5 1.3 %collective-permute-start.15 = (f32[24,512]{1,0:T(8,128)S(1)}, f32[24,512]{1,0:T(8,128)S(1)}, u32[]{:S(2)}, u32[]{:S(2)}) collective-permute-start(f32[24,512]{1,0:T(8,128)S(1)} %slice_select_fusion), channel_id=1, source_target_pairs={{0,1},{1,0},{2,3},{3,2},{4,5},{5,4},{6,7},{7,6},{8,9},{9,8},{10,11... | collective-permute-start | bytes 147464 | tf_op jit(solution)/shard_map/ppermute | solution.py:258
  50.8 5.7 %collective-permute-start.16 = (f32[24,512]{1,0:T(8,128)S(1)}, f32[24,512]{1,0:T(8,128)S(1)}, u32[]{:S(2)}, u32[]{:S(2)}) collective-permute-start(f32[24,512]{1,0:T(8,128)S(1)} %select_add_fusion), channel_id=1, source_target_pairs={{0,16},{1,17},{2,18},{3,19},{4,20},{5,21},{6,22},{7,23},{8,24},{9,... | collective-permute-start | bytes 147464 | tf_op jit(solution)/shard_map/ppermute | solution.py:262
  56.5 6.2 %collective-permute-start.17 = (f32[24,512]{1,0:T(8,128)S(1)}, f32[24,512]{1,0:T(8,128)S(1)}, u32[]{:S(2)}, u32[]{:S(2)}) collective-permute-start(f32[24,512]{1,0:T(8,128)S(1)} %add.56), channel_id=1, source_target_pairs={{0,2},{1,3},{2,0},{3,1},{4,6},{5,7},{6,4},{7,5},{8,10},{9,11},{10,... | collective-permute-start | bytes 147464 | tf_op jit(solution)/shard_map/ppermute | solution.py:262
  59.7 36.1 %collective-permute-start.13 = (f32[240,512]{1,0:T(8,128)S(1)}, f32[240,512]{1,0:T(8,128)S(1)}, u32[]{:S(2)}, u32[]{:S(2)}) collective-permute-start(f32[240,512]{1,0:T(8,128)S(1)} %get-tuple-element.32), channel_id=1, source_target_pairs={{0,32},{32,0},{64,96},{96,64},{128,160},{160,128},{192,224},{224,1... | collective-permute-start | bytes 1474568 | tf_op jit(solution)/shard_map/ppermute | solution.py:248
  61.1 34.7 %collective-permute-start.14 = (f32[240,512]{1,0:T(8,128)S(1)}, f32[240,512]{1,0:T(8,128)S(1)}, u32[]{:S(2)}, u32[]{:S(2)}) collective-permute-start(f32[240,512]{1,0:T(8,128)S(1)} %get-tuple-element.33), channel_id=1, source_target_pairs={{32,64},{64,32},{96,128},{128,96},{160,192},{192,160},{224,0},{0,2... | collective-permute-start | bytes 1474568 | tf_op jit(solution)/shard_map/ppermute | solution.py:249
  62.7 8.7 %collective-permute-start.20 = (f32[24,512]{1,0:T(8,128)S(1)}, f32[24,512]{1,0:T(8,128)S(1)}, u32[]{:S(2)}, u32[]{:S(2)}) collective-permute-start(f32[24,512]{1,0:T(8,128)S(1)} %add.57), channel_id=1, source_target_pairs={{0,12},{1,13},{2,14},{3,15},{4,8},{5,9},{6,10},{7,11},{8,4},{9,5},... | collective-permute-start | bytes 147464 | tf_op jit(solution)/shard_map/ppermute | solution.py:262
  68.2 8.1 %collective-permute-start.19 = (f32[24,512]{1,0:T(8,128)S(1)}, f32[24,512]{1,0:T(8,128)S(1)}, u32[]{:S(2)}, u32[]{:S(2)}) collective-permute-start(f32[24,512]{1,0:T(8,128)S(1)} %add.57), channel_id=1, source_target_pairs={{0,8},{1,9},{2,10},{3,11},{4,12},{5,13},{6,14},{7,15},{8,0},{9,1},... | collective-permute-start | bytes 147464 | tf_op jit(solution)/shard_map/ppermute | solution.py:262
  69.7 7.9 %collective-permute-start.18 = (f32[24,512]{1,0:T(8,128)S(1)}, f32[24,512]{1,0:T(8,128)S(1)}, u32[]{:S(2)}, u32[]{:S(2)}) collective-permute-start(f32[24,512]{1,0:T(8,128)S(1)} %add.57), channel_id=1, source_target_pairs={{0,4},{1,5},{2,6},{3,7},{4,0},{5,1},{6,2},{7,3},{8,12},{9,13},{10,... | collective-permute-start | bytes 147464 | tf_op jit(solution)/shard_map/ppermute | solution.py:262
  71.5 23.3 %collective-permute-start.11 = (f32[144,512]{1,0:T(8,128)S(1)}, f32[144,512]{1,0:T(8,128)S(1)}, u32[]{:S(2)}, u32[]{:S(2)}) collective-permute-start(f32[144,512]{1,0:T(8,128)S(1)} %get-tuple-element.29), channel_id=1, source_target_pairs={{0,32},{32,0},{64,96},{96,64},{128,160},{160,128},{192,224},{224,1... | collective-permute-start | bytes 884744 | tf_op jit(solution)/shard_map/ppermute | solution.py:248
  76.3 18.5 %collective-permute-start.12 = (f32[144,512]{1,0:T(8,128)S(1)}, f32[144,512]{1,0:T(8,128)S(1)}, u32[]{:S(2)}, u32[]{:S(2)}) collective-permute-start(f32[144,512]{1,0:T(8,128)S(1)} %get-tuple-element.30), channel_id=1, source_target_pairs={{32,64},{64,32},{96,128},{128,96},{160,192},{192,160},{224,0},{0,2... | collective-permute-start | bytes 884744 | tf_op jit(solution)/shard_map/ppermute | solution.py:249
  77.6 18.1 %collective-permute-start.21 = (f32[24,512]{1,0:T(8,128)S(1)}, f32[24,512]{1,0:T(8,128)S(1)}, u32[]{:S(2)}, u32[]{:S(2)}) collective-permute-start(f32[24,512]{1,0:T(8,128)S(1)} %add_add_fusion), channel_id=1, source_target_pairs={{0,1},{1,0},{2,3},{3,2},{4,5},{5,4},{6,7},{7,6},{8,9},{9,8},{10,11... | collective-permute-start | bytes 147464 | tf_op jit(solution)/shard_map/ppermute | solution.py:266

commit v3 on v2

--- a/solution.py
+++ b/solution.py
@@ -6,7 +6,8 @@
 from jax.sharding import PartitionSpec as P
 
 
-CHUNKS = (6, 10)
+CHUNKS = (10, 6)
+PARTS = ((4, 2, 4), (6,))
 BLOCK = 256
 step_rate = 0.3
 tie_weight = 1.0
@@ -30,15 +31,17 @@
     return high, (x - high.astype(F32)).astype(BF16)
 
 
-def call(kernel, outs, *, n_in, scratch=()):
+def call(kernel, outs, *, n_in, scratch=(), out_space=pltpu.VMEM, flops=4 << 30):
     vmem = pl.BlockSpec(memory_space=pltpu.VMEM)
+    out_spec = pl.BlockSpec(memory_space=out_space)
     return pl.pallas_call(
         kernel,
         out_shape=outs,
         in_specs=[vmem] * n_in,
-        out_specs=jax.tree.map(lambda _: vmem, outs),
+        out_specs=jax.tree.map(lambda _: out_spec, outs),
         scratch_shapes=list(scratch),
-        compiler_params=pltpu.CompilerParams(vmem_limit_bytes=24 << 20),
+        compiler_params=pltpu.CompilerParams(vmem_limit_bytes=16 << 20),
+        cost_estimate=pl.CostEstimate(flops=flops, transcendentals=0, bytes_accessed=1 << 20),
     )
 
 
@@ -119,10 +122,15 @@
     lax.fori_loop(0, upper.shape[1] // rows, one, 0)
 
 
-def theirs_into(pair, left, right):
-    slots = left.shape[1]
-    split_into(pair, left[...], pl.ds(0, slots))
-    split_into(pair, right[...], pl.ds(slots, slots))
+def theirs_into(pair, *ties):
+    rows, at = pair.shape[0] // 2, 0
+    for left, right in zip(ties[::2], ties[1::2]):
+        size, slots = left.shape
+        for start, side in ((0, left), (slots, right)):
+            high, low = high_low(side[...])
+            pair[at : at + size, start : start + slots] = high
+            pair[rows + at : rows + at + size, start : start + slots] = low
+        at += size
 
 
 def theirs_at(pair, select, at):
@@ -136,16 +144,14 @@
     return jnp.minimum(jnp.maximum(now - step_rate * slope, lower), upper)
 
 
-def first_kernel(start, state0, price, demand, matrix, select, left, right, mask, upper, plan, out, dual_out, total, even, other, base, pair):
+def first_kernel(start, *refs):
+    state0, slope0, price, demand, matrix, select, left, right, mask, upper, plan = refs[:11]
+    refs = refs[11:]
+    out, dual_out, total, even, other, base, pair = refs
     rows, buses = out.shape
     hours = plan.shape[0]
     part = slice(start, start + rows)
     theirs_into(pair, left, right)
-
-    def load(at):
-        even[:, at] = state0[part, at].astype(BF16)
-
-    over_blocks(buses, load)
 
     def zero(at):
         now = state0[part, at]
@@ -158,7 +164,7 @@
         day_dual = now - day_plan
         constant = price[part, at] - tie_weight * mask[:1, at] * target + day_weight * (day_dual - day_plan)
         base[:, at] = constant
-        new = stepped(now, dot(even[...], matrix[:, at]), constant, mask[:1, at], -demand[part, at], upper[:1, at])
+        new = stepped(now, slope0[part, at], constant, mask[:1, at], -demand[part, at], upper[:1, at])
         out[:, at] = new
         other[:, at] = new.astype(BF16)
 
@@ -178,15 +184,16 @@
     over_blocks(buses, two)
 
 
-def prepare_kernel(start, state0, state1, dual1, price, select, left, right, mask, plan1, base, pair):
+def prepare_kernel(start, inside, state0, state1, dual1, price, select, left, right, mask, plan1, base, pair):
     rows, buses = base.shape
     part = slice(start, start + rows)
+    inner = slice(inside, inside + rows)
     theirs_into(pair, left, right)
 
     def zero(at):
-        now = state1[:, at]
+        now = state1[inner, at]
         middle = 0.5 * (now + theirs_at(pair, select, at))
-        dual = dual1[:, at] + now - middle
+        dual = dual1[inner, at] + now - middle
         target = mask[:1, at] * (middle - dual)
         day_dual = state0[part, at] - for_scenarios(plan1[:, at], rows)
         base[:, at] = price[part, at] - tie_weight * mask[:1, at] * target + day_weight * (day_dual + now)
@@ -194,43 +201,75 @@
     over_blocks(buses, zero)
 
 
-def final_kernel(*refs):
-    count = len(CHUNKS)
-    states, bases = refs[:count], refs[count : 2 * count]
-    demand, matrix, mask, upper, plan, out, plan_out, even, other, base = refs[2 * count :]
-    buses = out.shape[1]
-    ends = [sum(r.shape[0] for r in states[:c]) for c in range(count + 1)]
-    plan_out[...] = plan[...]
-
-    def load(at):
-        for c in range(count):
-            even[ends[c] : ends[c + 1], at] = states[c][:, at].astype(BF16)
-
-    over_blocks(buses, load)
-
-    def step(source, target, first, last):
-        def one(at):
-            slope = dot(source[...], matrix[:, at])
-            for c in range(count):
-                part = slice(ends[c], ends[c + 1])
-                if first:
-                    day_plan = for_scenarios(plan[:, at], ends[c + 1] - ends[c])
-                    constant = bases[c][:, at] - 2 * day_weight * day_plan
-                    base[part, at] = constant
-                    now = states[c][:, at]
-                else:
-                    constant = base[part, at]
-                    now = out[part, at]
-                new = stepped(now, slope[part], constant, mask[:1, at], -demand[part, at], upper[:1, at])
-                out[part, at] = new
-                if not last:
-                    target[part, at] = new.astype(BF16)
-
-        over_blocks(buses, one)
-
-    step(even, other, True, False)
-    step(other, even, False, False)
-    step(even, other, False, True)
+def early_kernel(state, matrix, slope, rounded):
+    over_blocks(state.shape[1], lambda at: rounded.__setitem__((slice(None), at), state[:, at].astype(BF16)))
+
+    def one(at):
+        slope[:, at] = dot(rounded[...], matrix[:, at])
+
+    over_blocks(state.shape[1], one)
+
+
+def last_steps(start, insides, refs, written=None):
+    pieces = [refs[3 * k : 3 * k + 3] for k in range(len(insides))]
+    demand, matrix, mask, upper, plan, out, even, other, constants = refs[3 * len(insides) :]
+    rows, buses = out.shape
+    part = slice(start, start + rows)
+
+    def zero(at):
+        top = 0
+        for inside, (state, slope, base) in zip(insides, pieces):
+            size = base.shape[0]
+            inner, here = slice(inside, inside + size), slice(top, top + size)
+            lower = -demand[start + top : start + top + size, at]
+            constant = base[:, at] - 2 * day_weight * for_scenarios(plan[:, at], size)
+            constants[here, at] = constant
+            new = stepped(state[inner, at], slope[inner, at], constant, mask[:1, at], lower, upper[:1, at])
+            out[here, at] = new
+            even[here, at] = new.astype(BF16)
+            top += size
+
+    def one(at):
+        new = stepped(out[:, at], dot(even[...], matrix[:, at]), constants[:, at], mask[:1, at], -demand[part, at], upper[:1, at])
+        out[:, at] = new
+        other[:, at] = new.astype(BF16)
+
+    def two(at):
+        new = stepped(out[:, at], dot(other[...], matrix[:, at]), constants[:, at], mask[:1, at], -demand[part, at], upper[:1, at])
+        out[:, at] = new
+        if written is not None:
+            written(at)
+
+    over_blocks(buses, zero)
+    over_blocks(buses, one)
+    over_blocks(buses, two)
+
+
+def middle_kernel(start, insides, *refs):
+    last_steps(start, insides, refs)
+
+
+def end_kernel(start, insides, done, *refs):
+    ins = refs[: 3 * len(insides) + 5]
+    whole, plan_out, out, even, other, constants, sems = refs[3 * len(insides) + 5 :]
+    rows, _ = out.shape
+    copies = [
+        pltpu.make_async_copy(ins[-1], plan_out, sems.at[0]),
+        pltpu.make_async_copy(done, whole.at[pl.ds(0, done.shape[0]), :], sems.at[1]),
+    ]
+    for copy in copies:
+        copy.start()
+
+    def written(at):
+        copy = pltpu.make_async_copy(
+            out.at[:, at], whole.at[pl.ds(start, rows), at], sems.at[2 + at.start // BLOCK]
+        )
+        copy.start()
+        copies.append(copy)
+
+    last_steps(start, insides, (*ins, out, even, other, constants), written)
+    for copy in copies:
+        copy.wait()
 
 
 def flipped(size, bit):
@@ -250,23 +289,31 @@
     )
 
 
-def summed(total, core):
+def halves(total, core):
     size = lax.axis_size("scen")
     half = total.shape[1] // 2
     mine = jnp.where(core == 0, total[:, :half], total[:, half:])
     other = jnp.where(core == 0, total[:, half:], total[:, :half])
-    part = mine + lax.ppermute(other, "scen", flipped(size, 1))
-    for group in ((size // 2,), (2,), (4, 8, 12)):
-        others = []
-        for bit in group:
-            others.append(lax.ppermute(part, "scen", flipped(size, bit)))
-        part = part + others[0]
-        if len(group) > 1:
-            part = part + (others[1] + others[2])
-    back = lax.ppermute(part, "scen", flipped(size, 1))
+    return mine + lax.ppermute(other, "scen", flipped(size, 1))
+
+
+def joined(part, core):
+    back = lax.ppermute(part, "scen", flipped(lax.axis_size("scen"), 1))
     return jnp.where(
         core == 0, jnp.concatenate([part, back], axis=1), jnp.concatenate([back, part], axis=1)
     )
+
+
+def from_flipped(value, bit):
+    return lax.ppermute(value, "scen", flipped(lax.axis_size("scen"), bit))
+
+
+def summed(total, core):
+    part = halves(total, core)
+    for bit in (16, 2):
+        part = part + from_flipped(part, bit)
+    a, b, c = [from_flipped(part, bit) for bit in (4, 8, 12)]
+    return joined((part + a) + (b + c), core)
 
 
 def inner(start_state, price, demand, sens, gen_bus, gen_cap, tie_index, tie_len):
@@ -299,14 +346,19 @@
             scratch=[pltpu.VMEM((2 * size, buses), BF16)],
         )(state, select)
 
-    total0 = call(sum_kernel, shape(hours, buses), n_in=1)(state0)
-    select = call(select_kernel, shape(buses, 2 * slots, dtype=BF16), n_in=1)(index)
+    total0 = call(sum_kernel, shape(hours, buses), n_in=1, flops=1 << 20)(state0)
+    select = call(select_kernel, shape(buses, 2 * slots, dtype=BF16), n_in=1, flops=1 << 20)(index)
     starts = [sum(CHUNKS[:c]) * hours for c in range(len(CHUNKS))]
     sizes = [c * hours for c in CHUNKS]
     theirs = []
     for at, size in zip(starts, sizes):
         picked = pick(at, state0, size)
         theirs.append(exchange(*picked))
+
+    def early(state):
+        return call(early_kernel, shape(*state.shape), n_in=2, scratch=[pltpu.VMEM(state.shape, BF16)])(state, matrix)
+
+    slope0 = early(state0)
     mask, upper = call(bounds_kernel, (shape(8, buses), shape(8, buses)), n_in=4)(select, live, gen_bus, gen_cap)
     plan1 = summed(total0, core) / total_scen
 
@@ -317,39 +369,52 @@
         first = call(
             lambda *refs, at=at: first_kernel(at, *refs),
             (wide, wide, shape(hours, buses)),
-            n_in=10,
+            n_in=11,
             scratch=[
                 pltpu.VMEM((size, buses), BF16),
                 pltpu.VMEM((size, buses), BF16),
                 pltpu.VMEM((size, buses), F32),
                 pltpu.VMEM((2 * size, buses), BF16),
             ],
-        )(state0, prices, demands, matrix, select, *theirs[c], mask, upper, plan1)
+        )(state0, slope0, prices, demands, matrix, select, *theirs[c], mask, upper, plan1)
         firsts.append(first)
-        picked = pick(0, first[0], size)
-        theirs1.append(exchange(*picked))
+        inside = 0
+        for k, part in enumerate(PARTS[c]):
+            picked = pick(inside, first[0], part * hours)
+            theirs1.append((c, k, inside, part * hours, exchange(*picked)))
+            inside += part * hours
     total1 = sum(f[2] for f in firsts[1:]) + firsts[0][2]
-    bases = []
-    for c, (at, size) in enumerate(zip(starts, sizes)):
-        bases.append(
-            call(
-                lambda *refs, at=at: prepare_kernel(at, *refs),
-                shape(size, buses),
-                n_in=9,
-                scratch=[pltpu.VMEM((2 * size, buses), BF16)],
-            )(state0, firsts[c][0], firsts[c][1], prices, select, *theirs1[c], mask, plan1)
-        )
+    slopes = [early(first[0]) for first in firsts]
+    pieces = []
+    for c, k, inside, size, ties in theirs1:
+        base = call(
+            lambda *refs, at=starts[c] + inside, inside=inside: prepare_kernel(at, inside, *refs),
+            shape(size, buses),
+            n_in=9,
+            scratch=[pltpu.VMEM((2 * size, buses), BF16)],
+        )(state0, firsts[c][0], firsts[c][1], prices, select, *ties, mask, plan1)
+        pieces.append((inside, size, (firsts[c][0], slopes[c], base)))
     plan2 = summed(total1, core) / total_scen
-    final_state, plan2 = call(
-        final_kernel,
-        (shape(rows, buses), shape(hours, buses)),
-        n_in=2 * len(CHUNKS) + 5,
-        scratch=[
-            pltpu.VMEM((rows, buses), BF16),
-            pltpu.VMEM((rows, buses), BF16),
-            pltpu.VMEM((rows, buses), F32),
-        ],
-    )(*[f[0] for f in firsts], *bases, demands, matrix, mask, upper, plan2)
+    common = (demands, matrix, mask, upper, plan2)
+
+    def ending(kernel, at, parts, before, outs, **more):
+        size = sum(p[1] for p in parts)
+        insides = tuple(p[0] for p in parts)
+        ins = (*before, *[ref for p in parts for ref in p[2]], *common)
+        buffers = [
+            pltpu.VMEM((size, buses), BF16),
+            pltpu.VMEM((size, buses), BF16),
+            pltpu.VMEM((size, buses), F32),
+        ]
+        if before:
+            buffers = [pltpu.VMEM((size, buses), F32), *buffers, pltpu.SemaphoreType.DMA((2 + buses // BLOCK,))]
+        return call(lambda *refs: kernel(at, insides, *refs), outs, n_in=len(ins), scratch=buffers, **more)(*ins)
+
+    cut = rows - pieces[-1][1]
+    done = ending(middle_kernel, 0, pieces[:-1], (), shape(cut, buses))
+    final_state, plan2 = ending(
+        end_kernel, cut, pieces[-1:], (done,), (shape(rows, buses), shape(hours, buses)), out_space=pl.ANY
+    )
     return (final_state.reshape(start_state.shape), plan2[None])
 
 

time: 103 us -> 115 us (1.12)
  starting transfers between devices: 39.2 us -> 43.2 us
  waiting for transfers between devices: 41.1 us -> 45 us
  Pallas kernels: 18.8 us -> 21.3 us
    ppermute x14, waiting for transfers between devices: 13.1 us -> 29.7 us  [the longest x10 29.4 us: from_flipped(): return lax.ppermute(value, 'scen', flipped(lax.axis_size('scen'), bit))]
    ppermute x4 -> x6, waiting for transfers between devices: 28 us -> 15.2 us  [exchange(): lax.ppermute(a, 'region', borders(size, 0))]
    ppermute x4 -> x6, starting transfers between devices: 8.26 us -> 12.8 us  [exchange(): lax.ppermute(a, 'region', borders(size, 0))]
    ppermute x14, starting transfers between devices: 25.1 us -> 22 us  [the longest x10 21.7 us: from_flipped(): return lax.ppermute(value, 'scen', flipped(lax.axis_size('scen'), bit))]
    ppermute x4 -> x6, starting transfers between devices: 5.85 us -> 8.35 us  [exchange(): lax.ppermute(b, 'region', borders(size, 1))]
    pallas_call x5 -> x11, Pallas kernels: 7.44 us -> 9.86 us  [the longest x2 3.62 us: ending(): call(lambda *refs: kernel(at, insides, *refs), outs, n_in=len(ins), scrat...]
    pallas_call x4 -> x6, Pallas kernels: 3.9 us -> 4.35 us  [pick(): call(lambda *refs: pick_kernel(at, *refs), (shape(size, slots), shape(siz...]
  transfers between devices with their start and end apart: 22 -> 26, of which waited for: 8 -> 9; matrix products, arithmetic and copies ran while one was open for 0% -> 0% of each run, Pallas kernels for 9% -> 16%
where the time goes in v3:
time: 115 us; the launch traced here: 113 us
  waiting for transfers between devices  45 us (39%)
  starting transfers between devices  43.2 us (38%)
  Pallas kernels  21.3 us (19%)
  local copies, waits for them, and re-layouts  2.15 us (2%)
  between operations  1.3 us (1%)
    ppermute x10, waiting for transfers between devices, from_flipped(): return lax.ppermute(value, 'scen', flipped(lax.axis_size('scen'), bit))  29.4 us
    ppermute x10, starting transfers between devices, from_flipped(): return lax.ppermute(value, 'scen', flipped(lax.axis_size('scen'), bit))  21.7 us
    ppermute x6, waiting for transfers between devices, exchange(): lax.ppermute(a, 'region', borders(size, 0))  15.2 us
    ppermute x6, starting transfers between devices, exchange(): lax.ppermute(a, 'region', borders(size, 0))  12.8 us
    ppermute x6, starting transfers between devices, exchange(): lax.ppermute(b, 'region', borders(size, 1))  8.35 us
    pallas_call x2, Pallas kernels, inner(): call(lambda *refs, at=at: first_kernel(at, *refs), (wide, wide, shape(hou...  5.19 us
    pallas_call x6, Pallas kernels, pick(): call(lambda *refs: pick_kernel(at, *refs), (shape(size, slots), shape(siz...  4.35 us
    pallas_call x2, Pallas kernels, ending(): call(lambda *refs: kernel(at, insides, *refs), outs, n_in=len(ins), scrat...  3.62 us
  transfers between devices with their start and end apart: 26, of which 9 were waited for; matrix products, arithmetic and copies ran while one was open for 0% of the time, Pallas kernels for 16%

profile of v3, /device:TPU:8, one launch (start us, length us, event | category | flops | bytes accessed | tf_op | source)
XLA Modules:
  0.0 113.1 jit_solution(13336736900702033810)
XLA Ops:
  0.7 1.4 %copy-done = f32[1,16,24,1024]{3,2,1,0:T(8,128)S(1)} copy-done((f32[1,16,24,1024]{3,2,1,0:T(8,128)S(1)}, f32[1,16,24,1024]{3,2,1,0:T(8,128)}, u32[]{:S(2)}) %copy-start) | copy-done | bytes 1572888
  2.1 0.1 shard_map.99
  2.2 0.1 collective-permute-start.2
  2.4 0.4 shard_map.96.refs_1_.select.refs_5_.refs_4_
  2.8 0.7 copy-done.1
  3.5 0.8 shard_map.108
  4.2 2.2 %collective-permute-start.15 = (f32[144,512]{1,0:T(8,128)S(1)}, f32[144,512]{1,0:T(8,128)S(1)}, u32[]{:S(2)}, u32[]{:S(2)}) collective-permute-start(f32[144,512]{1,0:T(8,128)S(1)} %get-tuple-element.36), channel_id=1, source_target_pairs={{0,32},{32,0},{64,96},{96,64},{128,160},{160,128},{192,224},{224,1... | collective-permute-start | bytes 884744 | tf_op jit(solution)/shard_map/ppermute | solution.py:287
  6.5 0.8 collective-permute-start.16
  7.3 1.2 %shard_map.97 = (f32[240,512]{1,0:T(8,128)S(1)}, f32[240,512]{1,0:T(8,128)S(1)}) custom-call(f32[384,1024]{1,0:T(8,128)S(1)} %bitcast.13, bf16[1024,1024]{1,0:T(8,128)(2,1)S(1)} %shard_map.96.refs_1_.select.refs_5_.refs_4_), custom_call_target="tpu_custom_call" | custom-call | flops 4294967296 | bytes 1048576 | tf_op jit(solution)/shard_map/pallas_call | solution.py:342
  8.5 0.0 copy-start.8
  8.5 0.0 copy-start.5
  8.5 0.0 copy-start.6
  8.5 1.0 shard_map.95.refs_1_
  9.5 2.4 %collective-permute-start.3 = (f32[24,512]{1,0:T(8,128)S(1)}, f32[24,512]{1,0:T(8,128)S(1)}, u32[]{:S(2)}, u32[]{:S(2)}) collective-permute-start(f32[24,512]{1,0:T(8,128)S(1)} %select_add_fusion.1), channel_id=1, source_target_pairs={{0,16},{1,17},{2,18},{3,19},{4,20},{5,21},{6,22},{7,23},{8,24},{9,... | collective-permute-start | bytes 147464 | tf_op jit(solution)/shard_map/ppermute | solution.py:308
  11.9 0.1 compare_convert_fusion
  12.0 9.5 %collective-permute-done.3 = f32[24,512]{1,0:T(8,128)S(1)} collective-permute-done((f32[24,512]{1,0:T(8,128)S(1)}, f32[24,512]{1,0:T(8,128)S(1)}, u32[]{:S(2)}, u32[]{:S(2)}) %collective-permute-start.3) | collective-permute-done | bytes 49184 | tf_op jit(solution)/shard_map/ppermute | solution.py:308
  21.5 2.0 %collective-permute-start.4 = (f32[24,512]{1,0:T(8,128)S(1)}, f32[24,512]{1,0:T(8,128)S(1)}, u32[]{:S(2)}, u32[]{:S(2)}) collective-permute-start(f32[24,512]{1,0:T(8,128)S(1)} %add.49), channel_id=1, source_target_pairs={{0,2},{1,3},{2,0},{3,1},{4,6},{5,7},{6,4},{7,5},{8,10},{9,11},{10,... | collective-permute-start | bytes 147464 | tf_op jit(solution)/shard_map/ppermute | solution.py:308
  23.5 2.2 %collective-permute-done.4 = f32[24,512]{1,0:T(8,128)S(1)} collective-permute-done((f32[24,512]{1,0:T(8,128)S(1)}, f32[24,512]{1,0:T(8,128)S(1)}, u32[]{:S(2)}, u32[]{:S(2)}) %collective-permute-start.4) | collective-permute-done | bytes 49184 | tf_op jit(solution)/shard_map/ppermute | solution.py:308
  25.7 3.4 %collective-permute-start.5 = (f32[24,512]{1,0:T(8,128)S(1)}, f32[24,512]{1,0:T(8,128)S(1)}, u32[]{:S(2)}, u32[]{:S(2)}) collective-permute-start(f32[24,512]{1,0:T(8,128)S(1)} %add.50), channel_id=1, source_target_pairs={{0,4},{1,5},{2,6},{3,7},{4,0},{5,1},{6,2},{7,3},{8,12},{9,13},{10,... | collective-permute-start | bytes 147464 | tf_op jit(solution)/shard_map/ppermute | solution.py:308
  29.0 5.4 %collective-permute-start.6 = (f32[24,512]{1,0:T(8,128)S(1)}, f32[24,512]{1,0:T(8,128)S(1)}, u32[]{:S(2)}, u32[]{:S(2)}) collective-permute-start(f32[24,512]{1,0:T(8,128)S(1)} %add.50), channel_id=1, source_target_pairs={{0,8},{1,9},{2,10},{3,11},{4,12},{5,13},{6,14},{7,15},{8,0},{9,1},... | collective-permute-start | bytes 147464 | tf_op jit(solution)/shard_map/ppermute | solution.py:308
  34.4 0.0 collective-permute-start.7
  34.4 2.0 %collective-permute-start = (f32[240,512]{1,0:T(8,128)S(1)}, f32[240,512]{1,0:T(8,128)S(1)}, u32[]{:S(2)}, u32[]{:S(2)}) collective-permute-start(f32[240,512]{1,0:T(8,128)S(1)} %get-tuple-element.24), channel_id=1, source_target_pairs={{0,32},{32,0},{64,96},{96,64},{128,160},{160,128},{192,224},{224,1... | collective-permute-start | bytes 1474568 | tf_op jit(solution)/shard_map/ppermute | solution.py:287
  36.4 1.5 %collective-permute-done.6 = f32[24,512]{1,0:T(8,128)S(1)} collective-permute-done((f32[24,512]{1,0:T(8,128)S(1)}, f32[24,512]{1,0:T(8,128)S(1)}, u32[]{:S(2)}, u32[]{:S(2)}) %collective-permute-start.6) | collective-permute-done | bytes 49184 | tf_op jit(solution)/shard_map/ppermute | solution.py:308
  38.0 2.8 %collective-permute-start.1 = (f32[240,512]{1,0:T(8,128)S(1)}, f32[240,512]{1,0:T(8,128)S(1)}, u32[]{:S(2)}, u32[]{:S(2)}) collective-permute-start(f32[240,512]{1,0:T(8,128)S(1)} %get-tuple-element.25), channel_id=1, source_target_pairs={{32,64},{64,32},{96,128},{128,96},{160,192},{192,160},{224,0},{0,2... | collective-permute-start | bytes 1474568 | tf_op jit(solution)/shard_map/ppermute | solution.py:288
  40.8 0.0 collective-permute-done.7
  40.8 0.0 copy-start.3
  40.8 0.0 copy-start.4
  40.8 0.1 collective-permute-start.8
  40.9 1.9 %shard_map.98 = (f32[8,1024]{1,0:T(8,128)S(1)}, f32[8,1024]{1,0:T(8,128)S(1)}) custom-call(bf16[1024,1024]{1,0:T(8,128)(2,1)S(1)} %shard_map.96.refs_1_.select.refs_5_.refs_4_, f32[1,1024]{1,0:T(1,128)S(1)} %broadcast_select_fusion.live, s32[1,512]{1,0:T(1,128)S(1)} %copy-done.5, f32[1,512]{1,0:T(1,128)S(1)} %copy-done.6), custom_call_target="tpu_custom_call" | custom-call | flops 4294967296 | bytes 1048576 | tf_op jit(solution)/shard_map/pallas_call | solution.py:362
  42.9 2.1 %shard_map.109 = (f32[144,1024]{1,0:T(8,128)S(1)}, f32[144,1024]{1,0:T(8,128)S(1)}, f32[24,1024]{1,0:T(8,128)S(1)}) custom-call(f32[384,1024]{1,0:T(8,128)S(1)} %bitcast.15, f32[384,1024]{1,0:T(8,128)S(1)} %shard_map.95.refs_1_, f32[384,1024]{1,0:T(8,128)S(1)} %bitcast.28, f32[384,1024]{1,0:T(8,128)S(1)} %bitcast.34, bf16[1024,1024]{1,0:T(8,128)(2,1)S(1)} %bitcast.22, ...), custom_call_target="tpu_custom_call" | custom-call | flops 4294967296 | bytes 1048576 | tf_op jit(solution)/shard_map/pallas_call | solution.py:369
  45.0 0.8 shard_map.112
  45.8 1.9 %collective-permute-start.24 = (f32[144,512]{1,0:T(8,128)S(1)}, f32[144,512]{1,0:T(8,128)S(1)}, u32[]{:S(2)}, u32[]{:S(2)}) collective-permute-start(f32[144,512]{1,0:T(8,128)S(1)} %get-tuple-element.42), channel_id=1, source_target_pairs={{0,32},{32,0},{64,96},{96,64},{128,160},{160,128},{192,224},{224,1... | collective-permute-start | bytes 884744 | tf_op jit(solution)/shard_map/ppermute | solution.py:287
  47.7 1.2 %collective-permute-start.25 = (f32[144,512]{1,0:T(8,128)S(1)}, f32[144,512]{1,0:T(8,128)S(1)}, u32[]{:S(2)}, u32[]{:S(2)}) collective-permute-start(f32[144,512]{1,0:T(8,128)S(1)} %get-tuple-element.43), channel_id=1, source_target_pairs={{32,64},{64,32},{96,128},{128,96},{160,192},{192,160},{224,0},{0,2... | collective-permute-start | bytes 884744 | tf_op jit(solution)/shard_map/ppermute | solution.py:288
  48.9 0.5 shard_map.111.refs_2_
  49.4 15.2 %collective-permute-done.refs_6_ = f32[240,512]{1,0:T(8,128)S(1)} collective-permute-done((f32[240,512]{1,0:T(8,128)S(1)}, f32[240,512]{1,0:T(8,128)S(1)}, u32[]{:S(2)}, u32[]{:S(2)}) %collective-permute-start) | collective-permute-done | bytes 491552 | tf_op jit(solution)/shard_map/ppermute | solution.py:287
  64.6 3.1 %shard_map.100 = (f32[240,1024]{1,0:T(8,128)S(1)}, f32[240,1024]{1,0:T(8,128)S(1)}, f32[24,1024]{1,0:T(8,128)S(1)}) custom-call(f32[384,1024]{1,0:T(8,128)S(1)} %bitcast.16, f32[384,1024]{1,0:T(8,128)S(1)} %shard_map.95.refs_1_, f32[384,1024]{1,0:T(8,128)S(1)} %bitcast.29, f32[384,1024]{1,0:T(8,128)S(1)} %bitcast.35, bf16[1024,1024]{1,0:T(8,128)(2,1)S(1)} %bitcast.24, ...), custom_call_target="tpu_custom_call" | custom-call | flops 4294967296 | bytes 1048576 | tf_op jit(solution)/shard_map/pallas_call | solution.py:369
  67.7 0.6 shard_map.106
  68.3 0.4 shard_map.104
  68.8 0.6 shard_map.102
  69.4 0.1 collective-permute-start.17
  69.5 0.7 shard_map.101.refs_1_.refs_4_.refs_7_
  70.2 2.0 %collective-permute-start.13 = (f32[96,512]{1,0:T(8,128)S(1)}, f32[96,512]{1,0:T(8,128)S(1)}, u32[]{:S(2)}, u32[]{:S(2)}) collective-permute-start(f32[96,512]{1,0:T(8,128)S(1)} %get-tuple-element.34), channel_id=1, source_target_pairs={{0,32},{32,0},{64,96},{96,64},{128,160},{160,128},{192,224},{224,1... | collective-permute-start | bytes 589832 | tf_op jit(solution)/shard_map/ppermute | solution.py:287
  72.2 1.0 collective-permute-start.14
  73.2 3.0 %collective-permute-start.11 = (f32[48,512]{1,0:T(8,128)S(1)}, f32[48,512]{1,0:T(8,128)S(1)}, u32[]{:S(2)}, u32[]{:S(2)}) collective-permute-start(f32[48,512]{1,0:T(8,128)S(1)} %get-tuple-element.32), channel_id=1, source_target_pairs={{0,32},{32,0},{64,96},{96,64},{128,160},{160,128},{192,224},{224,1... | collective-permute-start | bytes 294920 | tf_op jit(solution)/shard_map/ppermute | solution.py:287
  76.2 0.1 collective-permute-start.12
  76.4 0.7 collective-permute-start.18
  77.1 1.0 shard_map.113.refs_3_
  78.0 8.9 %collective-permute-done.18 = f32[24,512]{1,0:T(8,128)S(1)} collective-permute-done((f32[24,512]{1,0:T(8,128)S(1)}, f32[24,512]{1,0:T(8,128)S(1)}, u32[]{:S(2)}, u32[]{:S(2)}) %collective-permute-start.18) | collective-permute-done | bytes 49184 | tf_op jit(solution)/shard_map/ppermute | solution.py:308
  87.0 2.4 %collective-permute-start.10 = (f32[96,512]{1,0:T(8,128)S(1)}, f32[96,512]{1,0:T(8,128)S(1)}, u32[]{:S(2)}, u32[]{:S(2)}) collective-permute-start(f32[96,512]{1,0:T(8,128)S(1)} %get-tuple-element.31), channel_id=1, source_target_pairs={{32,64},{64,32},{96,128},{128,96},{160,192},{192,160},{224,0},{0,2... | collective-permute-start | bytes 589832 | tf_op jit(solution)/shard_map/ppermute | solution.py:288
  89.4 1.7 %collective-permute-start.9 = (f32[96,512]{1,0:T(8,128)S(1)}, f32[96,512]{1,0:T(8,128)S(1)}, u32[]{:S(2)}, u32[]{:S(2)}) collective-permute-start(f32[96,512]{1,0:T(8,128)S(1)} %get-tuple-element.30), channel_id=1, source_target_pairs={{0,32},{32,0},{64,96},{96,64},{128,160},{160,128},{192,224},{224,1... | collective-permute-start | bytes 589832 | tf_op jit(solution)/shard_map/ppermute | solution.py:287
  91.1 1.2 %collective-permute-start.19 = (f32[24,512]{1,0:T(8,128)S(1)}, f32[24,512]{1,0:T(8,128)S(1)}, u32[]{:S(2)}, u32[]{:S(2)}) collective-permute-start(f32[24,512]{1,0:T(8,128)S(1)} %add.56), channel_id=1, source_target_pairs={{0,2},{1,3},{2,0},{3,1},{4,6},{5,7},{6,4},{7,5},{8,10},{9,11},{10,... | collective-permute-start | bytes 147464 | tf_op jit(solution)/shard_map/ppermute | solution.py:308
  92.3 0.8 shard_map.105.refs_5_
  93.1 2.1 %collective-permute-done.19 = f32[24,512]{1,0:T(8,128)S(1)} collective-permute-done((f32[24,512]{1,0:T(8,128)S(1)}, f32[24,512]{1,0:T(8,128)S(1)}, u32[]{:S(2)}, u32[]{:S(2)}) %collective-permute-start.19) | collective-permute-done | bytes 49184 | tf_op jit(solution)/shard_map/ppermute | solution.py:308
  95.2 1.0 collective-permute-start.20
  96.3 5.4 %collective-permute-start.21 = (f32[24,512]{1,0:T(8,128)S(1)}, f32[24,512]{1,0:T(8,128)S(1)}, u32[]{:S(2)}, u32[]{:S(2)}) collective-permute-start(f32[24,512]{1,0:T(8,128)S(1)} %add.57), channel_id=1, source_target_pairs={{0,8},{1,9},{2,10},{3,11},{4,12},{5,13},{6,14},{7,15},{8,0},{9,1},... | collective-permute-start | bytes 147464 | tf_op jit(solution)/shard_map/ppermute | solution.py:308
  101.7 0.1 collective-permute-start.22
  101.8 0.9 shard_map.107.refs_8_
  102.7 1.8 %collective-permute-done.21 = f32[24,512]{1,0:T(8,128)S(1)} collective-permute-done((f32[24,512]{1,0:T(8,128)S(1)}, f32[24,512]{1,0:T(8,128)S(1)}, u32[]{:S(2)}, u32[]{:S(2)}) %collective-permute-start.21) | collective-permute-done | bytes 49184 | tf_op jit(solution)/shard_map/ppermute | solution.py:308
  104.5 3.5 %collective-permute-done.22 = f32[24,512]{1,0:T(8,128)S(1)} collective-permute-done((f32[24,512]{1,0:T(8,128)S(1)}, f32[24,512]{1,0:T(8,128)S(1)}, u32[]{:S(2)}, u32[]{:S(2)}) %collective-permute-start.22) | collective-permute-done | bytes 49184 | tf_op jit(solution)/shard_map/ppermute | solution.py:308
  108.0 0.1 collective-permute-start.23
  108.1 0.9 shard_map.103.refs_2_
  109.0 0.3 collective-permute-done.23
  109.3 1.7 %shard_map.110.refs_0_ = f32[240,1024]{1,0:T(8,128)S(1)} custom-call(f32[240,1024]{1,0:T(8,128)S(1)} %get-tuple-element.28.state.refs_0_.refs_1_.refs_3_.refs_6_, f32[240,1024]{1,0:T(8,128)S(1)} %shard_map.101.refs_1_.refs_4_.refs_7_, f32[96,1024]{1,0:T(8,128)S(1)} %shard_map.103.refs_2_, ...), custom_call_target="tpu_custom_call" | custom-call | flops 4294967296 | bytes 1048576 | tf_op jit(solution)/shard_map/pallas_call | solution.py:411
  111.1 1.9 %shard_map.114 = (f32[384,1024]{1,0:T(8,128)}, f32[24,1024]{1,0:T(8,128)}) custom-call(f32[240,1024]{1,0:T(8,128)S(1)} %shard_map.110.refs_0_, f32[144,1024]{1,0:T(8,128)S(1)} %get-tuple-element.40.state.refs_0_.refs_1_, f32[144,1024]{1,0:T(8,128)S(1)} %shard_map.111.refs_2_, f32[144,1024]{1,0:T(8,128)S(1)} %shard_map.113.refs_3_, f32[384,1024]{1,0:T(8,128)S(1)} %bitcast.37, ...), custom_call_target="tpu_custom_call" | custom-call | flops 4294967296 | bytes 1048576 | tf_op jit(solution)/shard_map/pallas_call | solution.py:411
  (44 shorter events, 0.2 us)
Async XLA Ops:
  0.6 1.7 %copy-start.7 = (s32[1,2,512]{2,1,0:T(2,128)S(1)}, s32[1,2,512]{2,1,0:T(2,128)}, u32[]{:S(2)}) copy-start(s32[1,2,512]{2,1,0:T(2,128)} %param.14) | copy-start | bytes 12292
  0.7 1.4 %copy-start = (f32[1,16,24,1024]{3,2,1,0:T(8,128)S(1)}, f32[1,16,24,1024]{3,2,1,0:T(8,128)}, u32[]{:S(2)}) copy-start(f32[1,16,24,1024]{3,2,1,0:T(8,128)} %param.8) | copy-start | bytes 4718596
  2.1 1.4 %copy-start.1 = (f32[1,16,24,1024]{3,2,1,0:T(8,128)S(1)}, f32[1,16,24,1024]{3,2,1,0:T(8,128)}, u32[]{:S(2)}) copy-start(f32[1,16,24,1024]{3,2,1,0:T(8,128)} %param.8) | copy-start | bytes 4718596
  2.2 7.3 %collective-permute-start.2 = (f32[24,512]{1,0:T(8,128)S(1)}, f32[24,512]{1,0:T(8,128)S(1)}, u32[]{:S(2)}, u32[]{:S(2)}) collective-permute-start(f32[24,512]{1,0:T(8,128)S(1)} %slice_select_fusion.1), channel_id=1, source_target_pairs={{0,1},{1,0},{2,3},{3,2},{4,5},{5,4},{6,7},{7,6},{8,9},{9,8},{10,11... | collective-permute-start | bytes 147464 | tf_op jit(solution)/shard_map/ppermute | solution.py:297
  4.2 38.7 %collective-permute-start.15 = (f32[144,512]{1,0:T(8,128)S(1)}, f32[144,512]{1,0:T(8,128)S(1)}, u32[]{:S(2)}, u32[]{:S(2)}) collective-permute-start(f32[144,512]{1,0:T(8,128)S(1)} %get-tuple-element.36), channel_id=1, source_target_pairs={{0,32},{32,0},{64,96},{96,64},{128,160},{160,128},{192,224},{224,1... | collective-permute-start | bytes 884744 | tf_op jit(solution)/shard_map/ppermute | solution.py:287
  6.5 2.0 %copy-start.2 = (bf16[1,1024,1024]{2,1,0:T(8,128)(2,1)S(1)}, bf16[1,1024,1024]{2,1,0:T(8,128)(2,1)}, u32[]{:S(2)}) copy-start(bf16[1,1024,1024]{2,1,0:T(8,128)(2,1)} %param.11) | copy-start | bytes 6291460
  6.5 36.4 %collective-permute-start.16 = (f32[144,512]{1,0:T(8,128)S(1)}, f32[144,512]{1,0:T(8,128)S(1)}, u32[]{:S(2)}, u32[]{:S(2)}) collective-permute-start(f32[144,512]{1,0:T(8,128)S(1)} %get-tuple-element.37), channel_id=1, source_target_pairs={{32,64},{64,32},{96,128},{128,96},{160,192},{192,160},{224,0},{0,2... | collective-permute-start | bytes 884744 | tf_op jit(solution)/shard_map/ppermute | solution.py:288
  8.5 3.4 %copy-start.8 = (s32[1,2]{1,0:T(1,128)S(1)}, s32[1,2]{1,0:T(1,128)}, u32[]{:S(2)}) copy-start(s32[1,2]{1,0:T(1,128)} %param.15) | copy-start | bytes 28
  8.5 32.4 %copy-start.5 = (s32[1,512]{1,0:T(1,128)S(1)}, s32[1,512]{1,0:T(1,128)}, u32[]{:S(2)}) copy-start(s32[1,512]{1,0:T(1,128)} %gen_bus.1) | copy-start | bytes 6148
  8.5 32.4 %copy-start.6 = (f32[1,512]{1,0:T(1,128)S(1)}, f32[1,512]{1,0:T(1,128)}, u32[]{:S(2)}) copy-start(f32[1,512]{1,0:T(1,128)} %gen_cap.1) | copy-start | bytes 6148
  9.5 11.9 %collective-permute-start.3 = (f32[24,512]{1,0:T(8,128)S(1)}, f32[24,512]{1,0:T(8,128)S(1)}, u32[]{:S(2)}, u32[]{:S(2)}) collective-permute-start(f32[24,512]{1,0:T(8,128)S(1)} %select_add_fusion.1), channel_id=1, source_target_pairs={{0,16},{1,17},{2,18},{3,19},{4,20},{5,21},{6,22},{7,23},{8,24},{9,... | collective-permute-start | bytes 147464 | tf_op jit(solution)/shard_map/ppermute | solution.py:308
  21.5 4.2 %collective-permute-start.4 = (f32[24,512]{1,0:T(8,128)S(1)}, f32[24,512]{1,0:T(8,128)S(1)}, u32[]{:S(2)}, u32[]{:S(2)}) collective-permute-start(f32[24,512]{1,0:T(8,128)S(1)} %add.49), channel_id=1, source_target_pairs={{0,2},{1,3},{2,0},{3,1},{4,6},{5,7},{6,4},{7,5},{8,10},{9,11},{10,... | collective-permute-start | bytes 147464 | tf_op jit(solution)/shard_map/ppermute | solution.py:308
  25.7 8.8 %collective-permute-start.5 = (f32[24,512]{1,0:T(8,128)S(1)}, f32[24,512]{1,0:T(8,128)S(1)}, u32[]{:S(2)}, u32[]{:S(2)}) collective-permute-start(f32[24,512]{1,0:T(8,128)S(1)} %add.50), channel_id=1, source_target_pairs={{0,4},{1,5},{2,6},{3,7},{4,0},{5,1},{6,2},{7,3},{8,12},{9,13},{10,... | collective-permute-start | bytes 147464 | tf_op jit(solution)/shard_map/ppermute | solution.py:308
  29.0 8.9 %collective-permute-start.6 = (f32[24,512]{1,0:T(8,128)S(1)}, f32[24,512]{1,0:T(8,128)S(1)}, u32[]{:S(2)}, u32[]{:S(2)}) collective-permute-start(f32[24,512]{1,0:T(8,128)S(1)} %add.50), channel_id=1, source_target_pairs={{0,8},{1,9},{2,10},{3,11},{4,12},{5,13},{6,14},{7,15},{8,0},{9,1},... | collective-permute-start | bytes 147464 | tf_op jit(solution)/shard_map/ppermute | solution.py:308
  34.4 6.4 %collective-permute-start.7 = (f32[24,512]{1,0:T(8,128)S(1)}, f32[24,512]{1,0:T(8,128)S(1)}, u32[]{:S(2)}, u32[]{:S(2)}) collective-permute-start(f32[24,512]{1,0:T(8,128)S(1)} %add.50), channel_id=1, source_target_pairs={{0,12},{1,13},{2,14},{3,15},{4,8},{5,9},{6,10},{7,11},{8,4},{9,5},... | collective-permute-start | bytes 147464 | tf_op jit(solution)/shard_map/ppermute | solution.py:308
  34.4 30.2 %collective-permute-start = (f32[240,512]{1,0:T(8,128)S(1)}, f32[240,512]{1,0:T(8,128)S(1)}, u32[]{:S(2)}, u32[]{:S(2)}) collective-permute-start(f32[240,512]{1,0:T(8,128)S(1)} %get-tuple-element.24), channel_id=1, source_target_pairs={{0,32},{32,0},{64,96},{96,64},{128,160},{160,128},{192,224},{224,1... | collective-permute-start | bytes 1474568 | tf_op jit(solution)/shard_map/ppermute | solution.py:287
  38.0 26.7 %collective-permute-start.1 = (f32[240,512]{1,0:T(8,128)S(1)}, f32[240,512]{1,0:T(8,128)S(1)}, u32[]{:S(2)}, u32[]{:S(2)}) collective-permute-start(f32[240,512]{1,0:T(8,128)S(1)} %get-tuple-element.25), channel_id=1, source_target_pairs={{32,64},{64,32},{96,128},{128,96},{160,192},{192,160},{224,0},{0,2... | collective-permute-start | bytes 1474568 | tf_op jit(solution)/shard_map/ppermute | solution.py:288
  40.8 2.1 %copy-start.3 = (f32[1,16,24,1024]{3,2,1,0:T(8,128)S(1)}, f32[1,16,24,1024]{3,2,1,0:T(8,128)}, u32[]{:S(2)}) copy-start(f32[1,16,24,1024]{3,2,1,0:T(8,128)} %param.9) | copy-start | bytes 4718596
  40.8 2.1 %copy-start.4 = (f32[1,16,24,1024]{3,2,1,0:T(8,128)S(1)}, f32[1,16,24,1024]{3,2,1,0:T(8,128)}, u32[]{:S(2)}) copy-start(f32[1,16,24,1024]{3,2,1,0:T(8,128)} %param.10) | copy-start | bytes 4718596
  40.8 2.0 %collective-permute-start.8 = (f32[24,512]{1,0:T(8,128)S(1)}, f32[24,512]{1,0:T(8,128)S(1)}, u32[]{:S(2)}, u32[]{:S(2)}) collective-permute-start(f32[24,512]{1,0:T(8,128)S(1)} %add_add_fusion.1), channel_id=1, source_target_pairs={{0,1},{1,0},{2,3},{3,2},{4,5},{5,4},{6,7},{7,6},{8,9},{9,8},{10,11... | collective-permute-start | bytes 147464 | tf_op jit(solution)/shard_map/ppermute | solution.py:301
  45.8 30.4 %collective-permute-start.24 = (f32[144,512]{1,0:T(8,128)S(1)}, f32[144,512]{1,0:T(8,128)S(1)}, u32[]{:S(2)}, u32[]{:S(2)}) collective-permute-start(f32[144,512]{1,0:T(8,128)S(1)} %get-tuple-element.42), channel_id=1, source_target_pairs={{0,32},{32,0},{64,96},{96,64},{128,160},{160,128},{192,224},{224,1... | collective-permute-start | bytes 884744 | tf_op jit(solution)/shard_map/ppermute | solution.py:287
  47.7 28.7 %collective-permute-start.25 = (f32[144,512]{1,0:T(8,128)S(1)}, f32[144,512]{1,0:T(8,128)S(1)}, u32[]{:S(2)}, u32[]{:S(2)}) collective-permute-start(f32[144,512]{1,0:T(8,128)S(1)} %get-tuple-element.43), channel_id=1, source_target_pairs={{32,64},{64,32},{96,128},{128,96},{160,192},{192,160},{224,0},{0,2... | collective-permute-start | bytes 884744 | tf_op jit(solution)/shard_map/ppermute | solution.py:288
  69.4 3.8 %collective-permute-start.17 = (f32[24,512]{1,0:T(8,128)S(1)}, f32[24,512]{1,0:T(8,128)S(1)}, u32[]{:S(2)}, u32[]{:S(2)}) collective-permute-start(f32[24,512]{1,0:T(8,128)S(1)} %slice_select_fusion), channel_id=1, source_target_pairs={{0,1},{1,0},{2,3},{3,2},{4,5},{5,4},{6,7},{7,6},{8,9},{9,8},{10,11... | collective-permute-start | bytes 147464 | tf_op jit(solution)/shard_map/ppermute | solution.py:297
  70.2 26.1 %collective-permute-start.13 = (f32[96,512]{1,0:T(8,128)S(1)}, f32[96,512]{1,0:T(8,128)S(1)}, u32[]{:S(2)}, u32[]{:S(2)}) collective-permute-start(f32[96,512]{1,0:T(8,128)S(1)} %get-tuple-element.34), channel_id=1, source_target_pairs={{0,32},{32,0},{64,96},{96,64},{128,160},{160,128},{192,224},{224,1... | collective-permute-start | bytes 589832 | tf_op jit(solution)/shard_map/ppermute | solution.py:287
  72.2 29.5 %collective-permute-start.14 = (f32[96,512]{1,0:T(8,128)S(1)}, f32[96,512]{1,0:T(8,128)S(1)}, u32[]{:S(2)}, u32[]{:S(2)}) collective-permute-start(f32[96,512]{1,0:T(8,128)S(1)} %get-tuple-element.35), channel_id=1, source_target_pairs={{32,64},{64,32},{96,128},{128,96},{160,192},{192,160},{224,0},{0,2... | collective-permute-start | bytes 589832 | tf_op jit(solution)/shard_map/ppermute | solution.py:288
  73.2 16.1 %collective-permute-start.11 = (f32[48,512]{1,0:T(8,128)S(1)}, f32[48,512]{1,0:T(8,128)S(1)}, u32[]{:S(2)}, u32[]{:S(2)}) collective-permute-start(f32[48,512]{1,0:T(8,128)S(1)} %get-tuple-element.32), channel_id=1, source_target_pairs={{0,32},{32,0},{64,96},{96,64},{128,160},{160,128},{192,224},{224,1... | collective-permute-start | bytes 294920 | tf_op jit(solution)/shard_map/ppermute | solution.py:287
  76.2 14.9 %collective-permute-start.12 = (f32[48,512]{1,0:T(8,128)S(1)}, f32[48,512]{1,0:T(8,128)S(1)}, u32[]{:S(2)}, u32[]{:S(2)}) collective-permute-start(f32[48,512]{1,0:T(8,128)S(1)} %get-tuple-element.33), channel_id=1, source_target_pairs={{32,64},{64,32},{96,128},{128,96},{160,192},{192,160},{224,0},{0,2... | collective-permute-start | bytes 294920 | tf_op jit(solution)/shard_map/ppermute | solution.py:288
  76.4 10.6 %collective-permute-start.18 = (f32[24,512]{1,0:T(8,128)S(1)}, f32[24,512]{1,0:T(8,128)S(1)}, u32[]{:S(2)}, u32[]{:S(2)}) collective-permute-start(f32[24,512]{1,0:T(8,128)S(1)} %select_add_fusion), channel_id=1, source_target_pairs={{0,16},{1,17},{2,18},{3,19},{4,20},{5,21},{6,22},{7,23},{8,24},{9,... | collective-permute-start | bytes 147464 | tf_op jit(solution)/shard_map/ppermute | solution.py:308
  87.0 21.1 %collective-permute-start.10 = (f32[96,512]{1,0:T(8,128)S(1)}, f32[96,512]{1,0:T(8,128)S(1)}, u32[]{:S(2)}, u32[]{:S(2)}) collective-permute-start(f32[96,512]{1,0:T(8,128)S(1)} %get-tuple-element.31), channel_id=1, source_target_pairs={{32,64},{64,32},{96,128},{128,96},{160,192},{192,160},{224,0},{0,2... | collective-permute-start | bytes 589832 | tf_op jit(solution)/shard_map/ppermute | solution.py:288
  89.4 18.7 %collective-permute-start.9 = (f32[96,512]{1,0:T(8,128)S(1)}, f32[96,512]{1,0:T(8,128)S(1)}, u32[]{:S(2)}, u32[]{:S(2)}) collective-permute-start(f32[96,512]{1,0:T(8,128)S(1)} %get-tuple-element.30), channel_id=1, source_target_pairs={{0,32},{32,0},{64,96},{96,64},{128,160},{160,128},{192,224},{224,1... | collective-permute-start | bytes 589832 | tf_op jit(solution)/shard_map/ppermute | solution.py:287
  91.1 4.1 %collective-permute-start.19 = (f32[24,512]{1,0:T(8,128)S(1)}, f32[24,512]{1,0:T(8,128)S(1)}, u32[]{:S(2)}, u32[]{:S(2)}) collective-permute-start(f32[24,512]{1,0:T(8,128)S(1)} %add.56), channel_id=1, source_target_pairs={{0,2},{1,3},{2,0},{3,1},{4,6},{5,7},{6,4},{7,5},{8,10},{9,11},{10,... | collective-permute-start | bytes 147464 | tf_op jit(solution)/shard_map/ppermute | solution.py:308
  95.2 7.5 %collective-permute-start.20 = (f32[24,512]{1,0:T(8,128)S(1)}, f32[24,512]{1,0:T(8,128)S(1)}, u32[]{:S(2)}, u32[]{:S(2)}) collective-permute-start(f32[24,512]{1,0:T(8,128)S(1)} %add.57), channel_id=1, source_target_pairs={{0,4},{1,5},{2,6},{3,7},{4,0},{5,1},{6,2},{7,3},{8,12},{9,13},{10,... | collective-permute-start | bytes 147464 | tf_op jit(solution)/shard_map/ppermute | solution.py:308
  96.3 8.3 %collective-permute-start.21 = (f32[24,512]{1,0:T(8,128)S(1)}, f32[24,512]{1,0:T(8,128)S(1)}, u32[]{:S(2)}, u32[]{:S(2)}) collective-permute-start(f32[24,512]{1,0:T(8,128)S(1)} %add.57), channel_id=1, source_target_pairs={{0,8},{1,9},{2,10},{3,11},{4,12},{5,13},{6,14},{7,15},{8,0},{9,1},... | collective-permute-start | bytes 147464 | tf_op jit(solution)/shard_map/ppermute | solution.py:308
  101.7 6.3 %collective-permute-start.22 = (f32[24,512]{1,0:T(8,128)S(1)}, f32[24,512]{1,0:T(8,128)S(1)}, u32[]{:S(2)}, u32[]{:S(2)}) collective-permute-start(f32[24,512]{1,0:T(8,128)S(1)} %add.57), channel_id=1, source_target_pairs={{0,12},{1,13},{2,14},{3,15},{4,8},{5,9},{6,10},{7,11},{8,4},{9,5},... | collective-permute-start | bytes 147464 | tf_op jit(solution)/shard_map/ppermute | solution.py:308
  108.0 1.3 %collective-permute-start.23 = (f32[24,512]{1,0:T(8,128)S(1)}, f32[24,512]{1,0:T(8,128)S(1)}, u32[]{:S(2)}, u32[]{:S(2)}) collective-permute-start(f32[24,512]{1,0:T(8,128)S(1)} %add_add_fusion), channel_id=1, source_target_pairs={{0,1},{1,0},{2,3},{3,2},{4,5},{5,4},{6,7},{7,6},{8,9},{9,8},{10,11... | collective-permute-start | bytes 147464 | tf_op jit(solution)/shard_map/ppermute | solution.py:301

commit v4 on v3

--- a/solution.py
+++ b/solution.py
@@ -90,16 +90,18 @@
     pair[rows:, at] = low
 
 
-def pick_kernel(start, state, select, left, right, pair):
-    rows, slots = left.shape
+def pick_kernel(start, sides, state, select, *refs):
+    outs, pair = refs[:-1], refs[-1]
+    rows, slots = outs[0].shape
     over_blocks(state.shape[1], lambda at: split_into(pair, state[start : start + rows, at], at))
 
-    def one(at):
-        both = dot(pair[...], select[:, at])
-        out, base = (left, 0) if at.start < slots else (right, slots)
-        out[:, pl.ds(at.start - base, at.size)] = both[:rows] + both[rows:]
-
-    over_blocks(2 * slots, one)
+    for side, out in zip(sides, outs):
+
+        def one(at):
+            both = dot(pair[...], select[:, pl.ds(side * slots + at.start, at.size)])
+            out[:, at] = both[:rows] + both[rows:]
+
+        over_blocks(slots, one)
 
 
 def bounds_kernel(select, live, gen_bus, gen_cap, mask, upper):
@@ -249,16 +251,18 @@
     last_steps(start, insides, refs)
 
 
-def end_kernel(start, insides, done, *refs):
-    ins = refs[: 3 * len(insides) + 5]
-    whole, plan_out, out, even, other, constants, sems = refs[3 * len(insides) + 5 :]
-    rows, _ = out.shape
+def end_kernel(start, insides, *refs):
+    done, state0, dual, price, select, left, right, plan1 = refs[:8]
+    state, slope, demand, matrix, mask, upper, plan = refs[8:15]
+    whole, plan_out, out, base, pair, even, other, constants, sems = refs[15:]
+    rows = out.shape[0]
     copies = [
-        pltpu.make_async_copy(ins[-1], plan_out, sems.at[0]),
+        pltpu.make_async_copy(plan, plan_out, sems.at[0]),
         pltpu.make_async_copy(done, whole.at[pl.ds(0, done.shape[0]), :], sems.at[1]),
     ]
     for copy in copies:
         copy.start()
+    prepare_kernel(start, insides[0], state0, state, dual, price, select, left, right, mask, plan1, base, pair)
 
     def written(at):
         copy = pltpu.make_async_copy(
@@ -267,6 +271,7 @@
         copy.start()
         copies.append(copy)
 
+    ins = (state, slope, base, demand, matrix, mask, upper, plan)
     last_steps(start, insides, (*ins, out, even, other, constants), written)
     for copy in copies:
         copy.wait()
@@ -283,10 +288,9 @@
 
 def exchange(a, b):
     size = lax.axis_size("region")
-    return (
-        lax.ppermute(a, "region", borders(size, 0)),
-        lax.ppermute(b, "region", borders(size, 1)),
-    )
+    a = lax.ppermute(a, "region", borders(size, 0))
+    b = lax.ppermute(b, "region", borders(size, 1))
+    return a, b
 
 
 def halves(total, core):
@@ -338,10 +342,10 @@
     def shape(*dims, dtype=F32):
         return jax.ShapeDtypeStruct(dims, dtype)
 
-    def pick(at, state, size):
+    def pick(at, state, size, sides=(0, 1)):
         return call(
-            lambda *refs: pick_kernel(at, *refs),
-            (shape(size, slots), shape(size, slots)),
+            lambda *refs: pick_kernel(at, sides, *refs),
+            (shape(size, slots),) * len(sides),
             n_in=2,
             scratch=[pltpu.VMEM((2 * size, buses), BF16)],
         )(state, select)
@@ -351,8 +355,11 @@
     starts = [sum(CHUNKS[:c]) * hours for c in range(len(CHUNKS))]
     sizes = [c * hours for c in CHUNKS]
     theirs = []
-    for at, size in zip(starts, sizes):
-        picked = pick(at, state0, size)
+    for c, (at, size) in enumerate(zip(starts, sizes)):
+        if c == 0:
+            picked = pick(at, state0, size, (0,)) + pick(at, state0, size, (1,))
+        else:
+            picked = pick(at, state0, size)
         theirs.append(exchange(*picked))
 
     def early(state):
@@ -386,7 +393,7 @@
     total1 = sum(f[2] for f in firsts[1:]) + firsts[0][2]
     slopes = [early(first[0]) for first in firsts]
     pieces = []
-    for c, k, inside, size, ties in theirs1:
+    for c, k, inside, size, ties in theirs1[:-1]:
         base = call(
             lambda *refs, at=starts[c] + inside, inside=inside: prepare_kernel(at, inside, *refs),
             shape(size, buses),
@@ -397,23 +404,40 @@
     plan2 = summed(total1, core) / total_scen
     common = (demands, matrix, mask, upper, plan2)
 
-    def ending(kernel, at, parts, before, outs, **more):
-        size = sum(p[1] for p in parts)
-        insides = tuple(p[0] for p in parts)
-        ins = (*before, *[ref for p in parts for ref in p[2]], *common)
+    def ending(kernel, at, size, insides, ins, outs, more=(), **kwargs):
         buffers = [
+            *more,
             pltpu.VMEM((size, buses), BF16),
             pltpu.VMEM((size, buses), BF16),
             pltpu.VMEM((size, buses), F32),
         ]
-        if before:
-            buffers = [pltpu.VMEM((size, buses), F32), *buffers, pltpu.SemaphoreType.DMA((2 + buses // BLOCK,))]
-        return call(lambda *refs: kernel(at, insides, *refs), outs, n_in=len(ins), scratch=buffers, **more)(*ins)
-
-    cut = rows - pieces[-1][1]
-    done = ending(middle_kernel, 0, pieces[:-1], (), shape(cut, buses))
+        if more:
+            buffers.append(pltpu.SemaphoreType.DMA((2 + buses // BLOCK,)))
+        return call(lambda *refs: kernel(at, insides, *refs), outs, n_in=len(ins), scratch=buffers, **kwargs)(*ins)
+
+    c, _, inside, size, ties = theirs1[-1]
+    cut = rows - size
+    done = ending(
+        middle_kernel,
+        0,
+        cut,
+        tuple(p[0] for p in pieces),
+        (*[ref for p in pieces for ref in p[2]], *common),
+        shape(cut, buses),
+    )
     final_state, plan2 = ending(
-        end_kernel, cut, pieces[-1:], (done,), (shape(rows, buses), shape(hours, buses)), out_space=pl.ANY
+        end_kernel,
+        cut,
+        size,
+        (inside,),
+        (done, state0, firsts[c][1], prices, select, *ties, plan1, firsts[c][0], slopes[c], *common),
+        (shape(rows, buses), shape(hours, buses)),
+        more=(
+            pltpu.VMEM((size, buses), F32),
+            pltpu.VMEM((size, buses), F32),
+            pltpu.VMEM((2 * size, buses), BF16),
+        ),
+        out_space=pl.ANY,
     )
     return (final_state.reshape(start_state.shape), plan2[None])
 

time: 115 us -> 111 us (0.965)
  starting transfers between devices: 43.2 us -> 41.4 us
  waiting for transfers between devices: 45 us -> 43.4 us
    ppermute x12, waiting for transfers between devices: 15.3 us -> 10.2 us  [the longest x6 5.43 us: exchange(): a = lax.ppermute(a, 'region', borders(size, 0))]
    ppermute x10, waiting for transfers between devices: 29.4 us -> 33.2 us  [from_flipped(): return lax.ppermute(value, 'scen', flipped(lax.axis_size('scen'), bit))]
    ppermute x12, starting transfers between devices: 21.1 us -> 17.7 us  [the longest x6 12.6 us: exchange(): a = lax.ppermute(a, 'region', borders(size, 0))]
    ppermute x10, starting transfers between devices: 21.7 us -> 23.3 us  [from_flipped(): return lax.ppermute(value, 'scen', flipped(lax.axis_size('scen'), bit))]
    pallas_call x4 -> x3, Pallas kernels: 3.6 us -> 2.62 us  [inner(): call(lambda *refs, at=starts[c] + inside, inside=inside: prepare_kernel(a...]
    pallas_call x6 -> x7, Pallas kernels: 4.35 us -> 4.5 us  [pick(): call(lambda *refs: pick_kernel(at, sides, *refs), (shape(size, slots),) *...]
  transfers between devices with their start and end apart: 26 -> 26, of which waited for: 9 -> 11; matrix products, arithmetic and copies ran while one was open for 0% -> 0% of each run, Pallas kernels for 16% -> 17%
where the time goes in v4:
time: 111 us; the launch traced here: 110 us
  waiting for transfers between devices  43.4 us (39%)
  starting transfers between devices  41.4 us (37%)
  Pallas kernels  21.3 us (19%)
  local copies, waits for them, and re-layouts  2.16 us (2%)
  between operations  1.28 us (1%)
    ppermute x10, waiting for transfers between devices, from_flipped(): return lax.ppermute(value, 'scen', flipped(lax.axis_size('scen'), bit))  33.2 us
    ppermute x10, starting transfers between devices, from_flipped(): return lax.ppermute(value, 'scen', flipped(lax.axis_size('scen'), bit))  23.3 us
    ppermute x6, starting transfers between devices, exchange(): a = lax.ppermute(a, 'region', borders(size, 0))  12.6 us
    ppermute x6, waiting for transfers between devices, exchange(): a = lax.ppermute(a, 'region', borders(size, 0))  5.43 us
    pallas_call x2, Pallas kernels, inner(): call(lambda *refs, at=at: first_kernel(at, *refs), (wide, wide, shape(hou...  5.18 us
    ppermute x6, starting transfers between devices, exchange(): b = lax.ppermute(b, 'region', borders(size, 1))  5.17 us
    ppermute x6, waiting for transfers between devices, exchange(): b = lax.ppermute(b, 'region', borders(size, 1))  4.77 us
    pallas_call x7, Pallas kernels, pick(): call(lambda *refs: pick_kernel(at, sides, *refs), (shape(size, slots),) *...  4.5 us
  transfers between devices with their start and end apart: 26, of which 11 were waited for; matrix products, arithmetic and copies ran while one was open for 0% of the time, Pallas kernels for 17%

profile of v4, /device:TPU:8, one launch (start us, length us, event | category | flops | bytes accessed | tf_op | source)
XLA Modules:
  0.0 109.8 jit_solution(14271806711451941821)
XLA Ops:
  0.7 1.4 %copy-done = f32[1,16,24,1024]{3,2,1,0:T(8,128)S(1)} copy-done((f32[1,16,24,1024]{3,2,1,0:T(8,128)S(1)}, f32[1,16,24,1024]{3,2,1,0:T(8,128)}, u32[]{:S(2)}) %copy-start) | copy-done | bytes 1572888
  2.1 0.1 shard_map.100
  2.2 0.1 collective-permute-start.2
  2.4 0.4 shard_map.96.refs_1_.select.refs_5_.refs_4_
  2.8 0.7 copy-done.1
  3.5 0.7 shard_map.97
  4.1 2.2 %collective-permute-start = (f32[240,512]{1,0:T(8,128)S(1)}, f32[240,512]{1,0:T(8,128)S(1)}, u32[]{:S(2)}, u32[]{:S(2)}) collective-permute-start(f32[240,512]{1,0:T(8,128)S(1)} %shard_map.97), channel_id=1, source_target_pairs={{0,32},{32,0},{64,96},{96,64},{128,160},{160,128},{192,224},{224,1... | collective-permute-start | bytes 1474568 | tf_op jit(solution)/shard_map/ppermute | solution.py:291
  6.4 0.7 shard_map.98
  7.1 0.0 copy-start.2
  7.1 0.9 collective-permute-start.1
  8.0 0.8 shard_map.109
  8.7 0.0 copy-start.8
  8.8 0.0 copy-start.5
  8.8 0.0 copy-start.6
  8.8 1.0 shard_map.95.refs_1_
  9.8 2.4 %collective-permute-start.3 = (f32[24,512]{1,0:T(8,128)S(1)}, f32[24,512]{1,0:T(8,128)S(1)}, u32[]{:S(2)}, u32[]{:S(2)}) collective-permute-start(f32[24,512]{1,0:T(8,128)S(1)} %select_add_fusion.1), channel_id=1, source_target_pairs={{0,16},{1,17},{2,18},{3,19},{4,20},{5,21},{6,22},{7,23},{8,24},{9,... | collective-permute-start | bytes 147464 | tf_op jit(solution)/shard_map/ppermute | solution.py:312
  12.2 0.1 compare_convert_fusion
  12.2 17.5 %collective-permute-done.3 = f32[24,512]{1,0:T(8,128)S(1)} collective-permute-done((f32[24,512]{1,0:T(8,128)S(1)}, f32[24,512]{1,0:T(8,128)S(1)}, u32[]{:S(2)}, u32[]{:S(2)}) %collective-permute-start.3) | collective-permute-done | bytes 49184 | tf_op jit(solution)/shard_map/ppermute | solution.py:312
  29.8 2.0 %collective-permute-start.4 = (f32[24,512]{1,0:T(8,128)S(1)}, f32[24,512]{1,0:T(8,128)S(1)}, u32[]{:S(2)}, u32[]{:S(2)}) collective-permute-start(f32[24,512]{1,0:T(8,128)S(1)} %add.49), channel_id=1, source_target_pairs={{0,2},{1,3},{2,0},{3,1},{4,6},{5,7},{6,4},{7,5},{8,10},{9,11},{10,... | collective-permute-start | bytes 147464 | tf_op jit(solution)/shard_map/ppermute | solution.py:312
  31.8 2.2 %collective-permute-done.4 = f32[24,512]{1,0:T(8,128)S(1)} collective-permute-done((f32[24,512]{1,0:T(8,128)S(1)}, f32[24,512]{1,0:T(8,128)S(1)}, u32[]{:S(2)}, u32[]{:S(2)}) %collective-permute-start.4) | collective-permute-done | bytes 49184 | tf_op jit(solution)/shard_map/ppermute | solution.py:312
  34.0 6.4 %collective-permute-start.7 = (f32[24,512]{1,0:T(8,128)S(1)}, f32[24,512]{1,0:T(8,128)S(1)}, u32[]{:S(2)}, u32[]{:S(2)}) collective-permute-start(f32[24,512]{1,0:T(8,128)S(1)} %add.50), channel_id=1, source_target_pairs={{0,12},{1,13},{2,14},{3,15},{4,8},{5,9},{6,10},{7,11},{8,4},{9,5},... | collective-permute-start | bytes 147464 | tf_op jit(solution)/shard_map/ppermute | solution.py:312
  40.4 1.2 %collective-permute-start.6 = (f32[24,512]{1,0:T(8,128)S(1)}, f32[24,512]{1,0:T(8,128)S(1)}, u32[]{:S(2)}, u32[]{:S(2)}) collective-permute-start(f32[24,512]{1,0:T(8,128)S(1)} %add.50), channel_id=1, source_target_pairs={{0,8},{1,9},{2,10},{3,11},{4,12},{5,13},{6,14},{7,15},{8,0},{9,1},... | collective-permute-start | bytes 147464 | tf_op jit(solution)/shard_map/ppermute | solution.py:312
  41.6 1.2 %collective-permute-start.5 = (f32[24,512]{1,0:T(8,128)S(1)}, f32[24,512]{1,0:T(8,128)S(1)}, u32[]{:S(2)}, u32[]{:S(2)}) collective-permute-start(f32[24,512]{1,0:T(8,128)S(1)} %add.50), channel_id=1, source_target_pairs={{0,4},{1,5},{2,6},{3,7},{4,0},{5,1},{6,2},{7,3},{8,12},{9,13},{10,... | collective-permute-start | bytes 147464 | tf_op jit(solution)/shard_map/ppermute | solution.py:312
  42.9 2.0 %collective-permute-start.15 = (f32[144,512]{1,0:T(8,128)S(1)}, f32[144,512]{1,0:T(8,128)S(1)}, u32[]{:S(2)}, u32[]{:S(2)}) collective-permute-start(f32[144,512]{1,0:T(8,128)S(1)} %get-tuple-element.32), channel_id=1, source_target_pairs={{0,32},{32,0},{64,96},{96,64},{128,160},{160,128},{192,224},{224,1... | collective-permute-start | bytes 884744 | tf_op jit(solution)/shard_map/ppermute | solution.py:291
  44.8 3.6 %collective-permute-done.6 = f32[24,512]{1,0:T(8,128)S(1)} collective-permute-done((f32[24,512]{1,0:T(8,128)S(1)}, f32[24,512]{1,0:T(8,128)S(1)}, u32[]{:S(2)}, u32[]{:S(2)}) %collective-permute-start.6) | collective-permute-done | bytes 49184 | tf_op jit(solution)/shard_map/ppermute | solution.py:312
  48.4 2.8 %collective-permute-start.16 = (f32[144,512]{1,0:T(8,128)S(1)}, f32[144,512]{1,0:T(8,128)S(1)}, u32[]{:S(2)}, u32[]{:S(2)}) collective-permute-start(f32[144,512]{1,0:T(8,128)S(1)} %get-tuple-element.33), channel_id=1, source_target_pairs={{32,64},{64,32},{96,128},{128,96},{160,192},{192,160},{224,0},{0,2... | collective-permute-start | bytes 884744 | tf_op jit(solution)/shard_map/ppermute | solution.py:292
  51.3 0.0 copy-start.3
  51.3 0.0 copy-start.4
  51.3 0.1 collective-permute-start.8
  51.4 1.9 %shard_map.99 = (f32[8,1024]{1,0:T(8,128)S(1)}, f32[8,1024]{1,0:T(8,128)S(1)}) custom-call(bf16[1024,1024]{1,0:T(8,128)(2,1)S(1)} %shard_map.96.refs_1_.select.refs_5_.refs_4_, f32[1,1024]{1,0:T(1,128)S(1)} %broadcast_select_fusion.live, s32[1,512]{1,0:T(1,128)S(1)} %copy-done.5, f32[1,512]{1,0:T(1,128)S(1)} %copy-done.6), custom_call_target="tpu_custom_call" | custom-call | flops 4294967296 | bytes 1048576 | tf_op jit(solution)/shard_map/pallas_call | solution.py:369
  53.4 2.7 %collective-permute-done.16.refs_7_ = f32[144,512]{1,0:T(8,128)S(1)} collective-permute-done((f32[144,512]{1,0:T(8,128)S(1)}, f32[144,512]{1,0:T(8,128)S(1)}, u32[]{:S(2)}, u32[]{:S(2)}) %collective-permute-start.16) | collective-permute-done | bytes 294944 | tf_op jit(solution)/shard_map/ppermute | solution.py:292
  56.1 2.1 %shard_map.110 = (f32[144,1024]{1,0:T(8,128)S(1)}, f32[144,1024]{1,0:T(8,128)S(1)}, f32[24,1024]{1,0:T(8,128)S(1)}) custom-call(f32[384,1024]{1,0:T(8,128)S(1)} %bitcast.16, f32[384,1024]{1,0:T(8,128)S(1)} %shard_map.95.refs_1_, f32[384,1024]{1,0:T(8,128)S(1)} %bitcast.29, f32[384,1024]{1,0:T(8,128)S(1)} %bitcast.35, bf16[1024,1024]{1,0:T(8,128)(2,1)S(1)} %bitcast.23, ...), custom_call_target="tpu_custom_call" | custom-call | flops 4294967296 | bytes 1048576 | tf_op jit(solution)/shard_map/pallas_call | solution.py:376
  58.2 0.8 shard_map.112
  58.9 3.2 %collective-permute-start.24 = (f32[144,512]{1,0:T(8,128)S(1)}, f32[144,512]{1,0:T(8,128)S(1)}, u32[]{:S(2)}, u32[]{:S(2)}) collective-permute-start(f32[144,512]{1,0:T(8,128)S(1)} %get-tuple-element.38), channel_id=1, source_target_pairs={{0,32},{32,0},{64,96},{96,64},{128,160},{160,128},{192,224},{224,1... | collective-permute-start | bytes 884744 | tf_op jit(solution)/shard_map/ppermute | solution.py:291
  62.1 0.5 shard_map.113.refs_9_
  62.6 3.1 %shard_map.101 = (f32[240,1024]{1,0:T(8,128)S(1)}, f32[240,1024]{1,0:T(8,128)S(1)}, f32[24,1024]{1,0:T(8,128)S(1)}) custom-call(f32[384,1024]{1,0:T(8,128)S(1)} %bitcast.17, f32[384,1024]{1,0:T(8,128)S(1)} %shard_map.95.refs_1_, f32[384,1024]{1,0:T(8,128)S(1)} %bitcast.30, f32[384,1024]{1,0:T(8,128)S(1)} %bitcast.36, bf16[1024,1024]{1,0:T(8,128)(2,1)S(1)} %bitcast.25, ...), custom_call_target="tpu_custom_call" | custom-call | flops 4294967296 | bytes 1048576 | tf_op jit(solution)/shard_map/pallas_call | solution.py:376
  65.7 0.4 shard_map.105
  66.2 0.6 shard_map.107
  66.8 0.1 collective-permute-start.17
  66.9 0.6 shard_map.103
  67.5 3.1 %collective-permute-start.11 = (f32[48,512]{1,0:T(8,128)S(1)}, f32[48,512]{1,0:T(8,128)S(1)}, u32[]{:S(2)}, u32[]{:S(2)}) collective-permute-start(f32[48,512]{1,0:T(8,128)S(1)} %get-tuple-element.28), channel_id=1, source_target_pairs={{0,32},{32,0},{64,96},{96,64},{128,160},{160,128},{192,224},{224,1... | collective-permute-start | bytes 294920 | tf_op jit(solution)/shard_map/ppermute | solution.py:291
  70.6 0.0 collective-permute-start.12
  70.7 0.8 collective-permute-start.18
  71.5 0.7 shard_map.102.refs_1_.refs_4_.refs_7_
  72.1 5.5 %collective-permute-done.18 = f32[24,512]{1,0:T(8,128)S(1)} collective-permute-done((f32[24,512]{1,0:T(8,128)S(1)}, f32[24,512]{1,0:T(8,128)S(1)}, u32[]{:S(2)}, u32[]{:S(2)}) %collective-permute-start.18) | collective-permute-done | bytes 49184 | tf_op jit(solution)/shard_map/ppermute | solution.py:312
  77.7 1.0 collective-permute-start.13
  78.7 1.4 %collective-permute-start.14 = (f32[96,512]{1,0:T(8,128)S(1)}, f32[96,512]{1,0:T(8,128)S(1)}, u32[]{:S(2)}, u32[]{:S(2)}) collective-permute-start(f32[96,512]{1,0:T(8,128)S(1)} %get-tuple-element.31), channel_id=1, source_target_pairs={{32,64},{64,32},{96,128},{128,96},{160,192},{192,160},{224,0},{0,2... | collective-permute-start | bytes 589832 | tf_op jit(solution)/shard_map/ppermute | solution.py:292
  80.1 1.5 %collective-permute-start.19 = (f32[24,512]{1,0:T(8,128)S(1)}, f32[24,512]{1,0:T(8,128)S(1)}, u32[]{:S(2)}, u32[]{:S(2)}) collective-permute-start(f32[24,512]{1,0:T(8,128)S(1)} %add.56), channel_id=1, source_target_pairs={{0,2},{1,3},{2,0},{3,1},{4,6},{5,7},{6,4},{7,5},{8,10},{9,11},{10,... | collective-permute-start | bytes 147464 | tf_op jit(solution)/shard_map/ppermute | solution.py:312
  81.6 0.8 shard_map.106.refs_5_
  82.4 1.8 %collective-permute-done.19 = f32[24,512]{1,0:T(8,128)S(1)} collective-permute-done((f32[24,512]{1,0:T(8,128)S(1)}, f32[24,512]{1,0:T(8,128)S(1)}, u32[]{:S(2)}, u32[]{:S(2)}) %collective-permute-start.19) | collective-permute-done | bytes 49184 | tf_op jit(solution)/shard_map/ppermute | solution.py:312
  84.2 3.2 %collective-permute-start.22 = (f32[24,512]{1,0:T(8,128)S(1)}, f32[24,512]{1,0:T(8,128)S(1)}, u32[]{:S(2)}, u32[]{:S(2)}) collective-permute-start(f32[24,512]{1,0:T(8,128)S(1)} %add.57), channel_id=1, source_target_pairs={{0,12},{1,13},{2,14},{3,15},{4,8},{5,9},{6,10},{7,11},{8,4},{9,5},... | collective-permute-start | bytes 147464 | tf_op jit(solution)/shard_map/ppermute | solution.py:312
  87.4 1.4 %collective-permute-done.13.refs_5_ = f32[96,512]{1,0:T(8,128)S(1)} collective-permute-done((f32[96,512]{1,0:T(8,128)S(1)}, f32[96,512]{1,0:T(8,128)S(1)}, u32[]{:S(2)}, u32[]{:S(2)}) %collective-permute-start.13) | collective-permute-done | bytes 196640 | tf_op jit(solution)/shard_map/ppermute | solution.py:291
  88.8 3.1 %collective-permute-start.21 = (f32[24,512]{1,0:T(8,128)S(1)}, f32[24,512]{1,0:T(8,128)S(1)}, u32[]{:S(2)}, u32[]{:S(2)}) collective-permute-start(f32[24,512]{1,0:T(8,128)S(1)} %add.57), channel_id=1, source_target_pairs={{0,8},{1,9},{2,10},{3,11},{4,12},{5,13},{6,14},{7,15},{8,0},{9,1},... | collective-permute-start | bytes 147464 | tf_op jit(solution)/shard_map/ppermute | solution.py:312
  91.9 1.5 %collective-permute-start.20 = (f32[24,512]{1,0:T(8,128)S(1)}, f32[24,512]{1,0:T(8,128)S(1)}, u32[]{:S(2)}, u32[]{:S(2)}) collective-permute-start(f32[24,512]{1,0:T(8,128)S(1)} %add.57), channel_id=1, source_target_pairs={{0,4},{1,5},{2,6},{3,7},{4,0},{5,1},{6,2},{7,3},{8,12},{9,13},{10,... | collective-permute-start | bytes 147464 | tf_op jit(solution)/shard_map/ppermute | solution.py:312
  93.3 0.9 shard_map.108.refs_8_
  94.3 1.1 %collective-permute-start.9 = (f32[96,512]{1,0:T(8,128)S(1)}, f32[96,512]{1,0:T(8,128)S(1)}, u32[]{:S(2)}, u32[]{:S(2)}) collective-permute-start(f32[96,512]{1,0:T(8,128)S(1)} %get-tuple-element.26), channel_id=1, source_target_pairs={{0,32},{32,0},{64,96},{96,64},{128,160},{160,128},{192,224},{224,1... | collective-permute-start | bytes 589832 | tf_op jit(solution)/shard_map/ppermute | solution.py:291
  95.4 2.2 %collective-permute-done.21 = f32[24,512]{1,0:T(8,128)S(1)} collective-permute-done((f32[24,512]{1,0:T(8,128)S(1)}, f32[24,512]{1,0:T(8,128)S(1)}, u32[]{:S(2)}, u32[]{:S(2)}) %collective-permute-start.21) | collective-permute-done | bytes 49184 | tf_op jit(solution)/shard_map/ppermute | solution.py:312
  97.6 0.4 collective-permute-done.20
  98.0 0.1 collective-permute-start.23
  98.1 4.0 %collective-permute-done.9.refs_5_ = f32[96,512]{1,0:T(8,128)S(1)} collective-permute-done((f32[96,512]{1,0:T(8,128)S(1)}, f32[96,512]{1,0:T(8,128)S(1)}, u32[]{:S(2)}, u32[]{:S(2)}) %collective-permute-start.9) | collective-permute-done | bytes 196640 | tf_op jit(solution)/shard_map/ppermute | solution.py:291
  102.1 2.1 %collective-permute-done.10.refs_6_ = f32[96,512]{1,0:T(8,128)S(1)} collective-permute-done((f32[96,512]{1,0:T(8,128)S(1)}, f32[96,512]{1,0:T(8,128)S(1)}, u32[]{:S(2)}, u32[]{:S(2)}) %collective-permute-start.10) | collective-permute-done | bytes 196640 | tf_op jit(solution)/shard_map/ppermute | solution.py:292
  104.2 0.9 shard_map.104.refs_2_
  105.2 1.7 %shard_map.111.refs_0_ = f32[240,1024]{1,0:T(8,128)S(1)} custom-call(f32[240,1024]{1,0:T(8,128)S(1)} %get-tuple-element.24.state.refs_0_.refs_1_.refs_3_.refs_6_, f32[240,1024]{1,0:T(8,128)S(1)} %shard_map.102.refs_1_.refs_4_.refs_7_, f32[96,1024]{1,0:T(8,128)S(1)} %shard_map.104.refs_2_, ...), custom_call_target="tpu_custom_call" | custom-call | flops 4294967296 | bytes 1048576 | tf_op jit(solution)/shard_map/pallas_call | solution.py:416
  106.9 2.7 %shard_map.114 = (f32[384,1024]{1,0:T(8,128)}, f32[24,1024]{1,0:T(8,128)}) custom-call(f32[240,1024]{1,0:T(8,128)S(1)} %shard_map.111.refs_0_, f32[384,1024]{1,0:T(8,128)S(1)} %bitcast.21, f32[144,1024]{1,0:T(8,128)S(1)} %get-tuple-element.36.refs_2_, f32[384,1024]{1,0:T(8,128)S(1)} %bitcast.34, ...), custom_call_target="tpu_custom_call" | custom-call | flops 4294967296 | bytes 1048576 | tf_op jit(solution)/shard_map/pallas_call | solution.py:416
  (44 shorter events, 0.2 us)
Async XLA Ops:
  0.6 1.7 %copy-start.7 = (s32[1,2,512]{2,1,0:T(2,128)S(1)}, s32[1,2,512]{2,1,0:T(2,128)}, u32[]{:S(2)}) copy-start(s32[1,2,512]{2,1,0:T(2,128)} %param.14) | copy-start | bytes 12292
  0.7 1.4 %copy-start = (f32[1,16,24,1024]{3,2,1,0:T(8,128)S(1)}, f32[1,16,24,1024]{3,2,1,0:T(8,128)}, u32[]{:S(2)}) copy-start(f32[1,16,24,1024]{3,2,1,0:T(8,128)} %param.8) | copy-start | bytes 4718596
  2.1 1.4 %copy-start.1 = (f32[1,16,24,1024]{3,2,1,0:T(8,128)S(1)}, f32[1,16,24,1024]{3,2,1,0:T(8,128)}, u32[]{:S(2)}) copy-start(f32[1,16,24,1024]{3,2,1,0:T(8,128)} %param.8) | copy-start | bytes 4718596
  2.2 7.5 %collective-permute-start.2 = (f32[24,512]{1,0:T(8,128)S(1)}, f32[24,512]{1,0:T(8,128)S(1)}, u32[]{:S(2)}, u32[]{:S(2)}) collective-permute-start(f32[24,512]{1,0:T(8,128)S(1)} %slice_select_fusion.1), channel_id=1, source_target_pairs={{0,1},{1,0},{2,3},{3,2},{4,5},{5,4},{6,7},{7,6},{8,9},{9,8},{10,11... | collective-permute-start | bytes 147464 | tf_op jit(solution)/shard_map/ppermute | solution.py:301
  4.1 58.5 %collective-permute-start = (f32[240,512]{1,0:T(8,128)S(1)}, f32[240,512]{1,0:T(8,128)S(1)}, u32[]{:S(2)}, u32[]{:S(2)}) collective-permute-start(f32[240,512]{1,0:T(8,128)S(1)} %shard_map.97), channel_id=1, source_target_pairs={{0,32},{32,0},{64,96},{96,64},{128,160},{160,128},{192,224},{224,1... | collective-permute-start | bytes 1474568 | tf_op jit(solution)/shard_map/ppermute | solution.py:291
  7.1 1.7 %copy-start.2 = (bf16[1,1024,1024]{2,1,0:T(8,128)(2,1)S(1)}, bf16[1,1024,1024]{2,1,0:T(8,128)(2,1)}, u32[]{:S(2)}) copy-start(bf16[1,1024,1024]{2,1,0:T(8,128)(2,1)} %param.11) | copy-start | bytes 6291460
  7.1 55.5 %collective-permute-start.1 = (f32[240,512]{1,0:T(8,128)S(1)}, f32[240,512]{1,0:T(8,128)S(1)}, u32[]{:S(2)}, u32[]{:S(2)}) collective-permute-start(f32[240,512]{1,0:T(8,128)S(1)} %shard_map.98), channel_id=1, source_target_pairs={{32,64},{64,32},{96,128},{128,96},{160,192},{192,160},{224,0},{0,2... | collective-permute-start | bytes 1474568 | tf_op jit(solution)/shard_map/ppermute | solution.py:292
  8.7 3.4 %copy-start.8 = (s32[1,2]{1,0:T(1,128)S(1)}, s32[1,2]{1,0:T(1,128)}, u32[]{:S(2)}) copy-start(s32[1,2]{1,0:T(1,128)} %param.15) | copy-start | bytes 28
  8.8 42.7 %copy-start.5 = (s32[1,512]{1,0:T(1,128)S(1)}, s32[1,512]{1,0:T(1,128)}, u32[]{:S(2)}) copy-start(s32[1,512]{1,0:T(1,128)} %gen_bus.1) | copy-start | bytes 6148
  8.8 42.7 %copy-start.6 = (f32[1,512]{1,0:T(1,128)S(1)}, f32[1,512]{1,0:T(1,128)}, u32[]{:S(2)}) copy-start(f32[1,512]{1,0:T(1,128)} %gen_cap.1) | copy-start | bytes 6148
  9.8 20.0 %collective-permute-start.3 = (f32[24,512]{1,0:T(8,128)S(1)}, f32[24,512]{1,0:T(8,128)S(1)}, u32[]{:S(2)}, u32[]{:S(2)}) collective-permute-start(f32[24,512]{1,0:T(8,128)S(1)} %select_add_fusion.1), channel_id=1, source_target_pairs={{0,16},{1,17},{2,18},{3,19},{4,20},{5,21},{6,22},{7,23},{8,24},{9,... | collective-permute-start | bytes 147464 | tf_op jit(solution)/shard_map/ppermute | solution.py:312
  29.8 4.2 %collective-permute-start.4 = (f32[24,512]{1,0:T(8,128)S(1)}, f32[24,512]{1,0:T(8,128)S(1)}, u32[]{:S(2)}, u32[]{:S(2)}) collective-permute-start(f32[24,512]{1,0:T(8,128)S(1)} %add.49), channel_id=1, source_target_pairs={{0,2},{1,3},{2,0},{3,1},{4,6},{5,7},{6,4},{7,5},{8,10},{9,11},{10,... | collective-permute-start | bytes 147464 | tf_op jit(solution)/shard_map/ppermute | solution.py:312
  34.0 8.9 %collective-permute-start.7 = (f32[24,512]{1,0:T(8,128)S(1)}, f32[24,512]{1,0:T(8,128)S(1)}, u32[]{:S(2)}, u32[]{:S(2)}) collective-permute-start(f32[24,512]{1,0:T(8,128)S(1)} %add.50), channel_id=1, source_target_pairs={{0,12},{1,13},{2,14},{3,15},{4,8},{5,9},{6,10},{7,11},{8,4},{9,5},... | collective-permute-start | bytes 147464 | tf_op jit(solution)/shard_map/ppermute | solution.py:312
  40.4 8.1 %collective-permute-start.6 = (f32[24,512]{1,0:T(8,128)S(1)}, f32[24,512]{1,0:T(8,128)S(1)}, u32[]{:S(2)}, u32[]{:S(2)}) collective-permute-start(f32[24,512]{1,0:T(8,128)S(1)} %add.50), channel_id=1, source_target_pairs={{0,8},{1,9},{2,10},{3,11},{4,12},{5,13},{6,14},{7,15},{8,0},{9,1},... | collective-permute-start | bytes 147464 | tf_op jit(solution)/shard_map/ppermute | solution.py:312
  41.6 9.7 %collective-permute-start.5 = (f32[24,512]{1,0:T(8,128)S(1)}, f32[24,512]{1,0:T(8,128)S(1)}, u32[]{:S(2)}, u32[]{:S(2)}) collective-permute-start(f32[24,512]{1,0:T(8,128)S(1)} %add.50), channel_id=1, source_target_pairs={{0,4},{1,5},{2,6},{3,7},{4,0},{5,1},{6,2},{7,3},{8,12},{9,13},{10,... | collective-permute-start | bytes 147464 | tf_op jit(solution)/shard_map/ppermute | solution.py:312
  42.9 10.5 %collective-permute-start.15 = (f32[144,512]{1,0:T(8,128)S(1)}, f32[144,512]{1,0:T(8,128)S(1)}, u32[]{:S(2)}, u32[]{:S(2)}) collective-permute-start(f32[144,512]{1,0:T(8,128)S(1)} %get-tuple-element.32), channel_id=1, source_target_pairs={{0,32},{32,0},{64,96},{96,64},{128,160},{160,128},{192,224},{224,1... | collective-permute-start | bytes 884744 | tf_op jit(solution)/shard_map/ppermute | solution.py:291
  48.4 7.6 %collective-permute-start.16 = (f32[144,512]{1,0:T(8,128)S(1)}, f32[144,512]{1,0:T(8,128)S(1)}, u32[]{:S(2)}, u32[]{:S(2)}) collective-permute-start(f32[144,512]{1,0:T(8,128)S(1)} %get-tuple-element.33), channel_id=1, source_target_pairs={{32,64},{64,32},{96,128},{128,96},{160,192},{192,160},{224,0},{0,2... | collective-permute-start | bytes 884744 | tf_op jit(solution)/shard_map/ppermute | solution.py:292
  51.3 4.8 %copy-start.3 = (f32[1,16,24,1024]{3,2,1,0:T(8,128)S(1)}, f32[1,16,24,1024]{3,2,1,0:T(8,128)}, u32[]{:S(2)}) copy-start(f32[1,16,24,1024]{3,2,1,0:T(8,128)} %param.9) | copy-start | bytes 4718596
  51.3 4.8 %copy-start.4 = (f32[1,16,24,1024]{3,2,1,0:T(8,128)S(1)}, f32[1,16,24,1024]{3,2,1,0:T(8,128)}, u32[]{:S(2)}) copy-start(f32[1,16,24,1024]{3,2,1,0:T(8,128)} %param.10) | copy-start | bytes 4718596
  51.3 2.0 %collective-permute-start.8 = (f32[24,512]{1,0:T(8,128)S(1)}, f32[24,512]{1,0:T(8,128)S(1)}, u32[]{:S(2)}, u32[]{:S(2)}) collective-permute-start(f32[24,512]{1,0:T(8,128)S(1)} %add_add_fusion.1), channel_id=1, source_target_pairs={{0,1},{1,0},{2,3},{3,2},{4,5},{5,4},{6,7},{7,6},{8,9},{9,8},{10,11... | collective-permute-start | bytes 147464 | tf_op jit(solution)/shard_map/ppermute | solution.py:305
  58.9 48.0 %collective-permute-start.24 = (f32[144,512]{1,0:T(8,128)S(1)}, f32[144,512]{1,0:T(8,128)S(1)}, u32[]{:S(2)}, u32[]{:S(2)}) collective-permute-start(f32[144,512]{1,0:T(8,128)S(1)} %get-tuple-element.38), channel_id=1, source_target_pairs={{0,32},{32,0},{64,96},{96,64},{128,160},{160,128},{192,224},{224,1... | collective-permute-start | bytes 884744 | tf_op jit(solution)/shard_map/ppermute | solution.py:291
  62.1 44.8 %collective-permute-start.25 = (f32[144,512]{1,0:T(8,128)S(1)}, f32[144,512]{1,0:T(8,128)S(1)}, u32[]{:S(2)}, u32[]{:S(2)}) collective-permute-start(f32[144,512]{1,0:T(8,128)S(1)} %get-tuple-element.39), channel_id=1, source_target_pairs={{32,64},{64,32},{96,128},{128,96},{160,192},{192,160},{224,0},{0,2... | collective-permute-start | bytes 884744 | tf_op jit(solution)/shard_map/ppermute | solution.py:292
  66.8 3.8 %collective-permute-start.17 = (f32[24,512]{1,0:T(8,128)S(1)}, f32[24,512]{1,0:T(8,128)S(1)}, u32[]{:S(2)}, u32[]{:S(2)}) collective-permute-start(f32[24,512]{1,0:T(8,128)S(1)} %slice_select_fusion), channel_id=1, source_target_pairs={{0,1},{1,0},{2,3},{3,2},{4,5},{5,4},{6,7},{7,6},{8,9},{9,8},{10,11... | collective-permute-start | bytes 147464 | tf_op jit(solution)/shard_map/ppermute | solution.py:301
  67.5 11.1 %collective-permute-start.11 = (f32[48,512]{1,0:T(8,128)S(1)}, f32[48,512]{1,0:T(8,128)S(1)}, u32[]{:S(2)}, u32[]{:S(2)}) collective-permute-start(f32[48,512]{1,0:T(8,128)S(1)} %get-tuple-element.28), channel_id=1, source_target_pairs={{0,32},{32,0},{64,96},{96,64},{128,160},{160,128},{192,224},{224,1... | collective-permute-start | bytes 294920 | tf_op jit(solution)/shard_map/ppermute | solution.py:291
  70.6 9.5 %collective-permute-start.12 = (f32[48,512]{1,0:T(8,128)S(1)}, f32[48,512]{1,0:T(8,128)S(1)}, u32[]{:S(2)}, u32[]{:S(2)}) collective-permute-start(f32[48,512]{1,0:T(8,128)S(1)} %get-tuple-element.29), channel_id=1, source_target_pairs={{32,64},{64,32},{96,128},{128,96},{160,192},{192,160},{224,0},{0,2... | collective-permute-start | bytes 294920 | tf_op jit(solution)/shard_map/ppermute | solution.py:292
  70.7 7.0 %collective-permute-start.18 = (f32[24,512]{1,0:T(8,128)S(1)}, f32[24,512]{1,0:T(8,128)S(1)}, u32[]{:S(2)}, u32[]{:S(2)}) collective-permute-start(f32[24,512]{1,0:T(8,128)S(1)} %select_add_fusion), channel_id=1, source_target_pairs={{0,16},{1,17},{2,18},{3,19},{4,20},{5,21},{6,22},{7,23},{8,24},{9,... | collective-permute-start | bytes 147464 | tf_op jit(solution)/shard_map/ppermute | solution.py:312
  77.7 11.1 %collective-permute-start.13 = (f32[96,512]{1,0:T(8,128)S(1)}, f32[96,512]{1,0:T(8,128)S(1)}, u32[]{:S(2)}, u32[]{:S(2)}) collective-permute-start(f32[96,512]{1,0:T(8,128)S(1)} %get-tuple-element.30), channel_id=1, source_target_pairs={{0,32},{32,0},{64,96},{96,64},{128,160},{160,128},{192,224},{224,1... | collective-permute-start | bytes 589832 | tf_op jit(solution)/shard_map/ppermute | solution.py:291
  78.7 13.2 %collective-permute-start.14 = (f32[96,512]{1,0:T(8,128)S(1)}, f32[96,512]{1,0:T(8,128)S(1)}, u32[]{:S(2)}, u32[]{:S(2)}) collective-permute-start(f32[96,512]{1,0:T(8,128)S(1)} %get-tuple-element.31), channel_id=1, source_target_pairs={{32,64},{64,32},{96,128},{128,96},{160,192},{192,160},{224,0},{0,2... | collective-permute-start | bytes 589832 | tf_op jit(solution)/shard_map/ppermute | solution.py:292
  80.1 4.1 %collective-permute-start.19 = (f32[24,512]{1,0:T(8,128)S(1)}, f32[24,512]{1,0:T(8,128)S(1)}, u32[]{:S(2)}, u32[]{:S(2)}) collective-permute-start(f32[24,512]{1,0:T(8,128)S(1)} %add.56), channel_id=1, source_target_pairs={{0,2},{1,3},{2,0},{3,1},{4,6},{5,7},{6,4},{7,5},{8,10},{9,11},{10,... | collective-permute-start | bytes 147464 | tf_op jit(solution)/shard_map/ppermute | solution.py:312
  84.2 10.1 %collective-permute-start.22 = (f32[24,512]{1,0:T(8,128)S(1)}, f32[24,512]{1,0:T(8,128)S(1)}, u32[]{:S(2)}, u32[]{:S(2)}) collective-permute-start(f32[24,512]{1,0:T(8,128)S(1)} %add.57), channel_id=1, source_target_pairs={{0,12},{1,13},{2,14},{3,15},{4,8},{5,9},{6,10},{7,11},{8,4},{9,5},... | collective-permute-start | bytes 147464 | tf_op jit(solution)/shard_map/ppermute | solution.py:312
  88.8 8.8 %collective-permute-start.21 = (f32[24,512]{1,0:T(8,128)S(1)}, f32[24,512]{1,0:T(8,128)S(1)}, u32[]{:S(2)}, u32[]{:S(2)}) collective-permute-start(f32[24,512]{1,0:T(8,128)S(1)} %add.57), channel_id=1, source_target_pairs={{0,8},{1,9},{2,10},{3,11},{4,12},{5,13},{6,14},{7,15},{8,0},{9,1},... | collective-permute-start | bytes 147464 | tf_op jit(solution)/shard_map/ppermute | solution.py:312
  91.9 6.1 %collective-permute-start.20 = (f32[24,512]{1,0:T(8,128)S(1)}, f32[24,512]{1,0:T(8,128)S(1)}, u32[]{:S(2)}, u32[]{:S(2)}) collective-permute-start(f32[24,512]{1,0:T(8,128)S(1)} %add.57), channel_id=1, source_target_pairs={{0,4},{1,5},{2,6},{3,7},{4,0},{5,1},{6,2},{7,3},{8,12},{9,13},{10,... | collective-permute-start | bytes 147464 | tf_op jit(solution)/shard_map/ppermute | solution.py:312
  94.3 7.9 %collective-permute-start.9 = (f32[96,512]{1,0:T(8,128)S(1)}, f32[96,512]{1,0:T(8,128)S(1)}, u32[]{:S(2)}, u32[]{:S(2)}) collective-permute-start(f32[96,512]{1,0:T(8,128)S(1)} %get-tuple-element.26), channel_id=1, source_target_pairs={{0,32},{32,0},{64,96},{96,64},{128,160},{160,128},{192,224},{224,1... | collective-permute-start | bytes 589832 | tf_op jit(solution)/shard_map/ppermute | solution.py:291
  97.6 6.7 %collective-permute-start.10 = (f32[96,512]{1,0:T(8,128)S(1)}, f32[96,512]{1,0:T(8,128)S(1)}, u32[]{:S(2)}, u32[]{:S(2)}) collective-permute-start(f32[96,512]{1,0:T(8,128)S(1)} %get-tuple-element.27), channel_id=1, source_target_pairs={{32,64},{64,32},{96,128},{128,96},{160,192},{192,160},{224,0},{0,2... | collective-permute-start | bytes 589832 | tf_op jit(solution)/shard_map/ppermute | solution.py:292
  98.0 7.2 %collective-permute-start.23 = (f32[24,512]{1,0:T(8,128)S(1)}, f32[24,512]{1,0:T(8,128)S(1)}, u32[]{:S(2)}, u32[]{:S(2)}) collective-permute-start(f32[24,512]{1,0:T(8,128)S(1)} %add_add_fusion), channel_id=1, source_target_pairs={{0,1},{1,0},{2,3},{3,2},{4,5},{5,4},{6,7},{7,6},{8,9},{9,8},{10,11... | collective-permute-start | bytes 147464 | tf_op jit(solution)/shard_map/ppermute | solution.py:305
